TPU v7x, 512 devices: a whole 4x4x16 slice. The times are simulated.
512 devices in a mesh: gx: 16 (over x, z_hi), gy: 32 (over z_lo, y, core).
Axes of the slice: x: 4, y: 4, z: 16 (z_hi: 4, z_lo: 4; z = z_hi * 4 + z_lo), core: 2. Of those that a mesh axis runs over, the one named last changes fastest.
Arguments:
- fields: float32 [3, 512, 4096], P(None, 'gx', 'gy'), may hold values from -10 to 10
- lift_weight: float32 [12, 64], replicated, may hold values from -1.75 to 1.75
- lift_bias: float32 [64], replicated, may hold values from -3 to 3
- spectral_weight: float32 [2, 8, 8, 64, 64], replicated, may hold values from -4 to 4
- bypass_weight: float32 [64, 64], replicated, may hold values from -0.75 to 0.75
- layer_bias: float32 [64], replicated, may hold values from -3 to 3
- mlp_in_weight: float32 [64, 128], replicated, may hold values from -0.75 to 0.75
- mlp_in_bias: float32 [128], replicated, may hold values from -3 to 3
- mlp_out_weight: float32 [128, 64], replicated, may hold values from -0.5 to 0.5
- mlp_out_bias: float32 [64], replicated, may hold values from -3 to 3
- project_weight: float32 [64, 3], replicated, may hold values from -0.75 to 0.75
- project_bias: float32 [3], replicated, may hold values from -3 to 3
Outputs:
- next_fields: float32 [3, 512, 4096], P(None, 'gx', 'gy')
All inputs are finite; a program needn't handle non-finite values.
Results may differ from a plain program's by a relative error of at most 0.0001.
Values sent between devices are 32-bit elements; how exact they have to be, the bound alone decides.
No kernel may reach another device: no remote copies, remote signals or barrier semaphores. Data moves between devices by JAX's collectives and lax.ppermute only.
A program may use at most 64 MiB of HBM per device.

v0:
```python
import math

import jax
import jax.numpy as jnp
from jax import lax
from jax.sharding import PartitionSpec as P

MODES_X = 8
MODES_Y = 8
STEPS = 2


HIGHEST_PRECISION = lax.Precision.HIGHEST


def passed_along(block, axis, distance):
    devices = range(lax.axis_size(axis))
    route = [((i - distance) % len(devices), i) for i in devices]
    return lax.ppermute(block, axis, route)


def pointwise(weights, inputs, biases):
    return (
        jnp.einsum("io,ixy->oxy", weights, inputs, precision=HIGHEST_PRECISION)
        + biases[:, None, None]
    )


def pool_block(current, factor):
    channels, tile_rows, tile_cols = current.shape
    return current.reshape(channels, tile_rows // factor, factor, tile_cols // factor, factor).mean(
        axis=(2, 4)
    )


def offset_piece(level, extent, offset, dim):
    length = level.shape[dim]
    halfway = length // 2
    if offset == -extent:
        return lax.slice_in_dim(level, halfway, length, axis=dim)
    if offset == extent:
        return lax.slice_in_dim(level, 0, halfway, axis=dim)
    return level


def assemble_near(levels, dim, sender):
    extents = [2**ordinal for ordinal in range(len(levels))]
    greatest = max(extents)
    received = {}
    for offset in list(range(-greatest, 0)) + list(range(1, greatest + 1)):
        pieces = []
        for ordinal in range(len(levels)):
            if extents[ordinal] >= abs(offset):
                pieces.append(
                    (ordinal, offset_piece(levels[ordinal], extents[ordinal], offset, dim))
                )
        buffer = jnp.concatenate([piece.reshape(-1) for ordinal, piece in pieces])
        moved = sender(buffer, -offset)
        start = 0
        for ordinal, piece in pieces:
            received[ordinal, offset] = moved[start : start + piece.size].reshape(piece.shape)
            start = start + piece.size
    results = []
    for ordinal in range(len(levels)):
        portions = []
        for offset in range(-extents[ordinal], extents[ordinal] + 1):
            portions.append(levels[ordinal] if offset == 0 else received[ordinal, offset])
        results.append(jnp.concatenate(portions, axis=dim))
    return results


def merged_rows(levels):

    def send_rows(buffer, shift_by):
        return passed_along(buffer, "gx", shift_by)

    return assemble_near(levels, 1, send_rows)


def merged_cols(levels):

    def send_cols(buffer, shift_by):
        return passed_along(buffer, "gy", shift_by)

    return assemble_near(levels, 2, send_cols)


def fourier_tables(tile_rows, tile_cols):
    ordinal_cols = jnp.arange(MODES_Y, dtype=jnp.int32)
    ordinal_rows = jnp.arange(MODES_X, dtype=jnp.int32)
    signed_modes = jnp.where(ordinal_rows < MODES_X // 2, ordinal_rows, ordinal_rows - MODES_X)
    phase_cols = (
        jnp.arange(tile_cols, dtype=jnp.int32)[:, None] * ordinal_cols[None, :] % tile_cols
    ).astype(jnp.float32) * (2.0 * math.pi / tile_cols)
    phase_rows = (
        jnp.arange(tile_rows, dtype=jnp.int32)[:, None] * signed_modes[None, :] % tile_rows
    ).astype(jnp.float32) * (2.0 * math.pi / tile_rows)
    forward_cols = jnp.concatenate([jnp.cos(phase_cols), -jnp.sin(phase_cols)], axis=1)
    fold_weights = jnp.where(ordinal_cols == 0, 1.0, 2.0).astype(jnp.float32) / (
        tile_rows * tile_cols
    )
    inverse_cols = jnp.concatenate(
        [
            jnp.cos(phase_cols).T * fold_weights[:, None],
            -jnp.sin(phase_cols).T * fold_weights[:, None],
        ],
        axis=0,
    )
    return (forward_cols, jnp.cos(phase_rows), jnp.sin(phase_rows), inverse_cols)


def spectral_apply(hidden, tables, spectral_weight):
    forward_cols, cosine_rows, sine_rows, inverse_cols = tables
    channels, tile_rows, tile_cols = hidden.shape
    along_cols = jnp.dot(
        hidden.reshape(channels * tile_rows, tile_cols), forward_cols, precision=HIGHEST_PRECISION
    )
    along_cols = along_cols.reshape(channels, tile_rows, 2, MODES_Y)
    real_cols = along_cols[:, :, 0]
    imag_cols = along_cols[:, :, 1]
    real_modes = jnp.einsum(
        "cxj,xk->ckj", real_cols, cosine_rows, precision=HIGHEST_PRECISION
    ) + jnp.einsum("cxj,xk->ckj", imag_cols, sine_rows, precision=HIGHEST_PRECISION)
    imag_modes = jnp.einsum(
        "cxj,xk->ckj", imag_cols, cosine_rows, precision=HIGHEST_PRECISION
    ) - jnp.einsum("cxj,xk->ckj", real_cols, sine_rows, precision=HIGHEST_PRECISION)
    weight_real = spectral_weight[0]
    weight_imag = spectral_weight[1]
    out_real = jnp.einsum(
        "ckj,kjco->okj", real_modes, weight_real, precision=HIGHEST_PRECISION
    ) - jnp.einsum("ckj,kjco->okj", imag_modes, weight_imag, precision=HIGHEST_PRECISION)
    out_imag = jnp.einsum(
        "ckj,kjco->okj", real_modes, weight_imag, precision=HIGHEST_PRECISION
    ) + jnp.einsum("ckj,kjco->okj", imag_modes, weight_real, precision=HIGHEST_PRECISION)
    back_real = jnp.einsum(
        "okj,xk->oxj", out_real, cosine_rows, precision=HIGHEST_PRECISION
    ) - jnp.einsum("okj,xk->oxj", out_imag, sine_rows, precision=HIGHEST_PRECISION)
    back_imag = jnp.einsum(
        "okj,xk->oxj", out_real, sine_rows, precision=HIGHEST_PRECISION
    ) + jnp.einsum("okj,xk->oxj", out_imag, cosine_rows, precision=HIGHEST_PRECISION)
    outputs = back_real.shape[0]
    stacked = jnp.concatenate([back_real, back_imag], axis=2).reshape(
        outputs * tile_rows, 2 * MODES_Y
    )
    return jnp.dot(stacked, inverse_cols, precision=HIGHEST_PRECISION).reshape(
        outputs, tile_rows, tile_cols
    )


def shards(
    fields,
    lift_weight,
    lift_bias,
    spectral_weight,
    bypass_weight,
    layer_bias,
    mlp_in_weight,
    mlp_in_bias,
    mlp_out_weight,
    mlp_out_bias,
    project_weight,
    project_bias,
):
    channels, tile_rows, tile_cols = fields.shape
    tables = fourier_tables(tile_rows, tile_cols)
    current = fields
    for rollout in range(STEPS):
        pooled_levels = [pool_block(current, 2 ** (ordinal + 1)) for ordinal in range(3)]
        contexts = merged_cols(merged_rows(pooled_levels))
        features = jnp.concatenate([current] + contexts, axis=0)
        hidden = pointwise(lift_weight, features, lift_bias)
        spectral = spectral_apply(hidden, tables, spectral_weight)
        mixed = jax.nn.gelu(spectral + pointwise(bypass_weight, hidden, layer_bias))
        inner = jax.nn.gelu(pointwise(mlp_in_weight, mixed, mlp_in_bias))
        refined = mixed + pointwise(mlp_out_weight, inner, mlp_out_bias)
        current = current + pointwise(project_weight, refined, project_bias)
    return current


def solution(mesh):
    placed = (P(None, "gx", "gy"), P(), P(), P(), P(), P(), P(), P(), P(), P(), P(), P())
    return jax.shard_map(
        shards, mesh=mesh, in_specs=placed, out_specs=P(None, "gx", "gy"), check_vma=False
    )
```

profile of v0, /device:TPU:1, one launch (start us, length us, event | category | flops | bytes accessed | tf_op | source)
XLA Modules:
  0.0 279.1 jit_solution(9687122077670750319)
XLA Ops:
  0.0 1.2 reshape.510
  1.5 13.3 %collective-permute-start.5 = (f32[192]{0:T(256)S(1)}, f32[192]{0:T(256)S(1)}, u32[]{:S(2)}, u32[]{:S(2)}) collective-permute-start(f32[192]{0:T(256)S(1)} %div.35), channel_id=1, source_target_pairs={{416,0},{448,32},{480,64},{0,96},{32,128},{64,160},{96,192},{128,2... | collective-permute-start | bytes 2312 | tf_op jit(solution)/shard_map/ppermute | solution.py:19
  14.8 1.9 collective-permute-start.6
  16.8 3.1 %collective-permute-start.4 = (f32[96]{0:T(128)S(1)}, f32[96]{0:T(128)S(1)}, u32[]{:S(2)}, u32[]{:S(2)}) collective-permute-start(f32[96]{0:T(128)S(1)} %reshape.522), channel_id=1, source_target_pairs={{384,0},{416,32},{448,64},{480,96},{0,128},{32,160},{64,192},{96,2... | collective-permute-start | bytes 1160 | tf_op jit(solution)/shard_map/ppermute | solution.py:19
  20.0 3.4 %collective-permute-start.7 = (f32[96]{0:T(128)S(1)}, f32[96]{0:T(128)S(1)}, u32[]{:S(2)}, u32[]{:S(2)}) collective-permute-start(f32[96]{0:T(128)S(1)} %reshape.530), channel_id=1, source_target_pairs={{128,0},{160,32},{192,64},{224,96},{256,128},{288,160},{320,192},{... | collective-permute-start | bytes 1160 | tf_op jit(solution)/shard_map/ppermute | solution.py:19
  23.4 2.4 reshape.509
  26.2 12.1 %collective-permute-start.3 = (f32[576]{0:T(1024)S(1)}, f32[576]{0:T(1024)S(1)}, u32[]{:S(2)}, u32[]{:S(2)}) collective-permute-start(f32[576]{0:T(1024)S(1)} %get-tuple-element.63), channel_id=1, source_target_pairs={{64,0},{96,32},{128,64},{160,96},{192,128},{224,160},{256,192},{28... | collective-permute-start | bytes 6920 | tf_op jit(solution)/shard_map/ppermute | solution.py:19
  38.4 3.2 %reshape.507 = f32[3,16,2,64,2]{4,3,2,1,0:T(8,128)S(1)} reshape(f32[3,32,128]{2,1,0:T(8,128)S(1)} %copy-done.3) | data formatting | bytes 98304 | tf_op jit(solution)/shard_map/reshape | solution.py:31
  42.4 2.1 collective-permute-start.2
  44.6 10.1 %collective-permute-start.1 = (f32[2496]{0:T(1024)S(1)}, f32[2496]{0:T(1024)S(1)}, u32[]{:S(2)}, u32[]{:S(2)}) collective-permute-start(f32[2496]{0:T(1024)S(1)} %get-tuple-element.59), channel_id=1, source_target_pairs={{32,0},{64,32},{96,64},{128,96},{160,128},{192,160},{224,192},{256... | collective-permute-start | bytes 29960 | tf_op jit(solution)/shard_map/ppermute | solution.py:19
  54.7 1.9 collective-permute-start
  57.9 7.3 %collective-permute-done = f32[2496]{0:T(1024)S(1)} collective-permute-done((f32[2496]{0:T(1024)S(1)}, f32[2496]{0:T(1024)S(1)}, u32[]{:S(2)}, u32[]{:S(2)}) %collective-permute-start) | collective-permute-done | bytes 10016 | tf_op jit(solution)/shard_map/ppermute | solution.py:19
  65.7 8.5 %collective-permute-start.13 = (f32[1536]{0:T(1024)S(1)}, f32[1536]{0:T(1024)S(1)}, u32[]{:S(2)}, u32[]{:S(2)}) collective-permute-start(f32[1536]{0:T(1024)S(1)} %reshape.532), channel_id=1, source_target_pairs={{29,0},{30,1},{31,2},{0,3},{1,4},{2,5},{3,6},{4,7},{5,8},{6,9},{7,... | collective-permute-start | bytes 18440 | tf_op jit(solution)/shard_map/ppermute | solution.py:19
  74.1 3.1 %collective-permute-start.14 = (f32[1536]{0:T(1024)S(1)}, f32[1536]{0:T(1024)S(1)}, u32[]{:S(2)}, u32[]{:S(2)}) collective-permute-start(f32[1536]{0:T(1024)S(1)} %reshape.532), channel_id=1, source_target_pairs={{3,0},{4,1},{5,2},{6,3},{7,4},{8,5},{9,6},{10,7},{11,8},{12,9},{13... | collective-permute-start | bytes 18440 | tf_op jit(solution)/shard_map/ppermute | solution.py:19
  78.6 4.2 %collective-permute-start.11 = (f32[3072]{0:T(1024)S(1)}, f32[3072]{0:T(1024)S(1)}, u32[]{:S(2)}, u32[]{:S(2)}) collective-permute-start(f32[3072]{0:T(1024)S(1)} %get-tuple-element.51), channel_id=1, source_target_pairs={{2,0},{3,1},{4,2},{5,3},{6,4},{7,5},{8,6},{9,7},{10,8},{11,9},{12,... | collective-permute-start | bytes 36872 | tf_op jit(solution)/shard_map/ppermute | solution.py:19
  82.9 1.9 collective-permute-start.12
  84.9 7.6 %collective-permute-start.15 = (f32[768]{0:T(1024)S(1)}, f32[768]{0:T(1024)S(1)}, u32[]{:S(2)}, u32[]{:S(2)}) collective-permute-start(f32[768]{0:T(1024)S(1)} %reshape.550), channel_id=1, source_target_pairs={{4,0},{5,1},{6,2},{7,3},{8,4},{9,5},{10,6},{11,7},{12,8},{13,9},{1... | collective-permute-start | bytes 9224 | tf_op jit(solution)/shard_map/ppermute | solution.py:19
  93.2 4.4 %collective-permute-start.9 = (f32[7680]{0:T(1024)S(1)}, f32[7680]{0:T(1024)S(1)}, u32[]{:S(2)}, u32[]{:S(2)}) collective-permute-start(f32[7680]{0:T(1024)S(1)} %get-tuple-element.35), channel_id=1, source_target_pairs={{1,0},{2,1},{3,2},{4,3},{5,4},{6,5},{7,6},{8,7},{9,8},{10,9},{11,1... | collective-permute-start | bytes 92168 | tf_op jit(solution)/shard_map/ppermute | solution.py:19
  97.7 1.9 collective-permute-start.8
  99.7 2.9 %collective-permute-start.10 = (f32[3072]{0:T(1024)S(1)}, f32[3072]{0:T(1024)S(1)}, u32[]{:S(2)}, u32[]{:S(2)}) collective-permute-start(f32[3072]{0:T(1024)S(1)} %get-tuple-element.52), channel_id=1, source_target_pairs={{30,0},{31,1},{0,2},{1,3},{2,4},{3,5},{4,6},{5,7},{6,8},{7,9},{8,1... | collective-permute-start | bytes 36872 | tf_op jit(solution)/shard_map/ppermute | solution.py:19
  102.8 7.5 %collective-permute-done.10 = f32[3072]{0:T(1024)S(1)} collective-permute-done((f32[3072]{0:T(1024)S(1)}, f32[3072]{0:T(1024)S(1)}, u32[]{:S(2)}, u32[]{:S(2)}) %collective-permute-start.10) | collective-permute-done | bytes 12320 | tf_op jit(solution)/shard_map/ppermute | solution.py:19
  111.6 1.0 convolution_add_fusion.3
  112.7 4.2 %fusion.72 = f32[64,32,2,8]{1,3,2,0:T(8,128)S(1)} fusion(f32[64,32,128,1]{2,0,1,3:T(8,128)S(1)} %bitcast.248, f32[128,8]{0,1:T(8,128)S(1)} %get-tuple-element.67, f32[128,8]{0,1:T(8,128)S(1)} %get-tuple-element.68), kind=kOutput, calls=%fused_computation.88 | convolution fusion | flops 50333696 | bytes 1187840 | tf_op jit(solution)/shard_map/dot_general | solution.py:115
  118.2 3.6 %fusion.32 = f32[8,8,1,64]{3,2,1,0:T(1,128)S(1)} fusion(f32[2,8,8,64,64]{4,3,2,1,0:T(8,128)} %param.15, f32[64,8,8,1]{0,1,2,3:T(8,128)S(1)} %fusion.52), kind=kOutput, calls=%fused_computation.32 | convolution fusion | flops 3145728 | bytes 2129920 | tf_op jit(solution)/shard_map/ckj,kjco->okj/dot_general | solution.py:134
  121.7 3.4 %fusion.26 = f32[8,8,1,64]{3,2,1,0:T(1,128)S(1)} fusion(f32[2,8,8,64,64]{4,3,2,1,0:T(8,128)} %param.15, f32[64,8,8,1]{0,1,2,3:T(8,128)S(1)} %fusion.52), kind=kOutput, calls=%fused_computation.26 | convolution fusion | flops 3145728 | bytes 2129920 | tf_op jit(solution)/shard_map/ckj,kjco->okj/dot_general | solution.py:131
  125.4 1.9 fusion.24
  127.3 2.3 fusion.34
  131.7 1.0 fusion.74
  132.8 2.6 fusion.60
  135.5 3.7 %fusion.82 = f32[32,128,128]{2,1,0:T(8,128)S(1)} fusion(f32[64,32,128]{2,1,0:T(8,128)S(1)} %fusion.60, f32[64,128]{1,0:T(8,128)S(1)} %copy-done), kind=kOutput, calls=%fused_computation.101 | convolution fusion | flops 402653184 | bytes 3178496 | tf_op jit(solution)/shard_map/io,ixy->oxy/dot_general | solution.py:24
  139.2 3.0 %fusion.7 = f32[32,128,64]{1,2,0:T(8,128)S(1)} fusion(f32[32,128,128]{2,1,0:T(8,128)S(1)} %fusion.82, f32[128]{0:T(128)S(1)} %copy-done.12, f32[128,64]{0,1:T(8,128)S(1)} %copy-done.10), kind=kOutput, calls=%fused_computation.9 | convolution fusion | flops 407371776 | bytes 3179008 | tf_op jit(solution)/shard_map/io,ixy->oxy/dot_general | solution.py:24
  142.9 1.4 fusion.80
  145.1 1.6 reshape.554
  147.0 3.2 %reshape.552 = f32[3,16,2,64,2]{4,3,2,1,0:T(8,128)S(1)} reshape(f32[3,32,128]{2,1,0:T(8,128)S(1)} %bitcast_add_fusion.3) | data formatting | bytes 98304 | tf_op jit(solution)/shard_map/reshape | solution.py:31
  150.2 1.9 collective-permute-start.20
  153.0 5.3 %collective-permute-start.17 = (f32[2496]{0:T(1024)S(1)}, f32[2496]{0:T(1024)S(1)}, u32[]{:S(2)}, u32[]{:S(2)}) collective-permute-start(f32[2496]{0:T(1024)S(1)} %get-tuple-element.57), channel_id=1, source_target_pairs={{32,0},{64,32},{96,64},{128,96},{160,128},{192,160},{224,192},{256... | collective-permute-start | bytes 29960 | tf_op jit(solution)/shard_map/ppermute | solution.py:19
  158.3 3.8 %collective-permute-start.16 = (f32[2496]{0:T(1024)S(1)}, f32[2496]{0:T(1024)S(1)}, u32[]{:S(2)}, u32[]{:S(2)}) collective-permute-start(f32[2496]{0:T(1024)S(1)} %get-tuple-element.58), channel_id=1, source_target_pairs={{480,0},{0,32},{32,64},{64,96},{96,128},{128,160},{160,192},{192,2... | collective-permute-start | bytes 29960 | tf_op jit(solution)/shard_map/ppermute | solution.py:19
  162.2 5.4 %collective-permute-start.19 = (f32[576]{0:T(1024)S(1)}, f32[576]{0:T(1024)S(1)}, u32[]{:S(2)}, u32[]{:S(2)}) collective-permute-start(f32[576]{0:T(1024)S(1)} %get-tuple-element.61), channel_id=1, source_target_pairs={{64,0},{96,32},{128,64},{160,96},{192,128},{224,160},{256,192},{28... | collective-permute-start | bytes 6920 | tf_op jit(solution)/shard_map/ppermute | solution.py:19
  167.7 1.9 collective-permute-start.23
  169.6 11.3 %collective-permute-start.18 = (f32[576]{0:T(1024)S(1)}, f32[576]{0:T(1024)S(1)}, u32[]{:S(2)}, u32[]{:S(2)}) collective-permute-start(f32[576]{0:T(1024)S(1)} %get-tuple-element.62), channel_id=1, source_target_pairs={{448,0},{480,32},{0,64},{32,96},{64,128},{96,160},{128,192},{160,2... | collective-permute-start | bytes 6920 | tf_op jit(solution)/shard_map/ppermute | solution.py:19
  180.9 6.0 %collective-permute-start.21 = (f32[192]{0:T(256)S(1)}, f32[192]{0:T(256)S(1)}, u32[]{:S(2)}, u32[]{:S(2)}) collective-permute-start(f32[192]{0:T(256)S(1)} %div.41), channel_id=1, source_target_pairs={{416,0},{448,32},{480,64},{0,96},{32,128},{64,160},{96,192},{128,2... | collective-permute-start | bytes 2312 | tf_op jit(solution)/shard_map/ppermute | solution.py:19
  186.8 4.4 %collective-permute-done.21 = f32[192]{0:T(256)S(1)} collective-permute-done((f32[192]{0:T(256)S(1)}, f32[192]{0:T(256)S(1)}, u32[]{:S(2)}, u32[]{:S(2)}) %collective-permute-start.21) | collective-permute-done | bytes 800 | tf_op jit(solution)/shard_map/ppermute | solution.py:19
  191.2 1.9 collective-permute-start.22
  193.4 6.1 %collective-permute-done.22 = f32[192]{0:T(256)S(1)} collective-permute-done((f32[192]{0:T(256)S(1)}, f32[192]{0:T(256)S(1)}, u32[]{:S(2)}, u32[]{:S(2)}) %collective-permute-start.22) | collective-permute-done | bytes 800 | tf_op jit(solution)/shard_map/ppermute | solution.py:19
  200.5 2.4 collective-permute-start.29
  203.0 7.1 %collective-permute-start.30 = (f32[1536]{0:T(1024)S(1)}, f32[1536]{0:T(1024)S(1)}, u32[]{:S(2)}, u32[]{:S(2)}) collective-permute-start(f32[1536]{0:T(1024)S(1)} %reshape.577), channel_id=1, source_target_pairs={{3,0},{4,1},{5,2},{6,3},{7,4},{8,5},{9,6},{10,7},{11,8},{12,9},{13... | collective-permute-start | bytes 18440 | tf_op jit(solution)/shard_map/ppermute | solution.py:19
  211.3 2.3 collective-permute-start.27
  213.8 4.3 %collective-permute-start.28 = (f32[768]{0:T(1024)S(1)}, f32[768]{0:T(1024)S(1)}, u32[]{:S(2)}, u32[]{:S(2)}) collective-permute-start(f32[768]{0:T(1024)S(1)} %reshape.587), channel_id=1, source_target_pairs={{28,0},{29,1},{30,2},{31,3},{0,4},{1,5},{2,6},{3,7},{4,8},{5,9},{6... | collective-permute-start | bytes 9224 | tf_op jit(solution)/shard_map/ppermute | solution.py:19
  218.1 5.2 %collective-permute-start.31 = (f32[768]{0:T(1024)S(1)}, f32[768]{0:T(1024)S(1)}, u32[]{:S(2)}, u32[]{:S(2)}) collective-permute-start(f32[768]{0:T(1024)S(1)} %reshape.595), channel_id=1, source_target_pairs={{4,0},{5,1},{6,2},{7,3},{8,4},{9,5},{10,6},{11,7},{12,8},{13,9},{1... | collective-permute-start | bytes 9224 | tf_op jit(solution)/shard_map/ppermute | solution.py:19
  224.0 8.2 %collective-permute-start.25 = (f32[7680]{0:T(1024)S(1)}, f32[7680]{0:T(1024)S(1)}, u32[]{:S(2)}, u32[]{:S(2)}) collective-permute-start(f32[7680]{0:T(1024)S(1)} %get-tuple-element.33), channel_id=1, source_target_pairs={{1,0},{2,1},{3,2},{4,3},{5,4},{6,5},{7,6},{8,7},{9,8},{10,9},{11,1... | collective-permute-start | bytes 92168 | tf_op jit(solution)/shard_map/ppermute | solution.py:19
  232.3 3.5 %collective-permute-start.24 = (f32[7680]{0:T(1024)S(1)}, f32[7680]{0:T(1024)S(1)}, u32[]{:S(2)}, u32[]{:S(2)}) collective-permute-start(f32[7680]{0:T(1024)S(1)} %get-tuple-element.34), channel_id=1, source_target_pairs={{31,0},{0,1},{1,2},{2,3},{3,4},{4,5},{5,6},{6,7},{7,8},{8,9},{9,10... | collective-permute-start | bytes 92168 | tf_op jit(solution)/shard_map/ppermute | solution.py:19
  236.0 2.0 collective-permute-start.26
  238.2 6.5 %collective-permute-done.26 = f32[3072]{0:T(1024)S(1)} collective-permute-done((f32[3072]{0:T(1024)S(1)}, f32[3072]{0:T(1024)S(1)}, u32[]{:S(2)}, u32[]{:S(2)}) %collective-permute-start.26) | collective-permute-done | bytes 12320 | tf_op jit(solution)/shard_map/ppermute | solution.py:19
  246.0 1.0 convolution_add_fusion.1
  247.0 4.2 %fusion.68 = f32[64,32,2,8]{1,3,2,0:T(8,128)S(1)} fusion(f32[64,32,128,1]{2,0,1,3:T(8,128)S(1)} %bitcast.249, f32[128,8]{0,1:T(8,128)S(1)} %get-tuple-element.67, f32[128,8]{0,1:T(8,128)S(1)} %get-tuple-element.68), kind=kOutput, calls=%fused_computation.83 | convolution fusion | flops 50333696 | bytes 1187840 | tf_op jit(solution)/shard_map/dot_general | solution.py:115
  252.5 3.6 %fusion.28 = f32[8,8,1,64]{3,2,1,0:T(1,128)S(1)} fusion(f32[2,8,8,64,64]{4,3,2,1,0:T(8,128)} %param.15, f32[64,8,8,1]{0,1,2,3:T(8,128)S(1)} %fusion.50), kind=kOutput, calls=%fused_computation.28 | convolution fusion | flops 3145728 | bytes 2129920 | tf_op jit(solution)/shard_map/ckj,kjco->okj/dot_general | solution.py:134
  256.1 3.4 %fusion.22 = f32[8,8,1,64]{3,2,1,0:T(1,128)S(1)} fusion(f32[2,8,8,64,64]{4,3,2,1,0:T(8,128)} %param.15, f32[64,8,8,1]{0,1,2,3:T(8,128)S(1)} %fusion.50), kind=kOutput, calls=%fused_computation.22 | convolution fusion | flops 3145728 | bytes 2129920 | tf_op jit(solution)/shard_map/ckj,kjco->okj/dot_general | solution.py:131
  259.8 1.9 fusion.20
  261.6 2.1 fusion.30
  264.6 1.1 fusion.70
  266.8 2.6 fusion.67
  269.5 3.7 %fusion.78 = f32[32,128,128]{2,1,0:T(8,128)S(1)} fusion(f32[64,32,128]{2,1,0:T(8,128)S(1)} %fusion.67, f32[64,128]{1,0:T(8,128)S(1)} %copy-done), kind=kOutput, calls=%fused_computation.95 | convolution fusion | flops 402653184 | bytes 3178496 | tf_op jit(solution)/shard_map/io,ixy->oxy/dot_general | solution.py:24
  273.2 3.0 %fusion.16 = f32[32,128,64]{1,2,0:T(8,128)S(1)} fusion(f32[32,128,128]{2,1,0:T(8,128)S(1)} %fusion.78, f32[128]{0:T(128)S(1)} %copy-done.12, f32[128,64]{0,1:T(8,128)S(1)} %copy-done.10), kind=kOutput, calls=%fused_computation.17 | convolution fusion | flops 407371776 | bytes 3179008 | tf_op jit(solution)/shard_map/io,ixy->oxy/dot_general | solution.py:24
  276.8 1.2 fusion.76
  (252 shorter events, 23.2 us)
Async XLA Ops:
  0.0 135.4 %copy-start = (f32[64,128]{1,0:T(8,128)S(1)}, f32[64,128]{1,0:T(8,128)}, u32[]{:S(2)}) copy-start(f32[64,128]{1,0:T(8,128)} %param.18) | copy-start | bytes 98308
  1.2 37.2 %copy-start.3 = (f32[3,32,128]{2,1,0:T(8,128)S(1)}, f32[3,32,128]{2,1,0:T(8,128)}, u32[]{:S(2)}) copy-start(f32[3,32,128]{2,1,0:T(8,128)} %param.12) | copy-start | bytes 147460
  1.5 53.2 %collective-permute-start.5 = (f32[192]{0:T(256)S(1)}, f32[192]{0:T(256)S(1)}, u32[]{:S(2)}, u32[]{:S(2)}) collective-permute-start(f32[192]{0:T(256)S(1)} %div.35), channel_id=1, source_target_pairs={{416,0},{448,32},{480,64},{0,96},{32,128},{64,160},{96,192},{128,2... | collective-permute-start | bytes 2312 | tf_op jit(solution)/shard_map/ppermute | solution.py:19
  14.8 42.1 %collective-permute-start.6 = (f32[192]{0:T(256)S(1)}, f32[192]{0:T(256)S(1)}, u32[]{:S(2)}, u32[]{:S(2)}) collective-permute-start(f32[192]{0:T(256)S(1)} %div.35), channel_id=1, source_target_pairs={{96,0},{128,32},{160,64},{192,96},{224,128},{256,160},{288,192},{3... | collective-permute-start | bytes 2312 | tf_op jit(solution)/shard_map/ppermute | solution.py:19
  16.8 25.6 %collective-permute-start.4 = (f32[96]{0:T(128)S(1)}, f32[96]{0:T(128)S(1)}, u32[]{:S(2)}, u32[]{:S(2)}) collective-permute-start(f32[96]{0:T(128)S(1)} %reshape.522), channel_id=1, source_target_pairs={{384,0},{416,32},{448,64},{480,96},{0,128},{32,160},{64,192},{96,2... | collective-permute-start | bytes 1160 | tf_op jit(solution)/shard_map/ppermute | solution.py:19
  20.0 24.6 %collective-permute-start.7 = (f32[96]{0:T(128)S(1)}, f32[96]{0:T(128)S(1)}, u32[]{:S(2)}, u32[]{:S(2)}) collective-permute-start(f32[96]{0:T(128)S(1)} %reshape.530), channel_id=1, source_target_pairs={{128,0},{160,32},{192,64},{224,96},{256,128},{288,160},{320,192},{... | collective-permute-start | bytes 1160 | tf_op jit(solution)/shard_map/ppermute | solution.py:19
  26.2 30.8 %collective-permute-start.3 = (f32[576]{0:T(1024)S(1)}, f32[576]{0:T(1024)S(1)}, u32[]{:S(2)}, u32[]{:S(2)}) collective-permute-start(f32[576]{0:T(1024)S(1)} %get-tuple-element.63), channel_id=1, source_target_pairs={{64,0},{96,32},{128,64},{160,96},{192,128},{224,160},{256,192},{28... | collective-permute-start | bytes 6920 | tf_op jit(solution)/shard_map/ppermute | solution.py:19
  42.2 69.5 %copy-start.5 = (f32[12,64]{1,0:T(8,128)S(1)}, f32[12,64]{1,0:T(8,128)}, u32[]{:S(2)}) copy-start(f32[12,64]{1,0:T(8,128)} %param.13) | copy-start | bytes 9220
  42.2 69.5 %copy-start.7 = (f32[64]{0:T(128)S(1)}, f32[64]{0:T(128)}, u32[]{:S(2)}) copy-start(f32[64]{0:T(128)} %param.14) | copy-start | bytes 772
  42.4 15.2 %collective-permute-start.2 = (f32[576]{0:T(1024)S(1)}, f32[576]{0:T(1024)S(1)}, u32[]{:S(2)}, u32[]{:S(2)}) collective-permute-start(f32[576]{0:T(1024)S(1)} %get-tuple-element.64), channel_id=1, source_target_pairs={{448,0},{480,32},{0,64},{32,96},{64,128},{96,160},{128,192},{160,2... | collective-permute-start | bytes 6920 | tf_op jit(solution)/shard_map/ppermute | solution.py:19
  44.6 13.2 %collective-permute-start.1 = (f32[2496]{0:T(1024)S(1)}, f32[2496]{0:T(1024)S(1)}, u32[]{:S(2)}, u32[]{:S(2)}) collective-permute-start(f32[2496]{0:T(1024)S(1)} %get-tuple-element.59), channel_id=1, source_target_pairs={{32,0},{64,32},{96,64},{128,96},{160,128},{192,160},{224,192},{256... | collective-permute-start | bytes 29960 | tf_op jit(solution)/shard_map/ppermute | solution.py:19
  54.7 10.5 %collective-permute-start = (f32[2496]{0:T(1024)S(1)}, f32[2496]{0:T(1024)S(1)}, u32[]{:S(2)}, u32[]{:S(2)}) collective-permute-start(f32[2496]{0:T(1024)S(1)} %get-tuple-element.60), channel_id=1, source_target_pairs={{480,0},{0,32},{32,64},{64,96},{96,128},{128,160},{160,192},{192,2... | collective-permute-start | bytes 29960 | tf_op jit(solution)/shard_map/ppermute | solution.py:19
  65.7 37.0 %collective-permute-start.13 = (f32[1536]{0:T(1024)S(1)}, f32[1536]{0:T(1024)S(1)}, u32[]{:S(2)}, u32[]{:S(2)}) collective-permute-start(f32[1536]{0:T(1024)S(1)} %reshape.532), channel_id=1, source_target_pairs={{29,0},{30,1},{31,2},{0,3},{1,4},{2,5},{3,6},{4,7},{5,8},{6,9},{7,... | collective-permute-start | bytes 18440 | tf_op jit(solution)/shard_map/ppermute | solution.py:19
  74.1 25.5 %collective-permute-start.14 = (f32[1536]{0:T(1024)S(1)}, f32[1536]{0:T(1024)S(1)}, u32[]{:S(2)}, u32[]{:S(2)}) collective-permute-start(f32[1536]{0:T(1024)S(1)} %reshape.532), channel_id=1, source_target_pairs={{3,0},{4,1},{5,2},{6,3},{7,4},{8,5},{9,6},{10,7},{11,8},{12,9},{13... | collective-permute-start | bytes 18440 | tf_op jit(solution)/shard_map/ppermute | solution.py:19
  78.6 24.2 %collective-permute-start.11 = (f32[3072]{0:T(1024)S(1)}, f32[3072]{0:T(1024)S(1)}, u32[]{:S(2)}, u32[]{:S(2)}) collective-permute-start(f32[3072]{0:T(1024)S(1)} %get-tuple-element.51), channel_id=1, source_target_pairs={{2,0},{3,1},{4,2},{5,3},{6,4},{7,5},{8,6},{9,7},{10,8},{11,9},{12,... | collective-permute-start | bytes 36872 | tf_op jit(solution)/shard_map/ppermute | solution.py:19
  82.9 14.7 %collective-permute-start.12 = (f32[768]{0:T(1024)S(1)}, f32[768]{0:T(1024)S(1)}, u32[]{:S(2)}, u32[]{:S(2)}) collective-permute-start(f32[768]{0:T(1024)S(1)} %reshape.542), channel_id=1, source_target_pairs={{28,0},{29,1},{30,2},{31,3},{0,4},{1,5},{2,6},{3,7},{4,8},{5,9},{6... | collective-permute-start | bytes 9224 | tf_op jit(solution)/shard_map/ppermute | solution.py:19
  84.9 8.3 %collective-permute-start.15 = (f32[768]{0:T(1024)S(1)}, f32[768]{0:T(1024)S(1)}, u32[]{:S(2)}, u32[]{:S(2)}) collective-permute-start(f32[768]{0:T(1024)S(1)} %reshape.550), channel_id=1, source_target_pairs={{4,0},{5,1},{6,2},{7,3},{8,4},{9,5},{10,6},{11,7},{12,8},{13,9},{1... | collective-permute-start | bytes 9224 | tf_op jit(solution)/shard_map/ppermute | solution.py:19
  93.2 17.5 %collective-permute-start.9 = (f32[7680]{0:T(1024)S(1)}, f32[7680]{0:T(1024)S(1)}, u32[]{:S(2)}, u32[]{:S(2)}) collective-permute-start(f32[7680]{0:T(1024)S(1)} %get-tuple-element.35), channel_id=1, source_target_pairs={{1,0},{2,1},{3,2},{4,3},{5,4},{6,5},{7,6},{8,7},{9,8},{10,9},{11,1... | collective-permute-start | bytes 92168 | tf_op jit(solution)/shard_map/ppermute | solution.py:19
  97.7 13.2 %collective-permute-start.8 = (f32[7680]{0:T(1024)S(1)}, f32[7680]{0:T(1024)S(1)}, u32[]{:S(2)}, u32[]{:S(2)}) collective-permute-start(f32[7680]{0:T(1024)S(1)} %get-tuple-element.36), channel_id=1, source_target_pairs={{31,0},{0,1},{1,2},{2,3},{3,4},{4,5},{5,6},{6,7},{7,8},{8,9},{9,10... | collective-permute-start | bytes 92168 | tf_op jit(solution)/shard_map/ppermute | solution.py:19
  99.7 10.7 %collective-permute-start.10 = (f32[3072]{0:T(1024)S(1)}, f32[3072]{0:T(1024)S(1)}, u32[]{:S(2)}, u32[]{:S(2)}) collective-permute-start(f32[3072]{0:T(1024)S(1)} %get-tuple-element.52), channel_id=1, source_target_pairs={{30,0},{31,1},{0,2},{1,3},{2,4},{3,5},{4,6},{5,7},{6,8},{7,9},{8,1... | collective-permute-start | bytes 36872 | tf_op jit(solution)/shard_map/ppermute | solution.py:19
  118.1 7.3 %copy-start.1 = (f32[2,8,8,64,64]{4,3,2,1,0:T(8,128)S(1)}, f32[2,8,8,64,64]{4,3,2,1,0:T(8,128)}, u32[]{:S(2)}) copy-start(f32[2,8,8,64,64]{4,3,2,1,0:T(8,128)} %param.15) | copy-start | bytes 6291460
  127.3 4.4 %copy-start.4 = (f32[64,64]{1,0:T(8,128)S(1)}, f32[64,64]{1,0:T(8,128)}, u32[]{:S(2)}) copy-start(f32[64,64]{1,0:T(8,128)} %param.16) | copy-start | bytes 49156
  130.5 2.3 copy-start.11
  135.4 3.7 %copy-start.10 = (f32[128,64]{0,1:T(8,128)S(1)}, f32[128,64]{0,1:T(8,128)}, u32[]{:S(2)}) copy-start(f32[128,64]{0,1:T(8,128)} %param.20) | copy-start | bytes 98308
  135.5 3.7 %copy-start.12 = (f32[128]{0:T(128)S(1)}, f32[128]{0:T(128)}, u32[]{:S(2)}) copy-start(f32[128]{0:T(128)} %param.19) | copy-start | bytes 1540
  139.2 3.0 %copy-start.9 = (f32[64]{0:T(128)S(1)}, f32[64]{0:T(128)}, u32[]{:S(2)}) copy-start(f32[64]{0:T(128)} %param.21) | copy-start | bytes 772
  142.2 0.7 copy-start.6
  142.2 2.1 copy-start.8
  150.2 19.4 %collective-permute-start.20 = (f32[96]{0:T(128)S(1)}, f32[96]{0:T(128)S(1)}, u32[]{:S(2)}, u32[]{:S(2)}) collective-permute-start(f32[96]{0:T(128)S(1)} %reshape.567), channel_id=1, source_target_pairs={{384,0},{416,32},{448,64},{480,96},{0,128},{32,160},{64,192},{96,2... | collective-permute-start | bytes 1160 | tf_op jit(solution)/shard_map/ppermute | solution.py:19
  153.0 46.9 %collective-permute-start.17 = (f32[2496]{0:T(1024)S(1)}, f32[2496]{0:T(1024)S(1)}, u32[]{:S(2)}, u32[]{:S(2)}) collective-permute-start(f32[2496]{0:T(1024)S(1)} %get-tuple-element.57), channel_id=1, source_target_pairs={{32,0},{64,32},{96,64},{128,96},{160,128},{192,160},{224,192},{256... | collective-permute-start | bytes 29960 | tf_op jit(solution)/shard_map/ppermute | solution.py:19
  158.3 41.7 %collective-permute-start.16 = (f32[2496]{0:T(1024)S(1)}, f32[2496]{0:T(1024)S(1)}, u32[]{:S(2)}, u32[]{:S(2)}) collective-permute-start(f32[2496]{0:T(1024)S(1)} %get-tuple-element.58), channel_id=1, source_target_pairs={{480,0},{0,32},{32,64},{64,96},{96,128},{128,160},{160,192},{192,2... | collective-permute-start | bytes 29960 | tf_op jit(solution)/shard_map/ppermute | solution.py:19
  162.2 37.3 %collective-permute-start.19 = (f32[576]{0:T(1024)S(1)}, f32[576]{0:T(1024)S(1)}, u32[]{:S(2)}, u32[]{:S(2)}) collective-permute-start(f32[576]{0:T(1024)S(1)} %get-tuple-element.61), channel_id=1, source_target_pairs={{64,0},{96,32},{128,64},{160,96},{192,128},{224,160},{256,192},{28... | collective-permute-start | bytes 6920 | tf_op jit(solution)/shard_map/ppermute | solution.py:19
  167.7 13.2 %collective-permute-start.23 = (f32[96]{0:T(128)S(1)}, f32[96]{0:T(128)S(1)}, u32[]{:S(2)}, u32[]{:S(2)}) collective-permute-start(f32[96]{0:T(128)S(1)} %reshape.575), channel_id=1, source_target_pairs={{128,0},{160,32},{192,64},{224,96},{256,128},{288,160},{320,192},{... | collective-permute-start | bytes 1160 | tf_op jit(solution)/shard_map/ppermute | solution.py:19
  169.6 30.1 %collective-permute-start.18 = (f32[576]{0:T(1024)S(1)}, f32[576]{0:T(1024)S(1)}, u32[]{:S(2)}, u32[]{:S(2)}) collective-permute-start(f32[576]{0:T(1024)S(1)} %get-tuple-element.62), channel_id=1, source_target_pairs={{448,0},{480,32},{0,64},{32,96},{64,128},{96,160},{128,192},{160,2... | collective-permute-start | bytes 6920 | tf_op jit(solution)/shard_map/ppermute | solution.py:19
  180.9 10.3 %collective-permute-start.21 = (f32[192]{0:T(256)S(1)}, f32[192]{0:T(256)S(1)}, u32[]{:S(2)}, u32[]{:S(2)}) collective-permute-start(f32[192]{0:T(256)S(1)} %div.41), channel_id=1, source_target_pairs={{416,0},{448,32},{480,64},{0,96},{32,128},{64,160},{96,192},{128,2... | collective-permute-start | bytes 2312 | tf_op jit(solution)/shard_map/ppermute | solution.py:19
  191.2 8.2 %collective-permute-start.22 = (f32[192]{0:T(256)S(1)}, f32[192]{0:T(256)S(1)}, u32[]{:S(2)}, u32[]{:S(2)}) collective-permute-start(f32[192]{0:T(256)S(1)} %div.41), channel_id=1, source_target_pairs={{96,0},{128,32},{160,64},{192,96},{224,128},{256,160},{288,192},{3... | collective-permute-start | bytes 2312 | tf_op jit(solution)/shard_map/ppermute | solution.py:19
  200.5 37.5 %collective-permute-start.29 = (f32[1536]{0:T(1024)S(1)}, f32[1536]{0:T(1024)S(1)}, u32[]{:S(2)}, u32[]{:S(2)}) collective-permute-start(f32[1536]{0:T(1024)S(1)} %reshape.577), channel_id=1, source_target_pairs={{29,0},{30,1},{31,2},{0,3},{1,4},{2,5},{3,6},{4,7},{5,8},{6,9},{7,... | collective-permute-start | bytes 18440 | tf_op jit(solution)/shard_map/ppermute | solution.py:19
  203.0 33.0 %collective-permute-start.30 = (f32[1536]{0:T(1024)S(1)}, f32[1536]{0:T(1024)S(1)}, u32[]{:S(2)}, u32[]{:S(2)}) collective-permute-start(f32[1536]{0:T(1024)S(1)} %reshape.577), channel_id=1, source_target_pairs={{3,0},{4,1},{5,2},{6,3},{7,4},{8,5},{9,6},{10,7},{11,8},{12,9},{13... | collective-permute-start | bytes 18440 | tf_op jit(solution)/shard_map/ppermute | solution.py:19
  211.3 26.9 %collective-permute-start.27 = (f32[3072]{0:T(1024)S(1)}, f32[3072]{0:T(1024)S(1)}, u32[]{:S(2)}, u32[]{:S(2)}) collective-permute-start(f32[3072]{0:T(1024)S(1)} %get-tuple-element.49), channel_id=1, source_target_pairs={{2,0},{3,1},{4,2},{5,3},{6,4},{7,5},{8,6},{9,7},{10,8},{11,9},{12,... | collective-permute-start | bytes 36872 | tf_op jit(solution)/shard_map/ppermute | solution.py:19
  213.8 18.5 %collective-permute-start.28 = (f32[768]{0:T(1024)S(1)}, f32[768]{0:T(1024)S(1)}, u32[]{:S(2)}, u32[]{:S(2)}) collective-permute-start(f32[768]{0:T(1024)S(1)} %reshape.587), channel_id=1, source_target_pairs={{28,0},{29,1},{30,2},{31,3},{0,4},{1,5},{2,6},{3,7},{4,8},{5,9},{6... | collective-permute-start | bytes 9224 | tf_op jit(solution)/shard_map/ppermute | solution.py:19
  218.1 6.0 %collective-permute-start.31 = (f32[768]{0:T(1024)S(1)}, f32[768]{0:T(1024)S(1)}, u32[]{:S(2)}, u32[]{:S(2)}) collective-permute-start(f32[768]{0:T(1024)S(1)} %reshape.595), channel_id=1, source_target_pairs={{4,0},{5,1},{6,2},{7,3},{8,4},{9,5},{10,6},{11,7},{12,8},{13,9},{1... | collective-permute-start | bytes 9224 | tf_op jit(solution)/shard_map/ppermute | solution.py:19
  224.0 21.0 %collective-permute-start.25 = (f32[7680]{0:T(1024)S(1)}, f32[7680]{0:T(1024)S(1)}, u32[]{:S(2)}, u32[]{:S(2)}) collective-permute-start(f32[7680]{0:T(1024)S(1)} %get-tuple-element.33), channel_id=1, source_target_pairs={{1,0},{2,1},{3,2},{4,3},{5,4},{6,5},{7,6},{8,7},{9,8},{10,9},{11,1... | collective-permute-start | bytes 92168 | tf_op jit(solution)/shard_map/ppermute | solution.py:19
  232.3 12.9 %collective-permute-start.24 = (f32[7680]{0:T(1024)S(1)}, f32[7680]{0:T(1024)S(1)}, u32[]{:S(2)}, u32[]{:S(2)}) collective-permute-start(f32[7680]{0:T(1024)S(1)} %get-tuple-element.34), channel_id=1, source_target_pairs={{31,0},{0,1},{1,2},{2,3},{3,4},{4,5},{5,6},{6,7},{7,8},{8,9},{9,10... | collective-permute-start | bytes 92168 | tf_op jit(solution)/shard_map/ppermute | solution.py:19
  236.0 8.7 %collective-permute-start.26 = (f32[3072]{0:T(1024)S(1)}, f32[3072]{0:T(1024)S(1)}, u32[]{:S(2)}, u32[]{:S(2)}) collective-permute-start(f32[3072]{0:T(1024)S(1)} %get-tuple-element.50), channel_id=1, source_target_pairs={{30,0},{31,1},{0,2},{1,3},{2,4},{3,5},{4,6},{5,7},{6,8},{7,9},{8,1... | collective-permute-start | bytes 36872 | tf_op jit(solution)/shard_map/ppermute | solution.py:19
  252.5 7.3 %copy-start.2 = (f32[2,8,8,64,64]{4,3,2,1,0:T(8,128)S(1)}, f32[2,8,8,64,64]{4,3,2,1,0:T(8,128)}, u32[]{:S(2)}) copy-start(f32[2,8,8,64,64]{4,3,2,1,0:T(8,128)} %param.15) | copy-start | bytes 6291460
where the time goes:
time: 285 us; the launch traced here: 279 us
  starting transfers between devices  155 us (54%)
  matrix products  61.8 us (22%)
  waiting for transfers between devices  33.6 us (12%)
  local copies, waits for them, and re-layouts  22.8 us (8%)
  other arithmetic  4.19 us (1%)
    ppermute x32, starting transfers between devices, passed_along(): return lax.ppermute(block, axis, route)  155 us
    ppermute x32, waiting for transfers between devices, passed_along(): return lax.ppermute(block, axis, route)  33.6 us
    dot_general x10, matrix products, pointwise(): jnp.einsum('io,ixy->oxy', weights, inputs, precision=HIGHEST_PRECISION)  20.1 us
    reshape x6, local copies, waits for them, and re-layouts, pool_block(): current.reshape(channels, tile_rows // factor, factor, tile_cols // facto...  12 us
    dot_general x2, matrix products, spectral_apply(): jnp.dot(hidden.reshape(channels * tile_rows, tile_cols), forward_cols, pr...  8.49 us
    dot_general x2, matrix products, spectral_apply(): jnp.einsum('ckj,kjco->okj', imag_modes, weight_real, precision=HIGHEST_PR...  7.13 us
    dot_general x2, matrix products, spectral_apply(): jnp.einsum('ckj,kjco->okj', imag_modes, weight_imag, precision=HIGHEST_PR...  6.83 us
  transfers between devices with their start and end apart: 32, of which 8 were waited for; matrix products, arithmetic and copies ran while one was open for 5% of the time, Pallas kernels for 0%

commit v1 on v0

v1 whole, which is shorter than its diff:
```python
import math

import jax
import jax.numpy as jnp
import numpy as np
from jax import lax
from jax.experimental import pallas as pl
from jax.experimental.pallas import tpu as pltpu
from jax.sharding import PartitionSpec as P

STEPS = 2
ROWS = 32
COLS = 128
FEATURES = 12
PADDED = 16
LANE_L3 = 64
LANE_L2 = 80
LANE_L3_COPY = 112

BF16 = jnp.bfloat16
F32 = jnp.float32
GELU_SCALE = math.sqrt(2.0 / math.pi)


def pool_tables():
    columns = np.zeros((COLS, 128), np.float32)
    for cell in range(COLS):
        columns[cell, cell // 2] = 0.5
        columns[cell, LANE_L2 + cell // 4] = 0.25
        columns[cell, LANE_L3 + cell // 8] = 0.125
        columns[cell, LANE_L3_COPY + cell // 8] = 0.125
    rows = np.zeros((96, 96), np.float32)
    for channel in range(3):
        for sub in range(8):
            for kind, (factor, row) in enumerate(
                [(2, sub), (2, sub + 8), (4, (sub + 4) % 8), (8, (sub + 2) % 4)]
            ):
                for inner in range(factor):
                    rows[channel * 32 + kind * 8 + sub, channel * 32 + row * factor + inner] = (
                        1.0 / factor
                    )
    return (
        np.concatenate([columns, columns], axis=0),
        np.concatenate([rows, rows], axis=1),
    )


def fourier_tables():
    signed = np.array([0, 1, 2, 3, -4, -3, -2, -1])
    theta = 2.0 * np.pi * ((signed[:, None] * np.arange(ROWS)[None, :]) % ROWS) / ROWS
    phi = 2.0 * np.pi * ((np.arange(8)[:, None] * np.arange(COLS)[None, :]) % COLS) / COLS
    forward_rows = np.zeros((256, ROWS * PADDED))
    for feature in range(FEATURES):
        for mode in range(8):
            for row in range(ROWS):
                forward_rows[feature * 8 + mode, row * PADDED + feature] = math.cos(
                    theta[mode, row]
                )
                forward_rows[128 + feature * 8 + mode, row * PADDED + feature] = -math.sin(
                    theta[mode, row]
                )
    forward_cols = np.concatenate([np.cos(phi), -np.sin(phi)], axis=0)
    inverse_rows = np.zeros((2, 8, 8, ROWS, 2, 8))
    for mode in range(8):
        for column in range(8):
            inverse_rows[0, mode, column, :, 0, column] = np.cos(theta[mode])
            inverse_rows[1, mode, column, :, 0, column] = -np.sin(theta[mode])
            inverse_rows[0, mode, column, :, 1, column] = np.sin(theta[mode])
            inverse_rows[1, mode, column, :, 1, column] = np.cos(theta[mode])
    weight = np.where(np.arange(8) == 0, 1.0, 2.0)[:, None] / (ROWS * COLS)
    inverse_cols = np.zeros((4, 8, 16, 2, COLS))
    for pair in range(4):
        for half in range(2):
            inverse_cols[pair, 2 * pair + half, :8, half] = weight * np.cos(phi)
            inverse_cols[pair, 2 * pair + half, 8:, half] = -weight * np.sin(phi)
    return (
        forward_rows,
        forward_cols,
        inverse_rows.reshape(128, 512),
        inverse_cols.reshape(4 * 128, 256),
    )


def halves_of_table(table):
    table = jnp.asarray(table.astype(np.float32))
    high = table.astype(BF16)
    low = (table - high.astype(F32)).astype(BF16)
    return high, low


def split(value):
    high = value.astype(BF16)
    return high, (value - high.astype(F32)).astype(BF16)


def matmul(left, right):
    return jnp.dot(left, right, preferred_element_type=F32)


def product(left, right):
    left_high, left_low = left
    right_high, right_low = right
    return (
        matmul(left_high, right_high) + matmul(left_high, right_low) + matmul(left_low, right_high)
    )


def gelu(value):
    inner = value * (GELU_SCALE + (GELU_SCALE * 0.044715) * (value * value))
    half = 0.5 * value
    return half + half * jnp.tanh(inner)


def pooled_blocks(flat, pool_columns, pool_rows):
    high, low = split(flat)
    across = matmul(jnp.concatenate([high, low], axis=1), pool_columns)
    high, low = split(across)
    pooled = matmul(pool_rows, jnp.concatenate([high, low], axis=0))
    lane = lax.broadcasted_iota(jnp.int32, (8, 128), 1)
    first = lane < LANE_L3
    second = (lane >= LANE_L2) & (lane < LANE_L3_COPY)
    upper = []
    lower = []
    for channel in range(3):
        base = channel * 32
        coarse = jnp.where(second, pooled[base + 16 : base + 24], pooled[base + 24 : base + 32])
        upper.append(jnp.where(first, pooled[base : base + 8], coarse))
        lower.append(jnp.where(first, pooled[base + 8 : base + 16], coarse))
    return upper, lower


def emit_slots(slots_ref, position, upper, lower):
    count = slots_ref.shape[0]
    for slot in range(count):
        ahead = lax.rem(slot - position + count, count) < count // 2
        for channel in range(3):
            slots_ref[slot, channel] = jnp.where(ahead, lower[channel], upper[channel])


def pool_kernel(current_ref, columns_ref, rows_ref, slots_ref, own_ref):
    flat = current_ref[...].reshape(96, 128)
    upper, lower = pooled_blocks(flat, columns_ref[...], rows_ref[...])
    for channel in range(3):
        own_ref[0, channel] = upper[channel]
        own_ref[1, channel] = lower[channel]
    emit_slots(slots_ref, lax.axis_index("gx"), upper, lower)


def strip_kernel(own_ref, got_ref, ready_ref, slots_ref, strip_ref):
    position = lax.axis_index("gx")
    lane = lax.broadcasted_iota(jnp.int32, (8, 128), 1)
    sub = lax.broadcasted_iota(jnp.int32, (8, 128), 0)
    first = lane < LANE_L3
    second = (lane >= LANE_L2) & (lane < LANE_L3_COPY)
    top = sub < 4
    low_two = sub < 2
    high_two = sub >= 6
    quarter = lane // 32

    upper_out = []
    lower_out = []
    for channel in range(3):
        near = {
            offset: got_ref[lax.rem(position + offset + 16, 16), channel]
            for offset in (-4, -3, -2, -1, 1, 2, 3, 4)
        }
        near[0] = own_ref[0, channel]
        finest = [near[-1], own_ref[0, channel], own_ref[1, channel], near[1]]
        middle = [(-2, -1), (-1, 0), (0, 1), (1, 2)]
        coarse = [(-4, -3, -2), (-2, -1, 0), (0, 1, 2), (2, 3, 4)]
        upper = jnp.zeros((8, 128), F32)
        lower = jnp.zeros((8, 128), F32)
        for block in range(4):
            before, after = middle[block]
            start, centre, end = coarse[block]
            wide = jnp.where(
                low_two, near[start], jnp.where(high_two, near[end], near[centre])
            )
            value = jnp.where(
                first,
                finest[block],
                jnp.where(second, jnp.where(top, near[before], near[after]), wide),
            )
            strip_ref[channel, block * 8 : block * 8 + 8] = value
            here = quarter == block
            upper = jnp.where(here, pltpu.roll(value, (32 * block - 64) % 128, 1), upper)
            lower = jnp.where(here, pltpu.roll(value, (32 * block - 96) % 128, 1), lower)
        upper_out.append(upper)
        lower_out.append(lower)
    emit_slots(slots_ref, lax.axis_index("gy"), upper_out, lower_out)


def stacked_left(value):
    high, low = split(value)
    return jnp.concatenate([high, high, low], axis=1)


def stacked_right(value):
    high, low = split(value)
    return jnp.concatenate([high, low, high], axis=0)


def prepare_kernel(
    lift_ref,
    lift_bias_ref,
    weight_ref,
    bypass_ref,
    layer_bias_ref,
    mlp_in_ref,
    mlp_in_bias_ref,
    mlp_out_ref,
    mlp_out_bias_ref,
    project_ref,
    project_bias_ref,
    mixing_ref,
    skip_ref,
    inner_ref,
    inner_bias_ref,
    last_ref,
    offset_ref,
):
    highest = lax.Precision.HIGHEST
    lift = jnp.concatenate(
        [lift_ref[...], lift_bias_ref[...], jnp.zeros((PADDED - FEATURES - 1, 64), F32)], axis=0
    )
    left = stacked_left(lift)

    def mode_step(mode, carry):
        both = jnp.concatenate([weight_ref[0, mode], weight_ref[1, mode]], axis=1)
        mixing_ref[pl.ds(mode, PADDED, stride=64), :] = matmul(left, stacked_right(both))
        return carry

    lax.fori_loop(0, 64, mode_step, 0, unroll=8)

    skip = jnp.dot(lift, bypass_ref[...], precision=highest)
    row = lax.broadcasted_iota(jnp.int32, skip.shape, 0)
    skip = skip + jnp.where(row == FEATURES, layer_bias_ref[...], 0.0)
    square = jnp.concatenate([skip, jnp.zeros((128 - PADDED, 64), F32)], axis=0)
    square = jnp.concatenate([square, jnp.zeros((128, 64), F32)], axis=1)
    skip_ref[...] = stacked_left(jnp.transpose(square)[:64, :PADDED])

    project = jnp.concatenate([project_ref[...], jnp.zeros((5, 64), F32)], axis=0)
    wide = jnp.concatenate([mlp_in_ref[...], jnp.zeros((64, 128), F32)], axis=0)
    inner = jnp.concatenate([jnp.transpose(wide)[:, :64], project], axis=0)
    inner_ref[...] = stacked_left(inner)
    inner_bias_ref[...] = jnp.transpose(jnp.broadcast_to(mlp_in_bias_ref[...], (128, 128)))
    last_ref[...] = stacked_left(jnp.dot(project, mlp_out_ref[...], precision=highest))
    sub = lax.broadcasted_iota(jnp.int32, (8, 3), 0)
    lane = lax.broadcasted_iota(jnp.int32, (8, 3), 1)
    constant = jnp.sum(project * mlp_out_bias_ref[...], axis=1, keepdims=True) + jnp.sum(
        jnp.where(sub == lane, project_bias_ref[...], 0.0), axis=1, keepdims=True
    )
    offset_ref[...] = jnp.broadcast_to(constant, (8, 128))


def contexts(strip_ref, before_ref, after_ref, got_ref, position, channel, block):
    lane = lax.broadcasted_iota(jnp.int32, (8, 128), 1)
    rows = slice(block * 8, block * 8 + 8)
    here = strip_ref[channel, rows]
    before = before_ref[channel, rows]
    after = after_ref[channel, rows]
    far = {
        offset: got_ref[lax.rem(position + offset + 32, 32), channel]
        for offset in (-4, -3, -2, 2, 3, 4)
    }
    packed = 32 * block

    def moved(value, source, target):
        shift = (target - source) % 128
        return value if shift == 0 else pltpu.roll(value, shift, 1)

    def gathered(pieces):
        result = moved(*pieces[-1][1:])
        for piece in reversed(pieces[:-1]):
            result = jnp.where(lane < piece[0], moved(*piece[1:]), result)
        return result

    first = gathered([(32, before, 32, 0), (96, here, 0, 32), (128, after, 0, 96)])
    second = gathered(
        [
            (16, far[-2], packed, 0),
            (48, before, LANE_L2, 16),
            (80, here, LANE_L2, 48),
            (112, after, LANE_L2, 80),
            (128, far[2], packed + 16, 112),
        ]
    )
    third = gathered(
        [
            (8, far[-4], packed + 24, 0),
            (24, far[-3], packed + 16, 8),
            (40, far[-2], packed + 16, 24),
            (56, before, LANE_L3, 40),
            (72, here, LANE_L3, 56),
            (88, after, LANE_L3, 72),
            (104, far[2], packed, 88),
            (120, far[3], packed, 104),
            (128, far[4], packed, 120),
        ]
    )
    return first, second, third


def tile_step(
    current_ref,
    strip_ref,
    before_ref,
    after_ref,
    got_ref,
    mixing_ref,
    skip_ref,
    inner_ref,
    inner_bias_ref,
    last_ref,
    offset_ref,
    rows_high_ref,
    rows_low_ref,
    cols_high_ref,
    cols_low_ref,
    back_rows_high_ref,
    back_rows_low_ref,
    back_cols_high_ref,
    back_cols_low_ref,
    features_ref,
    results_ref,
):
    position = lax.axis_index("gy")
    for channel in range(3):
        for block in range(4):
            pieces = (
                current_ref[channel, block * 8 : block * 8 + 8],
                *contexts(strip_ref, before_ref, after_ref, got_ref, position, channel, block),
            )
            for level in range(4):
                features_ref[
                    pl.ds(block * 8 * PADDED + level * 3 + channel, 8, stride=PADDED), :
                ] = pieces[level]
    for row in range(ROWS):
        tail = lax.broadcasted_iota(jnp.int32, (4, 128), 0)
        features_ref[row * PADDED + FEATURES : (row + 1) * PADDED, :] = jnp.where(
            tail == 0, 1.0, 0.0
        )

    features = split(features_ref[...])
    along_rows = product((rows_high_ref[...], rows_low_ref[...]), features)
    contract = (((1,), (1,)), ((), ()))
    along_high, along_low = split(along_rows)

    def transposed(left, right):
        return lax.dot_general(left, right, contract, preferred_element_type=F32)

    spectrum = (
        transposed(cols_high_ref[...], along_high)
        + transposed(cols_high_ref[...], along_low)
        + transposed(cols_low_ref[...], along_high)
    )
    real = spectrum[:8, :128] - spectrum[8:, 128:]
    imag = spectrum[8:, :128] + spectrum[:8, 128:]
    lane = lax.broadcasted_iota(jnp.int32, (8, 128), 1)
    sub = lax.broadcasted_iota(jnp.int32, (8, 128), 0)
    real = jnp.where(
        (lane == 8 * FEATURES) & (sub == 0), float(ROWS * COLS), jnp.where(lane < 96, real, 0.0)
    )
    modes = []
    sign = jnp.where(lane < 64, -1.0, 1.0)
    for mode in range(8):
        with_real = None
        with_imag = None
        for feature in range(FEATURES + (1 if mode == 0 else 0)):
            place = feature * 8 + mode
            weights = mixing_ref[feature * 64 + mode * 8 : feature * 64 + mode * 8 + 8, :]
            term = jnp.broadcast_to(real[:, place : place + 1], (8, 128)) * weights
            with_real = term if with_real is None else with_real + term
            if feature < FEATURES:
                term = jnp.broadcast_to(imag[:, place : place + 1], (8, 128)) * weights
                with_imag = term if with_imag is None else with_imag + term
        modes.append(with_real + sign * pltpu.roll(with_imag, 64, 1))
    turned = jnp.transpose(jnp.concatenate(modes, axis=0))
    outputs = split(jnp.concatenate([turned[:64], turned[64:]], axis=1))
    back = product(outputs, (back_rows_high_ref[...], back_rows_low_ref[...]))
    stacked = split(
        jnp.concatenate([back[:, 128 * block : 128 * block + 128] for block in range(4)], axis=0)
    )

    skip = skip_ref[...]
    inner_left = inner_ref[...]
    inner_bias = jnp.concatenate([inner_bias_ref[...], inner_bias_ref[...]], axis=1)
    last_left = last_ref[...]
    offset = jnp.concatenate([offset_ref[...], offset_ref[...]], axis=1)
    for pair in range(4):
        table = (
            back_cols_high_ref[pair * 128 : pair * 128 + 128, :],
            back_cols_low_ref[pair * 128 : pair * 128 + 128, :],
        )
        spectral = product(stacked, table)
        for block in range(4):
            row = block * 8 + pair * 2
            cells = jnp.concatenate(
                [
                    features_ref[row * PADDED : (row + 1) * PADDED, :],
                    features_ref[(row + 1) * PADDED : (row + 2) * PADDED, :],
                ],
                axis=1,
            )
            mixed = gelu(
                spectral[block * 64 : block * 64 + 64] + matmul(skip, stacked_right(cells))
            )
            wide = matmul(inner_left, stacked_right(mixed))
            hidden = gelu(wide[:128] + inner_bias)
            total = wide[128:136] + offset + matmul(last_left, stacked_right(hidden))
            results_ref[row * 8 : row * 8 + 8, :] = total[:, :128]
            results_ref[(row + 1) * 8 : (row + 2) * 8, :] = total[:, 128:]
    return [
        current_ref[channel]
        + results_ref[pl.ds(channel, ROWS, stride=8), :]
        for channel in range(3)
    ]


def final_kernel(*refs):
    inputs, next_ref, scratch = refs[:19], refs[19], refs[20:]
    updated = tile_step(*inputs, *scratch)
    for channel in range(3):
        next_ref[channel] = updated[channel]


def middle_kernel(*refs):
    inputs, columns_ref, rows_ref = refs[:19], refs[19], refs[20]
    next_ref, slots_ref, own_ref = refs[21:24]
    updated = tile_step(*inputs, *refs[24:])
    for channel in range(3):
        next_ref[channel] = updated[channel]
    upper, lower = pooled_blocks(
        jnp.concatenate(updated, axis=0), columns_ref[...], rows_ref[...]
    )
    for channel in range(3):
        own_ref[0, channel] = upper[channel]
        own_ref[1, channel] = lower[channel]
    emit_slots(slots_ref, lax.axis_index("gx"), upper, lower)


VMEM = pl.BlockSpec(memory_space=pltpu.VMEM)


def resident(operand):
    return pltpu.with_memory_space_constraint(operand, pltpu.VMEM)


def call(body, name, operands, results, scratch=()):
    return pl.pallas_call(
        body,
        name=name,
        out_shape=[pltpu.VMEM(*(r if isinstance(r[0], tuple) else (r, F32))) for r in results],
        in_specs=[VMEM] * len(operands),
        out_specs=[VMEM] * len(results),
        scratch_shapes=list(scratch),
        compiler_params=pltpu.CompilerParams(vmem_limit_bytes=16 << 20),
    )(
        *(
            operand if operand.ndim == 4 and operand.shape[1] == 64 else resident(operand)
            for operand in operands
        )
    )


def shards(
    fields,
    lift_weight,
    lift_bias,
    spectral_weight,
    bypass_weight,
    layer_bias,
    mlp_in_weight,
    mlp_in_bias,
    mlp_out_weight,
    mlp_out_bias,
    project_weight,
    project_bias,
):
    n_gx = lax.axis_size("gx")
    n_gy = lax.axis_size("gy")
    pool_columns, pool_rows = (jnp.asarray(table).astype(BF16) for table in pool_tables())
    tables = [half for table in fourier_tables() for half in halves_of_table(table)]

    block = (3, 8, 128)
    slots_x, own = call(
        pool_kernel, "pool", [fields, pool_columns, pool_rows], [(n_gx, *block), (2, *block)]
    )
    prepared = call(
        prepare_kernel,
        "prepare",
        [
            lift_weight,
            lift_bias[None],
            spectral_weight.reshape(2, 64, 64, 64),
            bypass_weight,
            layer_bias[None],
            mlp_in_weight,
            mlp_in_bias[None],
            mlp_out_weight.T,
            mlp_out_bias[None],
            project_weight.T,
            project_bias[None],
        ],
        [
            (PADDED * 64, 128),
            ((64, 3 * PADDED), BF16),
            ((136, 192), BF16),
            (128, 128),
            ((8, 384), BF16),
            (8, 128),
        ],
    )

    forward = [(i, (i + 1) % n_gy) for i in range(n_gy)]
    backward = [((i + 1) % n_gy, i) for i in range(n_gy)]
    current = fields
    for step in range(STEPS):
        got_x = lax.all_to_all(slots_x, "gx", 0, 0, tiled=True)
        slots_y, strip = call(
            strip_kernel, "strip", [own, got_x, prepared[-1]], [(n_gy, *block), (3, ROWS, 128)]
        )
        got_y = lax.all_to_all(slots_y, "gy", 0, 0, tiled=True)
        before = lax.ppermute(strip, "gy", forward)
        after = lax.ppermute(strip, "gy", backward)
        operands = [
            current,
            strip,
            before,
            after,
            got_y,
            *prepared,
            *tables,
        ]
        scratch = [pltpu.VMEM((ROWS * PADDED, 128), F32), pltpu.VMEM((ROWS * 8, 128), F32)]
        if step + 1 < STEPS:
            current, slots_x, own = call(
                middle_kernel,
                "middle",
                [*operands, pool_columns, pool_rows],
                [fields.shape, (n_gx, *block), (2, *block)],
                scratch,
            )
        else:
            (current,) = call(final_kernel, "final", operands, [fields.shape], scratch)
    return current


def solution(mesh):
    placed = (P(None, "gx", "gy"), P(), P(), P(), P(), P(), P(), P(), P(), P(), P(), P())
    return jax.shard_map(
        shards, mesh=mesh, in_specs=placed, out_specs=P(None, "gx", "gy"), check_vma=False
    )
```

time: 285 us -> 123 us (0.43); the launches traced: 279 us -> 122 us
  starting transfers between devices: 155 us -> 47 us
  matrix products: 61.8 us -> 0 us
  blocking collectives: 0 us -> 24 us
  Pallas kernels: 0 us -> 18 us
  waiting for transfers between devices: 33.6 us -> 20.3 us
  local copies, waits for them, and re-layouts: 22.8 us -> 12.3 us
  other arithmetic: 4.19 us -> 0 us
    ppermute x32 -> x4, starting transfers between devices: 155 us -> 11.1 us  [the longest x2 6.84 us: shards(): before = lax.ppermute(strip, 'gy', forward)]
    dot_general x38 -> x0, matrix products: 61.8 us -> none  [the longest x10 20.1 us: pointwise(): jnp.einsum('io,ixy->oxy', weights, inputs, precision=HIGHEST_PRECISION)]
    all_to_all x0 -> x3, starting transfers between devices: none -> 35.8 us  [the longest x1 18.2 us: shards(): got_x = lax.all_to_all(slots_x, 'gx', 0, 0, tiled=True)]
    ppermute x32 -> x4, waiting for transfers between devices: 33.6 us -> 9.42 us  [the longest x2 7.59 us: shards(): before = lax.ppermute(strip, 'gy', forward)]
    all_to_all x0 -> x1, blocking collectives: none -> 24 us  [shards(): got_x = lax.all_to_all(slots_x, 'gx', 0, 0, tiled=True)]
    reshape x90 -> x0, local copies, waits for them, and re-layouts: 18.7 us -> none  [the longest x6 12 us: pool_block(): current.reshape(channels, tile_rows // factor, factor, tile_cols // facto...]
    pallas_call x0 -> x6, Pallas kernels: none -> 18 us  [call(): pl.pallas_call(body, name=name, out_shape=[pltpu.VMEM(*(r if isinstance(r...]
    unnamed x26 -> x51, local copies, waits for them, and re-layouts: 0.08 us -> 12.3 us
  transfers between devices with their start and end apart: 32 -> 7, of which waited for: 8 -> 7; matrix products, arithmetic and copies ran while one was open for 5% -> 0% of each run, Pallas kernels for 0% -> 2%
where the time goes in v1:
time: 123 us; the launch traced here: 122 us
  starting transfers between devices  47 us (38%)
  blocking collectives  24 us (20%)
  waiting for transfers between devices  20.3 us (17%)
  Pallas kernels  18 us (15%)
  local copies, waits for them, and re-layouts  12.3 us (10%)
    all_to_all x1, blocking collectives, shards(): got_x = lax.all_to_all(slots_x, 'gx', 0, 0, tiled=True)  24 us
    all_to_all x1, starting transfers between devices, shards(): got_x = lax.all_to_all(slots_x, 'gx', 0, 0, tiled=True)  18.2 us
    pallas_call x6, Pallas kernels, call(): pl.pallas_call(body, name=name, out_shape=[pltpu.VMEM(*(r if isinstance(r...  18 us
    all_to_all x2, starting transfers between devices, shards(): got_y = lax.all_to_all(slots_y, 'gy', 0, 0, tiled=True)  17.6 us
    unnamed x51, local copies, waits for them, and re-layouts  12.3 us
    ppermute x2, waiting for transfers between devices, shards(): before = lax.ppermute(strip, 'gy', forward)  7.59 us
    all_to_all x2, waiting for transfers between devices, shards(): got_y = lax.all_to_all(slots_y, 'gy', 0, 0, tiled=True)  6.93 us
    ppermute x2, starting transfers between devices, shards(): before = lax.ppermute(strip, 'gy', forward)  6.84 us
  transfers between devices with their start and end apart: 7, of which 7 were waited for; matrix products, arithmetic and copies ran while one was open for 0% of the time, Pallas kernels for 2%

profile of v1, /device:TPU:1, one launch (start us, length us, event | category | flops | bytes accessed | tf_op | source)
XLA Modules:
  0.0 121.8 jit_solution(9534854740173126866)
XLA Ops:
  0.0 0.0 copy-start.1
  0.0 0.0 copy-start.2
  0.0 0.0 copy-start.7
  0.0 0.9 copy-done.7
  0.9 0.0 copy-start.9
  0.9 0.8 copy-done.9
  1.7 0.0 copy-start.11
  1.7 0.8 copy-done.11
  2.5 0.0 copy-start.10
  2.5 0.0 copy-start.16
  2.5 0.0 copy-start.17
  2.5 1.0 pool.1
  3.5 18.2 %all-to-all-start = ((f32[16,3,8,128]{3,2,1,0:T(8,128)}), f32[16,3,8,128]{3,2,1,0:T(8,128)S(1)}, u32[]{:S(2)}, u32[]{:S(2)}) async-start(f32[16,3,8,128]{3,2,1,0:T(8,128)} %get-tuple-element.21), calls=%async_computation | async-start | bytes 393216 | tf_op jit(solution)/shard_map/all_to_all | solution.py:519
  21.7 0.0 copy-start
  21.7 2.2 %copy-done = f32[2,8,8,64,64]{4,3,2,1,0:T(8,128)S(1)} copy-done((f32[2,8,8,64,64]{4,3,2,1,0:T(8,128)S(1)}, f32[2,8,8,64,64]{4,3,2,1,0:T(8,128)}, u32[]{:S(2)}) %copy-start) | copy-done | bytes 2097176
  23.9 0.0 copy-start.13
  23.9 0.8 copy-done.13
  24.6 0.0 copy-start.14
  24.6 0.8 copy-done.14
  25.4 0.0 copy-start.15
  25.4 0.8 copy-done.15
  26.2 0.0 copy-start.18
  26.2 0.7 copy-done.18
  26.9 0.0 copy-start.19
  26.9 0.7 copy-done.19
  27.5 0.0 copy-start.20
  27.5 0.7 copy-done.20
  28.2 0.7 copy-done.21
  28.9 0.7 copy-done.22
  29.5 0.7 copy-done.23
  30.2 0.7 copy-done.24
  30.8 0.0 copy-start.8
  30.8 0.0 copy-start.12
  30.9 2.9 %prepare.1 = (f32[1024,128]{1,0:T(8,128)S(1)}, bf16[64,48]{1,0:T(8,128)(2,1)S(1)}, bf16[136,192]{1,0:T(8,128)(2,1)S(1)}, f32[128,128]{1,0:T(8,128)S(1)}, bf16[8,...) custom-call(f32[12,64]{1,0:T(8,128)S(1)} %copy-done.18, f32[1,64]{1,0:T(1,128)S(1)} %bitcast.11, f32[2,64,64,64]{3,2,1,0:T(8,128)S(1)} %bitcast.8, ...), custom_call_target="tpu_custom_call" | custom-call | tf_op jit(solution)/shard_map/prepare/pallas_call | solution.py:450
  33.7 4.0 %all-to-all-done.got_ref = f32[16,3,8,128]{3,2,1,0:T(8,128)S(1)} async-done(((f32[16,3,8,128]{3,2,1,0:T(8,128)}), f32[16,3,8,128]{3,2,1,0:T(8,128)S(1)}, u32[]{:S(2)}, u32[]{:S(2)}) %all-to-all-start) | async-done | bytes 196640 | tf_op jit(solution)/shard_map/all_to_all | solution.py:519
  37.7 0.9 strip.2
  38.6 11.4 %all-to-all-start.1 = ((f32[32,3,8,128]{3,2,1,0:T(8,128)}), f32[32,3,8,128]{3,2,1,0:T(8,128)S(1)}, u32[]{:S(2)}, u32[]{:S(2)}) async-start(f32[32,3,8,128]{3,2,1,0:T(8,128)} %get-tuple-element.24), calls=%async_computation.1 | async-start | bytes 786432 | tf_op jit(solution)/shard_map/all_to_all | solution.py:523
  50.0 2.1 %collective-permute-start.1 = (f32[3,32,128]{2,1,0:T(8,128)S(1)}, f32[3,32,128]{2,1,0:T(8,128)S(1)}, u32[]{:S(2)}, u32[]{:S(2)}) collective-permute-start(f32[3,32,128]{2,1,0:T(8,128)S(1)} %get-tuple-element.23.refs_1_), channel_id=1, source_target_pairs={{1,0},{2,1},{3,2},{4,3},{5,4},{6,5},{7,6},{8,7},{9,8},{10,9},{11,1... | collective-permute-start | bytes 147464 | tf_op jit(solution)/shard_map/ppermute | solution.py:525
  52.2 3.4 %collective-permute-start = (f32[3,32,128]{2,1,0:T(8,128)S(1)}, f32[3,32,128]{2,1,0:T(8,128)S(1)}, u32[]{:S(2)}, u32[]{:S(2)}) collective-permute-start(f32[3,32,128]{2,1,0:T(8,128)S(1)} %get-tuple-element.23.refs_1_), channel_id=1, source_target_pairs={{0,1},{1,2},{2,3},{3,4},{4,5},{5,6},{6,7},{7,8},{8,9},{9,10},{10,1... | collective-permute-start | bytes 147464 | tf_op jit(solution)/shard_map/ppermute | solution.py:524
  55.6 0.9 collective-permute-done.1.refs_3_
  56.5 3.8 %collective-permute-done.refs_2_ = f32[3,32,128]{2,1,0:T(8,128)S(1)} collective-permute-done((f32[3,32,128]{2,1,0:T(8,128)S(1)}, f32[3,32,128]{2,1,0:T(8,128)S(1)}, u32[]{:S(2)}, u32[]{:S(2)}) %collective-permute-start) | collective-permute-done | bytes 49184 | tf_op jit(solution)/shard_map/ppermute | solution.py:524
  60.3 3.5 %all-to-all-done.1.refs_4_ = f32[32,3,8,128]{3,2,1,0:T(8,128)S(1)} async-done(((f32[32,3,8,128]{3,2,1,0:T(8,128)}), f32[32,3,8,128]{3,2,1,0:T(8,128)S(1)}, u32[]{:S(2)}, u32[]{:S(2)}) %all-to-all-start.1) | async-done | bytes 393248 | tf_op jit(solution)/shard_map/all_to_all | solution.py:523
  63.8 0.0 copy-done.1
  63.8 0.0 copy-done.2
  63.8 0.0 copy-done.10
  63.8 0.0 copy-done.16
  63.8 0.0 copy-done.17
  63.8 0.0 copy-done.3
  63.8 0.0 copy-done.4
  63.8 0.0 copy-done.5
  63.8 0.0 copy-done.6
  63.8 0.0 copy-done.8
  63.8 0.0 copy-done.12
  63.8 6.2 %middle.1 = (f32[3,32,128]{2,1,0:T(8,128)S(1)}, f32[16,3,8,128]{3,2,1,0:T(8,128)S(1)}, f32[2,3,8,128]{3,2,1,0:T(8,128)S(1)}) custom-call(f32[3,32,128]{2,1,0:T(8,128)S(1)} %copy-done.10, f32[3,32,128]{2,1,0:T(8,128)S(1)} %get-tuple-element.23.refs_1_, f32[3,32,128]{2,1,0:T(8,128)S(1)} %collective-permute-done.refs_2_, ...), custom_call_target="tpu_custom_call" | custom-call | tf_op jit(solution)/shard_map/middle/pallas_call | solution.py:450
  70.0 24.0 %all_to_all.20.got_ref = f32[16,3,8,128]{3,2,1,0:T(8,128)S(1)} all-to-all(f32[16,3,8,128]{3,2,1,0:T(8,128)S(1)} %get-tuple-element.32), channel_id=1, replica_groups=mesh['gx'=16,'gy'=32] {'gx'}, dimensions={0} | all-to-all | bytes 393216 | tf_op jit(solution)/shard_map/all_to_all | solution.py:519
  94.1 0.9 strip.3
  95.0 6.2 %all-to-all-start.3 = ((f32[32,3,8,128]{3,2,1,0:T(8,128)}), f32[32,3,8,128]{3,2,1,0:T(8,128)S(1)}, u32[]{:S(2)}, u32[]{:S(2)}) async-start(f32[32,3,8,128]{3,2,1,0:T(8,128)} %get-tuple-element.34), calls=%async_computation.3 | async-start | bytes 786432 | tf_op jit(solution)/shard_map/all_to_all | solution.py:523
  101.2 2.1 %collective-permute-start.3 = (f32[3,32,128]{2,1,0:T(8,128)S(1)}, f32[3,32,128]{2,1,0:T(8,128)S(1)}, u32[]{:S(2)}, u32[]{:S(2)}) collective-permute-start(f32[3,32,128]{2,1,0:T(8,128)S(1)} %get-tuple-element.33.refs_1_), channel_id=1, source_target_pairs={{1,0},{2,1},{3,2},{4,3},{5,4},{6,5},{7,6},{8,7},{9,8},{10,9},{11,1... | collective-permute-start | bytes 147464 | tf_op jit(solution)/shard_map/ppermute | solution.py:525
  103.3 3.4 %collective-permute-start.2 = (f32[3,32,128]{2,1,0:T(8,128)S(1)}, f32[3,32,128]{2,1,0:T(8,128)S(1)}, u32[]{:S(2)}, u32[]{:S(2)}) collective-permute-start(f32[3,32,128]{2,1,0:T(8,128)S(1)} %get-tuple-element.33.refs_1_), channel_id=1, source_target_pairs={{0,1},{1,2},{2,3},{3,4},{4,5},{5,6},{6,7},{7,8},{8,9},{9,10},{10,1... | collective-permute-start | bytes 147464 | tf_op jit(solution)/shard_map/ppermute | solution.py:524
  106.8 0.9 collective-permute-done.3.refs_3_
  107.7 3.8 %collective-permute-done.2.refs_2_ = f32[3,32,128]{2,1,0:T(8,128)S(1)} collective-permute-done((f32[3,32,128]{2,1,0:T(8,128)S(1)}, f32[3,32,128]{2,1,0:T(8,128)S(1)}, u32[]{:S(2)}, u32[]{:S(2)}) %collective-permute-start.2) | collective-permute-done | bytes 49184 | tf_op jit(solution)/shard_map/ppermute | solution.py:524
  111.5 3.5 %all-to-all-done.3.refs_4_ = f32[32,3,8,128]{3,2,1,0:T(8,128)S(1)} async-done(((f32[32,3,8,128]{3,2,1,0:T(8,128)}), f32[32,3,8,128]{3,2,1,0:T(8,128)S(1)}, u32[]{:S(2)}, u32[]{:S(2)}) %all-to-all-start.3) | async-done | bytes 393248 | tf_op jit(solution)/shard_map/all_to_all | solution.py:523
  114.9 6.2 %final.1 = f32[3,32,128]{2,1,0:T(8,128)S(1)} custom-call(f32[3,32,128]{2,1,0:T(8,128)S(1)} %get-tuple-element.30.refs_0_, f32[3,32,128]{2,1,0:T(8,128)S(1)} %get-tuple-element.33.refs_1_, f32[3,32,128]{2,1,0:T(8,128)S(1)} %collective-permute-done.2.refs_2_, f32[3,32,128]{2,1,0:T(8,128)S(1)} %collective-permute-done.3.refs_3_, ...), custom_call_target="tpu_custom_call" | custom-call | tf_op jit(solution)/shard_map/final/pallas_call | solution.py:450
  121.1 0.6 copy.19
  (8 shorter events, 0.0 us)
Async XLA Ops:
  0.0 63.8 %copy-start.1 = (bf16[512,256]{1,0:T(8,128)(2,1)S(1)}, bf16[512,256]{1,0:T(8,128)(2,1)}, u32[]{:S(2)}) copy-start(bf16[512,256]{1,0:T(8,128)(2,1)} %constant.35.refs_18_) | copy-start | bytes 786436
  0.0 63.8 %copy-start.2 = (bf16[512,256]{1,0:T(8,128)(2,1)S(1)}, bf16[512,256]{1,0:T(8,128)(2,1)}, u32[]{:S(2)}) copy-start(bf16[512,256]{1,0:T(8,128)(2,1)} %constant.32.refs_17_) | copy-start | bytes 786436
  0.0 0.9 copy-start.7
  0.9 0.8 copy-start.9
  1.7 0.8 copy-start.11
  2.5 61.3 %copy-start.10 = (f32[3,32,128]{2,1,0:T(8,128)S(1)}, f32[3,32,128]{2,1,0:T(8,128)}, u32[]{:S(2)}) copy-start(f32[3,32,128]{2,1,0:T(8,128)} %refs_0_.1) | copy-start | bytes 147460
  2.5 61.3 %copy-start.16 = (bf16[16,128]{1,0:T(8,128)(2,1)S(1)}, bf16[16,128]{1,0:T(8,128)(2,1)}, u32[]{:S(2)}) copy-start(bf16[16,128]{1,0:T(8,128)(2,1)} %constant.27.refs_14_) | copy-start | bytes 12292
  2.5 61.3 %copy-start.17 = (bf16[16,128]{1,0:T(8,128)(2,1)S(1)}, bf16[16,128]{1,0:T(8,128)(2,1)}, u32[]{:S(2)}) copy-start(bf16[16,128]{1,0:T(8,128)(2,1)} %constant.24.refs_13_) | copy-start | bytes 12292
  3.5 34.2 %all-to-all-start = ((f32[16,3,8,128]{3,2,1,0:T(8,128)}), f32[16,3,8,128]{3,2,1,0:T(8,128)S(1)}, u32[]{:S(2)}, u32[]{:S(2)}) async-start(f32[16,3,8,128]{3,2,1,0:T(8,128)} %get-tuple-element.21), calls=%async_computation | async-start | bytes 393216 | tf_op jit(solution)/shard_map/all_to_all | solution.py:519
  21.7 2.2 %copy-start = (f32[2,8,8,64,64]{4,3,2,1,0:T(8,128)S(1)}, f32[2,8,8,64,64]{4,3,2,1,0:T(8,128)}, u32[]{:S(2)}) copy-start(f32[2,8,8,64,64]{4,3,2,1,0:T(8,128)} %param.21) | copy-start | bytes 6291460
  23.9 0.8 copy-start.13
  24.6 0.8 copy-start.14
  25.4 0.8 copy-start.15
  26.2 0.7 copy-start.18
  26.9 0.7 copy-start.19
  27.5 0.7 copy-start.20
  28.2 0.7 copy-start.21
  28.9 0.7 copy-start.22
  29.5 0.7 copy-start.23
  30.2 0.7 copy-start.24
  30.8 33.0 %copy-start.3 = (bf16[256,512]{1,0:T(8,128)(2,1)S(1)}, bf16[256,512]{1,0:T(8,128)(2,1)}, u32[]{:S(2)}) copy-start(bf16[256,512]{1,0:T(8,128)(2,1)} %constant.23.refs_12_) | copy-start | bytes 786436
  30.8 33.0 %copy-start.4 = (bf16[256,512]{1,0:T(8,128)(2,1)S(1)}, bf16[256,512]{1,0:T(8,128)(2,1)}, u32[]{:S(2)}) copy-start(bf16[256,512]{1,0:T(8,128)(2,1)} %constant.20.refs_11_) | copy-start | bytes 786436
  30.8 33.0 %copy-start.5 = (bf16[128,512]{1,0:T(8,128)(2,1)S(1)}, bf16[128,512]{1,0:T(8,128)(2,1)}, u32[]{:S(2)}) copy-start(bf16[128,512]{1,0:T(8,128)(2,1)} %constant.31.refs_16_) | copy-start | bytes 393220
  30.8 33.0 %copy-start.6 = (bf16[128,512]{1,0:T(8,128)(2,1)S(1)}, bf16[128,512]{1,0:T(8,128)(2,1)}, u32[]{:S(2)}) copy-start(bf16[128,512]{1,0:T(8,128)(2,1)} %constant.28.refs_15_) | copy-start | bytes 393220
  30.8 33.0 %copy-start.8 = (bf16[256,128]{1,0:T(8,128)(2,1)S(1)}, bf16[256,128]{1,0:T(8,128)(2,1)}, u32[]{:S(2)}) copy-start(bf16[256,128]{1,0:T(8,128)(2,1)} %constant.18.columns_ref.refs_19_) | copy-start | bytes 196612
  30.8 33.0 %copy-start.12 = (bf16[96,192]{1,0:T(8,128)(2,1)S(1)}, bf16[96,192]{1,0:T(8,128)(2,1)}, u32[]{:S(2)}) copy-start(bf16[96,192]{1,0:T(8,128)(2,1)} %constant.19.rows_ref.refs_20_) | copy-start | bytes 110596
  38.6 25.2 %all-to-all-start.1 = ((f32[32,3,8,128]{3,2,1,0:T(8,128)}), f32[32,3,8,128]{3,2,1,0:T(8,128)S(1)}, u32[]{:S(2)}, u32[]{:S(2)}) async-start(f32[32,3,8,128]{3,2,1,0:T(8,128)} %get-tuple-element.24), calls=%async_computation.1 | async-start | bytes 786432 | tf_op jit(solution)/shard_map/all_to_all | solution.py:523
  50.0 6.5 %collective-permute-start.1 = (f32[3,32,128]{2,1,0:T(8,128)S(1)}, f32[3,32,128]{2,1,0:T(8,128)S(1)}, u32[]{:S(2)}, u32[]{:S(2)}) collective-permute-start(f32[3,32,128]{2,1,0:T(8,128)S(1)} %get-tuple-element.23.refs_1_), channel_id=1, source_target_pairs={{1,0},{2,1},{3,2},{4,3},{5,4},{6,5},{7,6},{8,7},{9,8},{10,9},{11,1... | collective-permute-start | bytes 147464 | tf_op jit(solution)/shard_map/ppermute | solution.py:525
  52.2 8.1 %collective-permute-start = (f32[3,32,128]{2,1,0:T(8,128)S(1)}, f32[3,32,128]{2,1,0:T(8,128)S(1)}, u32[]{:S(2)}, u32[]{:S(2)}) collective-permute-start(f32[3,32,128]{2,1,0:T(8,128)S(1)} %get-tuple-element.23.refs_1_), channel_id=1, source_target_pairs={{0,1},{1,2},{2,3},{3,4},{4,5},{5,6},{6,7},{7,8},{8,9},{9,10},{10,1... | collective-permute-start | bytes 147464 | tf_op jit(solution)/shard_map/ppermute | solution.py:524
  95.0 20.0 %all-to-all-start.3 = ((f32[32,3,8,128]{3,2,1,0:T(8,128)}), f32[32,3,8,128]{3,2,1,0:T(8,128)S(1)}, u32[]{:S(2)}, u32[]{:S(2)}) async-start(f32[32,3,8,128]{3,2,1,0:T(8,128)} %get-tuple-element.34), calls=%async_computation.3 | async-start | bytes 786432 | tf_op jit(solution)/shard_map/all_to_all | solution.py:523
  101.2 6.5 %collective-permute-start.3 = (f32[3,32,128]{2,1,0:T(8,128)S(1)}, f32[3,32,128]{2,1,0:T(8,128)S(1)}, u32[]{:S(2)}, u32[]{:S(2)}) collective-permute-start(f32[3,32,128]{2,1,0:T(8,128)S(1)} %get-tuple-element.33.refs_1_), channel_id=1, source_target_pairs={{1,0},{2,1},{3,2},{4,3},{5,4},{6,5},{7,6},{8,7},{9,8},{10,9},{11,1... | collective-permute-start | bytes 147464 | tf_op jit(solution)/shard_map/ppermute | solution.py:525
  103.3 8.1 %collective-permute-start.2 = (f32[3,32,128]{2,1,0:T(8,128)S(1)}, f32[3,32,128]{2,1,0:T(8,128)S(1)}, u32[]{:S(2)}, u32[]{:S(2)}) collective-permute-start(f32[3,32,128]{2,1,0:T(8,128)S(1)} %get-tuple-element.33.refs_1_), channel_id=1, source_target_pairs={{0,1},{1,2},{2,3},{3,4},{4,5},{5,6},{6,7},{7,8},{8,9},{9,10},{10,1... | collective-permute-start | bytes 147464 | tf_op jit(solution)/shard_map/ppermute | solution.py:524

commit v2 on v1

--- a/solution.py
+++ b/solution.py
@@ -23,26 +23,31 @@
 
 
 def pool_tables():
-    columns = np.zeros((COLS, 128), np.float32)
-    for cell in range(COLS):
-        columns[cell, cell // 2] = 0.5
-        columns[cell, LANE_L2 + cell // 4] = 0.25
-        columns[cell, LANE_L3 + cell // 8] = 0.125
-        columns[cell, LANE_L3_COPY + cell // 8] = 0.125
-    rows = np.zeros((96, 96), np.float32)
-    for channel in range(3):
-        for sub in range(8):
-            for kind, (factor, row) in enumerate(
-                [(2, sub), (2, sub + 8), (4, (sub + 4) % 8), (8, (sub + 2) % 4)]
-            ):
-                for inner in range(factor):
-                    rows[channel * 32 + kind * 8 + sub, channel * 32 + row * factor + inner] = (
-                        1.0 / factor
-                    )
-    return (
-        np.concatenate([columns, columns], axis=0),
-        np.concatenate([rows, rows], axis=1),
-    )
+    cell = lax.broadcasted_iota(jnp.int32, (COLS, 128), 0)
+    lane = lax.broadcasted_iota(jnp.int32, (COLS, 128), 1)
+    eighth = cell >> 3
+    columns = jnp.where(
+        lane < LANE_L3,
+        jnp.where(cell >> 1 == lane, 0.5, 0.0),
+        jnp.where(
+            (lane >= LANE_L2) & (lane < LANE_L3_COPY),
+            jnp.where(cell >> 2 == lane - LANE_L2, 0.25, 0.0),
+            jnp.where(
+                (eighth == lane - LANE_L3) | (eighth == lane - LANE_L3_COPY), 0.125, 0.0
+            ),
+        ),
+    ).astype(BF16)
+    out = lax.broadcasted_iota(jnp.int32, (96, 96), 0)
+    cell = lax.broadcasted_iota(jnp.int32, (96, 96), 1)
+    kind = (out >> 3) & 3
+    sub = out & 7
+    row = cell & 31
+    fine = jnp.where(row >> 1 == sub + 8 * kind, 0.5, 0.0)
+    middle = jnp.where(row >> 2 == ((sub + 4) & 7), 0.25, 0.0)
+    coarse = jnp.where(row >> 3 == ((sub + 2) & 3), 0.125, 0.0)
+    rows = jnp.where(kind < 2, fine, jnp.where(kind == 2, middle, coarse))
+    rows = jnp.where(out >> 5 == cell >> 5, rows, 0.0).astype(BF16)
+    return jnp.concatenate([columns, columns], axis=0), jnp.concatenate([rows, rows], axis=1)
 
 
 def fourier_tables():
@@ -71,8 +76,8 @@
     inverse_cols = np.zeros((4, 8, 16, 2, COLS))
     for pair in range(4):
         for half in range(2):
-            inverse_cols[pair, 2 * pair + half, :8, half] = weight * np.cos(phi)
-            inverse_cols[pair, 2 * pair + half, 8:, half] = -weight * np.sin(phi)
+            inverse_cols[pair, 2 * pair + half, :8, half] = 0.5 * weight * np.cos(phi)
+            inverse_cols[pair, 2 * pair + half, 8:, half] = -0.5 * weight * np.sin(phi)
     return (
         forward_rows,
         forward_cols,
@@ -105,13 +110,13 @@
     )
 
 
-def gelu(value):
-    inner = value * (GELU_SCALE + (GELU_SCALE * 0.044715) * (value * value))
-    half = 0.5 * value
+def gelu_of_double(half):
+    inner = half * (2.0 * GELU_SCALE + (8.0 * GELU_SCALE * 0.044715) * (half * half))
     return half + half * jnp.tanh(inner)
 
 
-def pooled_blocks(flat, pool_columns, pool_rows):
+def pooled_blocks(flat):
+    pool_columns, pool_rows = pool_tables()
     high, low = split(flat)
     across = matmul(jnp.concatenate([high, low], axis=1), pool_columns)
     high, low = split(across)
@@ -137,9 +142,9 @@
             slots_ref[slot, channel] = jnp.where(ahead, lower[channel], upper[channel])
 
 
-def pool_kernel(current_ref, columns_ref, rows_ref, slots_ref, own_ref):
+def pool_kernel(current_ref, slots_ref, own_ref):
     flat = current_ref[...].reshape(96, 128)
-    upper, lower = pooled_blocks(flat, columns_ref[...], rows_ref[...])
+    upper, lower = pooled_blocks(flat)
     for channel in range(3):
         own_ref[0, channel] = upper[channel]
         own_ref[1, channel] = lower[channel]
@@ -235,16 +240,22 @@
     skip = jnp.dot(lift, bypass_ref[...], precision=highest)
     row = lax.broadcasted_iota(jnp.int32, skip.shape, 0)
     skip = skip + jnp.where(row == FEATURES, layer_bias_ref[...], 0.0)
-    square = jnp.concatenate([skip, jnp.zeros((128 - PADDED, 64), F32)], axis=0)
+    square = jnp.concatenate([0.5 * skip, jnp.zeros((128 - PADDED, 64), F32)], axis=0)
     square = jnp.concatenate([square, jnp.zeros((128, 64), F32)], axis=1)
     skip_ref[...] = stacked_left(jnp.transpose(square)[:64, :PADDED])
 
     project = jnp.concatenate([project_ref[...], jnp.zeros((5, 64), F32)], axis=0)
     wide = jnp.concatenate([mlp_in_ref[...], jnp.zeros((64, 128), F32)], axis=0)
-    inner = jnp.concatenate([jnp.transpose(wide)[:, :64], project], axis=0)
+    inner = jnp.concatenate([0.5 * jnp.transpose(wide)[:, :64], project], axis=0)
     inner_ref[...] = stacked_left(inner)
-    inner_bias_ref[...] = jnp.transpose(jnp.broadcast_to(mlp_in_bias_ref[...], (128, 128)))
-    last_ref[...] = stacked_left(jnp.dot(project, mlp_out_ref[...], precision=highest))
+    inner_bias_ref[...] = jnp.transpose(
+        jnp.broadcast_to(0.5 * mlp_in_bias_ref[...], (128, 128))
+    )
+    last = jnp.dot(project, mlp_out_ref[...], precision=highest)
+    for channel in range(3):
+        last_ref[channel] = jnp.transpose(
+            jnp.broadcast_to(last[channel : channel + 1], (128, 128))
+        )
     sub = lax.broadcasted_iota(jnp.int32, (8, 3), 0)
     lane = lax.broadcasted_iota(jnp.int32, (8, 3), 1)
     constant = jnp.sum(project * mlp_out_bias_ref[...], axis=1, keepdims=True) + jnp.sum(
@@ -253,12 +264,15 @@
     offset_ref[...] = jnp.broadcast_to(constant, (8, 128))
 
 
-def contexts(strip_ref, before_ref, after_ref, got_ref, position, channel, block):
+def contexts(strip_ref, twin_ref, other_ref, got_ref, position, channel, block):
     lane = lax.broadcasted_iota(jnp.int32, (8, 128), 1)
     rows = slice(block * 8, block * 8 + 8)
     here = strip_ref[channel, rows]
-    before = before_ref[channel, rows]
-    after = after_ref[channel, rows]
+    twin = twin_ref[channel, rows]
+    other = other_ref[channel, rows]
+    even = position % 2 == 0
+    before = jnp.where(even, other, twin)
+    after = jnp.where(even, twin, other)
     far = {
         offset: got_ref[lax.rem(position + offset + 32, 32), channel]
         for offset in (-4, -3, -2, 2, 3, 4)
@@ -304,8 +318,8 @@
 def tile_step(
     current_ref,
     strip_ref,
-    before_ref,
-    after_ref,
+    twin_ref,
+    other_ref,
     got_ref,
     mixing_ref,
     skip_ref,
@@ -323,13 +337,14 @@
     back_cols_low_ref,
     features_ref,
     results_ref,
+    partial_ref,
 ):
     position = lax.axis_index("gy")
     for channel in range(3):
         for block in range(4):
             pieces = (
                 current_ref[channel, block * 8 : block * 8 + 8],
-                *contexts(strip_ref, before_ref, after_ref, got_ref, position, channel, block),
+                *contexts(strip_ref, twin_ref, other_ref, got_ref, position, channel, block),
             )
             for level in range(4):
                 features_ref[
@@ -385,7 +400,6 @@
     skip = skip_ref[...]
     inner_left = inner_ref[...]
     inner_bias = jnp.concatenate([inner_bias_ref[...], inner_bias_ref[...]], axis=1)
-    last_left = last_ref[...]
     offset = jnp.concatenate([offset_ref[...], offset_ref[...]], axis=1)
     for pair in range(4):
         table = (
@@ -402,37 +416,46 @@
                 ],
                 axis=1,
             )
-            mixed = gelu(
+            mixed = gelu_of_double(
                 spectral[block * 64 : block * 64 + 64] + matmul(skip, stacked_right(cells))
             )
             wide = matmul(inner_left, stacked_right(mixed))
-            hidden = gelu(wide[:128] + inner_bias)
-            total = wide[128:136] + offset + matmul(last_left, stacked_right(hidden))
-            results_ref[row * 8 : row * 8 + 8, :] = total[:, :128]
-            results_ref[(row + 1) * 8 : (row + 2) * 8, :] = total[:, 128:]
-    return [
-        current_ref[channel]
-        + results_ref[pl.ds(channel, ROWS, stride=8), :]
-        for channel in range(3)
-    ]
+            hidden = gelu_of_double(wide[:128] + inner_bias)
+            total = wide[128:136] + offset
+            for half in range(2):
+                lanes = slice(half * 128, half * 128 + 128)
+                results_ref[(row + half) * 8 : (row + half) * 8 + 8, :] = total[:, lanes]
+                for channel in range(3):
+                    partial = None
+                    for start in range(0, 128, 8):
+                        term = hidden[start : start + 8, lanes] * last_ref[
+                            channel, start : start + 8
+                        ]
+                        partial = term if partial is None else partial + term
+                    partial_ref[channel, (row + half) * 8 : (row + half) * 8 + 8] = partial
+
+    def sublane_sum(channel):
+        total = results_ref[pl.ds(channel, ROWS, stride=8), :]
+        for sub in range(8):
+            total = total + partial_ref[channel, pl.ds(sub, ROWS, stride=8), :]
+        return total
+
+    return [current_ref[channel] + sublane_sum(channel) for channel in range(3)]
 
 
 def final_kernel(*refs):
-    inputs, next_ref, scratch = refs[:19], refs[19], refs[20:]
-    updated = tile_step(*inputs, *scratch)
+    next_ref = refs[19]
+    updated = tile_step(*refs[:19], *refs[20:])
     for channel in range(3):
         next_ref[channel] = updated[channel]
 
 
 def middle_kernel(*refs):
-    inputs, columns_ref, rows_ref = refs[:19], refs[19], refs[20]
-    next_ref, slots_ref, own_ref = refs[21:24]
-    updated = tile_step(*inputs, *refs[24:])
+    next_ref, slots_ref, own_ref = refs[19:22]
+    updated = tile_step(*refs[:19], *refs[22:])
     for channel in range(3):
         next_ref[channel] = updated[channel]
-    upper, lower = pooled_blocks(
-        jnp.concatenate(updated, axis=0), columns_ref[...], rows_ref[...]
-    )
+    upper, lower = pooled_blocks(jnp.concatenate(updated, axis=0))
     for channel in range(3):
         own_ref[0, channel] = upper[channel]
         own_ref[1, channel] = lower[channel]
@@ -479,12 +502,11 @@
 ):
     n_gx = lax.axis_size("gx")
     n_gy = lax.axis_size("gy")
-    pool_columns, pool_rows = (jnp.asarray(table).astype(BF16) for table in pool_tables())
     tables = [half for table in fourier_tables() for half in halves_of_table(table)]
 
     block = (3, 8, 128)
     slots_x, own = call(
-        pool_kernel, "pool", [fields, pool_columns, pool_rows], [(n_gx, *block), (2, *block)]
+        pool_kernel, "pool", [fields], [(n_gx, *block), (2, *block)]
     )
     prepared = call(
         prepare_kernel,
@@ -507,13 +529,13 @@
             ((64, 3 * PADDED), BF16),
             ((136, 192), BF16),
             (128, 128),
-            ((8, 384), BF16),
+            (3, 128, 128),
             (8, 128),
         ],
     )
 
-    forward = [(i, (i + 1) % n_gy) for i in range(n_gy)]
-    backward = [((i + 1) % n_gy, i) for i in range(n_gy)]
+    twins = [(i, i ^ 1) for i in range(n_gy)]
+    others = [(i, (i + 1 if i % 2 else i - 1) % n_gy) for i in range(n_gy)]
     current = fields
     for step in range(STEPS):
         got_x = lax.all_to_all(slots_x, "gx", 0, 0, tiled=True)
@@ -521,23 +543,23 @@
             strip_kernel, "strip", [own, got_x, prepared[-1]], [(n_gy, *block), (3, ROWS, 128)]
         )
         got_y = lax.all_to_all(slots_y, "gy", 0, 0, tiled=True)
-        before = lax.ppermute(strip, "gy", forward)
-        after = lax.ppermute(strip, "gy", backward)
+        twin = lax.ppermute(strip, "gy", twins)
+        other = lax.ppermute(strip, "gy", others)
         operands = [
             current,
             strip,
-            before,
-            after,
+            twin,
+            other,
             got_y,
             *prepared,
             *tables,
         ]
-        scratch = [pltpu.VMEM((ROWS * PADDED, 128), F32), pltpu.VMEM((ROWS * 8, 128), F32)]
+        scratch = [pltpu.VMEM((ROWS * PADDED, 128), F32), pltpu.VMEM((ROWS * 8, 128), F32), pltpu.VMEM((3, ROWS * 8, 128), F32)]
         if step + 1 < STEPS:
             current, slots_x, own = call(
                 middle_kernel,
                 "middle",
-                [*operands, pool_columns, pool_rows],
+                operands,
                 [fields.shape, (n_gx, *block), (2, *block)],
                 scratch,
             )

time: 123 us -> 117 us (0.951)
  starting transfers between devices: 47 us -> 57.5 us
  waiting for transfers between devices: 20.3 us -> 12.3 us
  Pallas kernels: 18 us -> 13.9 us
  blocking collectives: 24 us -> 21.5 us
  local copies, waits for them, and re-layouts: 12.3 us -> 10.6 us
    ppermute x4, starting transfers between devices: 11.1 us -> 19.1 us  [the longest x2 12 us: shards(): twin = lax.ppermute(strip, 'gy', twins)]
    ppermute x4, waiting for transfers between devices: 9.42 us -> 1.7 us  [the longest x2 1.7 us: shards(): twin = lax.ppermute(strip, 'gy', twins)]
    pallas_call x6, Pallas kernels: 18 us -> 13.9 us  [call(): pl.pallas_call(body, name=name, out_shape=[pltpu.VMEM(*(r if isinstance(r...]
    all_to_all x1, blocking collectives: 24 us -> 21.5 us  [shards(): got_x = lax.all_to_all(slots_x, 'gx', 0, 0, tiled=True)]
    all_to_all x2, starting transfers between devices: 17.6 us -> 20.1 us  [shards(): got_y = lax.all_to_all(slots_y, 'gy', 0, 0, tiled=True)]
    unnamed x51 -> x43, local copies, waits for them, and re-layouts: 12.3 us -> 10.6 us
  transfers between devices with their start and end apart: 7 -> 7, of which waited for: 7 -> 5; matrix products, arithmetic and copies ran while one was open for 0% -> 0% of each run, Pallas kernels for 2% -> 2%
where the time goes in v2:
time: 117 us; the launch traced here: 116 us
  starting transfers between devices  57.5 us (49%)
  blocking collectives  21.5 us (18%)
  Pallas kernels  13.9 us (12%)
  waiting for transfers between devices  12.3 us (11%)
  local copies, waits for them, and re-layouts  10.6 us (9%)
    all_to_all x1, blocking collectives, shards(): got_x = lax.all_to_all(slots_x, 'gx', 0, 0, tiled=True)  21.5 us
    all_to_all x2, starting transfers between devices, shards(): got_y = lax.all_to_all(slots_y, 'gy', 0, 0, tiled=True)  20.1 us
    all_to_all x1, starting transfers between devices, shards(): got_x = lax.all_to_all(slots_x, 'gx', 0, 0, tiled=True)  18.2 us
    pallas_call x6, Pallas kernels, call(): pl.pallas_call(body, name=name, out_shape=[pltpu.VMEM(*(r if isinstance(r...  13.9 us
    ppermute x2, starting transfers between devices, shards(): twin = lax.ppermute(strip, 'gy', twins)  12 us
    unnamed x43, local copies, waits for them, and re-layouts  10.6 us
    ppermute x2, starting transfers between devices, shards(): other = lax.ppermute(strip, 'gy', others)  7.08 us
    all_to_all x2, waiting for transfers between devices, shards(): got_y = lax.all_to_all(slots_y, 'gy', 0, 0, tiled=True)  6.65 us
  transfers between devices with their start and end apart: 7, of which 5 were waited for; matrix products, arithmetic and copies ran while one was open for 0% of the time, Pallas kernels for 2%

profile of v2, /device:TPU:1, one launch (start us, length us, event | category | flops | bytes accessed | tf_op | source)
XLA Modules:
  0.0 115.9 jit_solution(7838148577896098412)
XLA Ops:
  0.0 0.0 copy-start.1
  0.0 0.0 copy-start.5
  0.0 0.0 copy-start.7
  0.0 0.8 copy-done.7
  0.9 0.0 copy-start.8
  0.9 0.0 copy-start.12
  0.9 0.0 copy-start.13
  0.9 1.0 pool.1
  1.9 18.2 %all-to-all-start = ((f32[16,3,8,128]{3,2,1,0:T(8,128)}), f32[16,3,8,128]{3,2,1,0:T(8,128)S(1)}, u32[]{:S(2)}, u32[]{:S(2)}) async-start(f32[16,3,8,128]{3,2,1,0:T(8,128)} %get-tuple-element.21), calls=%async_computation | async-start | bytes 393216 | tf_op jit(solution)/shard_map/all_to_all | solution.py:541
  20.1 0.0 copy-start
  20.1 2.2 %copy-done = f32[2,8,8,64,64]{4,3,2,1,0:T(8,128)S(1)} copy-done((f32[2,8,8,64,64]{4,3,2,1,0:T(8,128)S(1)}, f32[2,8,8,64,64]{4,3,2,1,0:T(8,128)}, u32[]{:S(2)}) %copy-start) | copy-done | bytes 2097176
  22.3 0.0 copy-start.9
  22.3 0.8 copy-done.9
  23.0 0.0 copy-start.10
  23.0 0.8 copy-done.10
  23.8 0.0 copy-start.11
  23.8 0.8 copy-done.11
  24.5 0.0 copy-start.14
  24.5 0.7 copy-done.14
  25.2 0.0 copy-start.15
  25.2 0.7 copy-done.15
  25.9 0.0 copy-start.16
  25.9 0.7 copy-done.16
  26.6 0.0 copy-start.17
  26.6 0.7 copy-done.17
  27.2 0.0 copy-start.18
  27.2 0.7 copy-done.18
  27.9 0.0 copy-start.19
  27.9 0.7 copy-done.19
  28.5 0.0 copy-start.20
  28.5 0.7 copy-done.20
  29.2 0.0 copy-start.2
  29.2 0.0 copy-start.3
  29.2 0.0 copy-start.4
  29.2 0.0 copy-start.6
  29.2 2.9 %prepare.1 = (f32[1024,128]{1,0:T(8,128)S(1)}, bf16[64,48]{1,0:T(8,128)(2,1)S(1)}, bf16[136,192]{1,0:T(8,128)(2,1)S(1)}, f32[128,128]{1,0:T(8,128)S(1)}, f32[3,1...) custom-call(f32[12,64]{1,0:T(8,128)S(1)} %copy-done.14, f32[1,64]{1,0:T(1,128)S(1)} %bitcast.11, f32[2,64,64,64]{3,2,1,0:T(8,128)S(1)} %bitcast.8, ...), custom_call_target="tpu_custom_call" | custom-call | tf_op jit(solution)/shard_map/prepare/pallas_call | solution.py:473
  32.1 4.0 %all-to-all-done.got_ref = f32[16,3,8,128]{3,2,1,0:T(8,128)S(1)} async-done(((f32[16,3,8,128]{3,2,1,0:T(8,128)}), f32[16,3,8,128]{3,2,1,0:T(8,128)S(1)}, u32[]{:S(2)}, u32[]{:S(2)}) %all-to-all-start) | async-done | bytes 196640 | tf_op jit(solution)/shard_map/all_to_all | solution.py:541
  36.1 0.9 strip.2
  36.9 11.4 %all-to-all-start.1 = ((f32[32,3,8,128]{3,2,1,0:T(8,128)}), f32[32,3,8,128]{3,2,1,0:T(8,128)S(1)}, u32[]{:S(2)}, u32[]{:S(2)}) async-start(f32[32,3,8,128]{3,2,1,0:T(8,128)} %get-tuple-element.24), calls=%async_computation.1 | async-start | bytes 786432 | tf_op jit(solution)/shard_map/all_to_all | solution.py:545
  48.4 3.5 %collective-permute-start.1 = (f32[3,32,128]{2,1,0:T(8,128)S(1)}, f32[3,32,128]{2,1,0:T(8,128)S(1)}, u32[]{:S(2)}, u32[]{:S(2)}) collective-permute-start(f32[3,32,128]{2,1,0:T(8,128)S(1)} %get-tuple-element.23.refs_1_), channel_id=1, source_target_pairs={{0,31},{1,2},{2,1},{3,4},{4,3},{5,6},{6,5},{7,8},{8,7},{9,10},{10,... | collective-permute-start | bytes 147464 | tf_op jit(solution)/shard_map/ppermute | solution.py:547
  51.9 6.0 %collective-permute-start = (f32[3,32,128]{2,1,0:T(8,128)S(1)}, f32[3,32,128]{2,1,0:T(8,128)S(1)}, u32[]{:S(2)}, u32[]{:S(2)}) collective-permute-start(f32[3,32,128]{2,1,0:T(8,128)S(1)} %get-tuple-element.23.refs_1_), channel_id=1, source_target_pairs={{0,1},{1,0},{2,3},{3,2},{4,5},{5,4},{6,7},{7,6},{8,9},{9,8},{10,11... | collective-permute-start | bytes 147464 | tf_op jit(solution)/shard_map/ppermute | solution.py:546
  57.9 0.0 collective-permute-done.1.refs_3_
  57.9 0.8 collective-permute-done.refs_2_
  58.8 3.3 %all-to-all-done.1.refs_4_ = f32[32,3,8,128]{3,2,1,0:T(8,128)S(1)} async-done(((f32[32,3,8,128]{3,2,1,0:T(8,128)}), f32[32,3,8,128]{3,2,1,0:T(8,128)S(1)}, u32[]{:S(2)}, u32[]{:S(2)}) %all-to-all-start.1) | async-done | bytes 393248 | tf_op jit(solution)/shard_map/all_to_all | solution.py:545
  62.1 0.0 copy-done.1
  62.1 0.0 copy-done.5
  62.1 0.0 copy-done.8
  62.1 0.0 copy-done.12
  62.1 0.0 copy-done.13
  62.2 0.0 copy-done.2
  62.2 0.0 copy-done.3
  62.2 0.0 copy-done.4
  62.2 0.0 copy-done.6
  62.2 4.3 %middle.1 = (f32[3,32,128]{2,1,0:T(8,128)S(1)}, f32[16,3,8,128]{3,2,1,0:T(8,128)S(1)}, f32[2,3,8,128]{3,2,1,0:T(8,128)S(1)}) custom-call(f32[3,32,128]{2,1,0:T(8,128)S(1)} %copy-done.8, f32[3,32,128]{2,1,0:T(8,128)S(1)} %get-tuple-element.23.refs_1_, f32[3,32,128]{2,1,0:T(8,128)S(1)} %collective-permute-done.refs_2_, ...), custom_call_target="tpu_custom_call" | custom-call | tf_op jit(solution)/shard_map/middle/pallas_call | solution.py:473
  66.5 21.5 %all_to_all.20.got_ref = f32[16,3,8,128]{3,2,1,0:T(8,128)S(1)} all-to-all(f32[16,3,8,128]{3,2,1,0:T(8,128)S(1)} %get-tuple-element.32), channel_id=1, replica_groups=mesh['gx'=16,'gy'=32] {'gx'}, dimensions={0} | all-to-all | bytes 393216 | tf_op jit(solution)/shard_map/all_to_all | solution.py:541
  88.0 0.9 strip.3
  88.8 8.7 %all-to-all-start.3 = ((f32[32,3,8,128]{3,2,1,0:T(8,128)}), f32[32,3,8,128]{3,2,1,0:T(8,128)S(1)}, u32[]{:S(2)}, u32[]{:S(2)}) async-start(f32[32,3,8,128]{3,2,1,0:T(8,128)} %get-tuple-element.34), calls=%async_computation.3 | async-start | bytes 786432 | tf_op jit(solution)/shard_map/all_to_all | solution.py:545
  97.6 3.5 %collective-permute-start.3 = (f32[3,32,128]{2,1,0:T(8,128)S(1)}, f32[3,32,128]{2,1,0:T(8,128)S(1)}, u32[]{:S(2)}, u32[]{:S(2)}) collective-permute-start(f32[3,32,128]{2,1,0:T(8,128)S(1)} %get-tuple-element.33.refs_1_), channel_id=1, source_target_pairs={{0,31},{1,2},{2,1},{3,4},{4,3},{5,6},{6,5},{7,8},{8,7},{9,10},{10,... | collective-permute-start | bytes 147464 | tf_op jit(solution)/shard_map/ppermute | solution.py:547
  101.1 6.0 %collective-permute-start.2 = (f32[3,32,128]{2,1,0:T(8,128)S(1)}, f32[3,32,128]{2,1,0:T(8,128)S(1)}, u32[]{:S(2)}, u32[]{:S(2)}) collective-permute-start(f32[3,32,128]{2,1,0:T(8,128)S(1)} %get-tuple-element.33.refs_1_), channel_id=1, source_target_pairs={{0,1},{1,0},{2,3},{3,2},{4,5},{5,4},{6,7},{7,6},{8,9},{9,8},{10,11... | collective-permute-start | bytes 147464 | tf_op jit(solution)/shard_map/ppermute | solution.py:546
  107.1 0.0 collective-permute-done.3.refs_3_
  107.1 0.8 collective-permute-done.2.refs_2_
  108.0 3.3 %all-to-all-done.3.refs_4_ = f32[32,3,8,128]{3,2,1,0:T(8,128)S(1)} async-done(((f32[32,3,8,128]{3,2,1,0:T(8,128)}), f32[32,3,8,128]{3,2,1,0:T(8,128)S(1)}, u32[]{:S(2)}, u32[]{:S(2)}) %all-to-all-start.3) | async-done | bytes 393248 | tf_op jit(solution)/shard_map/all_to_all | solution.py:545
  111.3 4.0 %final.1 = f32[3,32,128]{2,1,0:T(8,128)S(1)} custom-call(f32[3,32,128]{2,1,0:T(8,128)S(1)} %get-tuple-element.30.refs_0_, f32[3,32,128]{2,1,0:T(8,128)S(1)} %get-tuple-element.33.refs_1_, f32[3,32,128]{2,1,0:T(8,128)S(1)} %collective-permute-done.2.refs_2_, f32[3,32,128]{2,1,0:T(8,128)S(1)} %collective-permute-done.3.refs_3_, ...), custom_call_target="tpu_custom_call" | custom-call | tf_op jit(solution)/shard_map/final/pallas_call | solution.py:473
  115.3 0.6 copy.17
Async XLA Ops:
  0.0 62.1 %copy-start.1 = (bf16[512,256]{1,0:T(8,128)(2,1)S(1)}, bf16[512,256]{1,0:T(8,128)(2,1)}, u32[]{:S(2)}) copy-start(bf16[512,256]{1,0:T(8,128)(2,1)} %constant.27.refs_18_) | copy-start | bytes 786436
  0.0 62.1 %copy-start.5 = (bf16[128,512]{1,0:T(8,128)(2,1)S(1)}, bf16[128,512]{1,0:T(8,128)(2,1)}, u32[]{:S(2)}) copy-start(bf16[128,512]{1,0:T(8,128)(2,1)} %constant.23.refs_16_) | copy-start | bytes 393220
  0.0 0.8 copy-start.7
  0.9 61.3 %copy-start.8 = (f32[3,32,128]{2,1,0:T(8,128)S(1)}, f32[3,32,128]{2,1,0:T(8,128)}, u32[]{:S(2)}) copy-start(f32[3,32,128]{2,1,0:T(8,128)} %refs_0_.1) | copy-start | bytes 147460
  0.9 61.3 %copy-start.12 = (bf16[16,128]{1,0:T(8,128)(2,1)S(1)}, bf16[16,128]{1,0:T(8,128)(2,1)}, u32[]{:S(2)}) copy-start(bf16[16,128]{1,0:T(8,128)(2,1)} %constant.19.refs_14_) | copy-start | bytes 12292
  0.9 61.3 %copy-start.13 = (bf16[16,128]{1,0:T(8,128)(2,1)S(1)}, bf16[16,128]{1,0:T(8,128)(2,1)}, u32[]{:S(2)}) copy-start(bf16[16,128]{1,0:T(8,128)(2,1)} %constant.16.refs_13_) | copy-start | bytes 12292
  1.9 34.2 %all-to-all-start = ((f32[16,3,8,128]{3,2,1,0:T(8,128)}), f32[16,3,8,128]{3,2,1,0:T(8,128)S(1)}, u32[]{:S(2)}, u32[]{:S(2)}) async-start(f32[16,3,8,128]{3,2,1,0:T(8,128)} %get-tuple-element.21), calls=%async_computation | async-start | bytes 393216 | tf_op jit(solution)/shard_map/all_to_all | solution.py:541
  20.1 2.2 %copy-start = (f32[2,8,8,64,64]{4,3,2,1,0:T(8,128)S(1)}, f32[2,8,8,64,64]{4,3,2,1,0:T(8,128)}, u32[]{:S(2)}) copy-start(f32[2,8,8,64,64]{4,3,2,1,0:T(8,128)} %param.19) | copy-start | bytes 6291460
  22.3 0.8 copy-start.9
  23.0 0.8 copy-start.10
  23.8 0.8 copy-start.11
  24.5 0.7 copy-start.14
  25.2 0.7 copy-start.15
  25.9 0.7 copy-start.16
  26.6 0.7 copy-start.17
  27.2 0.7 copy-start.18
  27.9 0.7 copy-start.19
  28.5 0.7 copy-start.20
  29.2 33.0 %copy-start.2 = (bf16[512,256]{1,0:T(8,128)(2,1)S(1)}, bf16[512,256]{1,0:T(8,128)(2,1)}, u32[]{:S(2)}) copy-start(bf16[512,256]{1,0:T(8,128)(2,1)} %constant.24.refs_17_) | copy-start | bytes 786436
  29.2 33.0 %copy-start.3 = (bf16[256,512]{1,0:T(8,128)(2,1)S(1)}, bf16[256,512]{1,0:T(8,128)(2,1)}, u32[]{:S(2)}) copy-start(bf16[256,512]{1,0:T(8,128)(2,1)} %constant.15.refs_12_) | copy-start | bytes 786436
  29.2 33.0 %copy-start.4 = (bf16[256,512]{1,0:T(8,128)(2,1)S(1)}, bf16[256,512]{1,0:T(8,128)(2,1)}, u32[]{:S(2)}) copy-start(bf16[256,512]{1,0:T(8,128)(2,1)} %constant.12.refs_11_) | copy-start | bytes 786436
  29.2 33.0 %copy-start.6 = (bf16[128,512]{1,0:T(8,128)(2,1)S(1)}, bf16[128,512]{1,0:T(8,128)(2,1)}, u32[]{:S(2)}) copy-start(bf16[128,512]{1,0:T(8,128)(2,1)} %constant.20.refs_15_) | copy-start | bytes 393220
  36.9 25.2 %all-to-all-start.1 = ((f32[32,3,8,128]{3,2,1,0:T(8,128)}), f32[32,3,8,128]{3,2,1,0:T(8,128)S(1)}, u32[]{:S(2)}, u32[]{:S(2)}) async-start(f32[32,3,8,128]{3,2,1,0:T(8,128)} %get-tuple-element.24), calls=%async_computation.1 | async-start | bytes 786432 | tf_op jit(solution)/shard_map/all_to_all | solution.py:545
  48.4 9.6 %collective-permute-start.1 = (f32[3,32,128]{2,1,0:T(8,128)S(1)}, f32[3,32,128]{2,1,0:T(8,128)S(1)}, u32[]{:S(2)}, u32[]{:S(2)}) collective-permute-start(f32[3,32,128]{2,1,0:T(8,128)S(1)} %get-tuple-element.23.refs_1_), channel_id=1, source_target_pairs={{0,31},{1,2},{2,1},{3,4},{4,3},{5,6},{6,5},{7,8},{8,7},{9,10},{10,... | collective-permute-start | bytes 147464 | tf_op jit(solution)/shard_map/ppermute | solution.py:547
  51.9 6.9 %collective-permute-start = (f32[3,32,128]{2,1,0:T(8,128)S(1)}, f32[3,32,128]{2,1,0:T(8,128)S(1)}, u32[]{:S(2)}, u32[]{:S(2)}) collective-permute-start(f32[3,32,128]{2,1,0:T(8,128)S(1)} %get-tuple-element.23.refs_1_), channel_id=1, source_target_pairs={{0,1},{1,0},{2,3},{3,2},{4,5},{5,4},{6,7},{7,6},{8,9},{9,8},{10,11... | collective-permute-start | bytes 147464 | tf_op jit(solution)/shard_map/ppermute | solution.py:546
  88.8 22.5 %all-to-all-start.3 = ((f32[32,3,8,128]{3,2,1,0:T(8,128)}), f32[32,3,8,128]{3,2,1,0:T(8,128)S(1)}, u32[]{:S(2)}, u32[]{:S(2)}) async-start(f32[32,3,8,128]{3,2,1,0:T(8,128)} %get-tuple-element.34), calls=%async_computation.3 | async-start | bytes 786432 | tf_op jit(solution)/shard_map/all_to_all | solution.py:545
  97.6 9.6 %collective-permute-start.3 = (f32[3,32,128]{2,1,0:T(8,128)S(1)}, f32[3,32,128]{2,1,0:T(8,128)S(1)}, u32[]{:S(2)}, u32[]{:S(2)}) collective-permute-start(f32[3,32,128]{2,1,0:T(8,128)S(1)} %get-tuple-element.33.refs_1_), channel_id=1, source_target_pairs={{0,31},{1,2},{2,1},{3,4},{4,3},{5,6},{6,5},{7,8},{8,7},{9,10},{10,... | collective-permute-start | bytes 147464 | tf_op jit(solution)/shard_map/ppermute | solution.py:547
  101.1 6.9 %collective-permute-start.2 = (f32[3,32,128]{2,1,0:T(8,128)S(1)}, f32[3,32,128]{2,1,0:T(8,128)S(1)}, u32[]{:S(2)}, u32[]{:S(2)}) collective-permute-start(f32[3,32,128]{2,1,0:T(8,128)S(1)} %get-tuple-element.33.refs_1_), channel_id=1, source_target_pairs={{0,1},{1,0},{2,3},{3,2},{4,5},{5,4},{6,7},{7,6},{8,9},{9,8},{10,11... | collective-permute-start | bytes 147464 | tf_op jit(solution)/shard_map/ppermute | solution.py:546

commit v3 on v2

--- a/solution.py
+++ b/solution.py
@@ -20,6 +20,37 @@
 BF16 = jnp.bfloat16
 F32 = jnp.float32
 GELU_SCALE = math.sqrt(2.0 / math.pi)
+
+
+def refill_tables():
+    columns = np.zeros((128, 256), np.float32)
+    for cell in range(64):
+        columns[cell, LANE_L2 + cell // 2] = 0.5
+        columns[cell, LANE_L3 + cell // 4] = 0.25
+        columns[cell, LANE_L3_COPY + cell // 4] = 0.25
+    for cell in range(32):
+        columns[64 + cell, 128 + LANE_L2 + cell] = 1.0
+        columns[64 + cell, 128 + LANE_L3 + cell // 2] = 0.5
+        columns[64 + cell, 128 + LANE_L3_COPY + cell // 2] = 0.5
+    rows = np.zeros((96, 96), np.float32)
+    for side in range(2):
+        for channel in range(3):
+            base = side * 24 + channel * 8
+            for sub in range(8):
+                row = (sub + 4) % 8
+                if (row >= 4) == (side == 0):
+                    start = base + 2 * (row % 4)
+                    rows[base + sub, start : start + 2] = 0.5
+                else:
+                    rows[base + sub, 48 + base + sub] = 1.0
+                row = (sub + 2) % 4
+                if (row >= 2) == (side == 0):
+                    start = base + 4 * (row % 2)
+                    rows[48 + base + sub, start : start + 4] = 0.25
+                else:
+                    start = 48 + base + (2 * row + 4) % 8
+                    rows[48 + base + sub, start : start + 2] = 0.5
+    return np.concatenate([columns, columns], axis=0), np.concatenate([rows, rows], axis=1)
 
 
 def pool_tables():
@@ -142,17 +173,85 @@
             slots_ref[slot, channel] = jnp.where(ahead, lower[channel], upper[channel])
 
 
+def near_tiles(pieces, kept):
+    lane = lax.broadcasted_iota(jnp.int32, (8, 128), 1)
+    shared = jnp.where(
+        kept, pltpu.roll(pieces[0], 112, 1), pltpu.roll(pltpu.roll(pieces[1], 112, 1), 4, 0)
+    )
+    rest = jnp.where(lane < 96, shared, pltpu.roll(pieces[2], 16, 1))
+    return (
+        jnp.where(lane < 64, pieces[0], pltpu.roll(pieces[1], 64, 1)),
+        jnp.where(lane < 64, pieces[2], rest),
+    )
+
+
+def far_tiles(pieces):
+    lane = lax.broadcasted_iota(jnp.int32, (8, 128), 1)
+    return (
+        jnp.where(lane < 64, pltpu.roll(pieces[0], 64, 1), pieces[1]),
+        pltpu.roll(pieces[2], 64, 1),
+    )
+
+
+def emit_row_slots(slots_ref, position, upper, lower):
+    top = lax.broadcasted_iota(jnp.int32, (8, 128), 0) < 4
+    near = near_tiles(upper, top), near_tiles(lower, jnp.logical_not(top))
+    far = far_tiles(upper), far_tiles(lower)
+    count = slots_ref.shape[0]
+    for slot in range(count):
+        distance = lax.rem(slot - position + count, count)
+        ahead = distance < count // 2
+        beside = (distance == 1) | (distance == count - 1)
+        for tile in range(2):
+            slots_ref[slot, tile] = jnp.where(
+                beside,
+                jnp.where(ahead, near[1][tile], near[0][tile]),
+                jnp.where(ahead, far[1][tile], far[0][tile]),
+            )
+
+
+def received_rows(got_ref, position, columns, rows):
+    lane = lax.broadcasted_iota(jnp.int32, (8, 128), 1)
+    first = lane < LANE_L3
+    second = (lane >= LANE_L2) & (lane < LANE_L3_COPY)
+    near = {}
+    for offset in (-4, -3, -2, 2, 3, 4):
+        place = lax.rem(position + offset + 16, 16)
+        head, tail = got_ref[place, 0], got_ref[place, 1]
+        near[offset] = [pltpu.roll(head, 64, 1), head, pltpu.roll(tail, 64, 1)]
+    beside = []
+    for offset in (-1, 1):
+        place = lax.rem(position + offset + 16, 16)
+        head, tail = got_ref[place, 0], got_ref[place, 1]
+        beside.append(jnp.where(first, head, tail))
+        beside.append(jnp.where(first, pltpu.roll(head, 64, 1), pltpu.roll(tail, 4, 0)))
+        beside.append(jnp.where(first, tail, pltpu.roll(tail, 96, 1)))
+    high, low = split(jnp.concatenate(beside, axis=0))
+    across = matmul(jnp.concatenate([high, low], axis=1), columns)
+    high, low = split(jnp.concatenate([across[:, :128], across[:, 128:]], axis=0))
+    pooled = matmul(rows, jnp.concatenate([high, low], axis=0))
+    for side, offset in enumerate((-1, 1)):
+        near[offset] = []
+        for channel in range(3):
+            base = side * 24 + channel * 8
+            coarse = jnp.where(
+                second, pooled[base : base + 8], pooled[48 + base : 48 + base + 8]
+            )
+            near[offset].append(jnp.where(first, beside[side * 3 + channel], coarse))
+    return near
+
+
 def pool_kernel(current_ref, slots_ref, own_ref):
     flat = current_ref[...].reshape(96, 128)
     upper, lower = pooled_blocks(flat)
     for channel in range(3):
         own_ref[0, channel] = upper[channel]
         own_ref[1, channel] = lower[channel]
-    emit_slots(slots_ref, lax.axis_index("gx"), upper, lower)
-
-
-def strip_kernel(own_ref, got_ref, ready_ref, slots_ref, strip_ref):
-    position = lax.axis_index("gx")
+    emit_row_slots(slots_ref, lax.axis_index("gx"), upper, lower)
+
+
+def strip_kernel(own_ref, got_ref, columns_ref, rows_ref, ready_ref, slots_ref, strip_ref):
+    received = received_rows(got_ref, lax.axis_index("gx"), columns_ref[...], rows_ref[...])
     lane = lax.broadcasted_iota(jnp.int32, (8, 128), 1)
     sub = lax.broadcasted_iota(jnp.int32, (8, 128), 0)
     first = lane < LANE_L3
@@ -165,10 +264,7 @@
     upper_out = []
     lower_out = []
     for channel in range(3):
-        near = {
-            offset: got_ref[lax.rem(position + offset + 16, 16), channel]
-            for offset in (-4, -3, -2, -1, 1, 2, 3, 4)
-        }
+        near = {offset: blocks[channel] for offset, blocks in received.items()}
         near[0] = own_ref[0, channel]
         finest = [near[-1], own_ref[0, channel], own_ref[1, channel], near[1]]
         middle = [(-2, -1), (-1, 0), (0, 1), (1, 2)]
@@ -459,7 +555,7 @@
     for channel in range(3):
         own_ref[0, channel] = upper[channel]
         own_ref[1, channel] = lower[channel]
-    emit_slots(slots_ref, lax.axis_index("gx"), upper, lower)
+    emit_row_slots(slots_ref, lax.axis_index("gx"), upper, lower)
 
 
 VMEM = pl.BlockSpec(memory_space=pltpu.VMEM)
@@ -504,9 +600,12 @@
     n_gy = lax.axis_size("gy")
     tables = [half for table in fourier_tables() for half in halves_of_table(table)]
 
+    refill = [jnp.asarray(table).astype(BF16) for table in refill_tables()]
+
     block = (3, 8, 128)
+    row_block = (2, 8, 128)
     slots_x, own = call(
-        pool_kernel, "pool", [fields], [(n_gx, *block), (2, *block)]
+        pool_kernel, "pool", [fields], [(n_gx, *row_block), (2, *block)]
     )
     prepared = call(
         prepare_kernel,
@@ -540,7 +639,7 @@
     for step in range(STEPS):
         got_x = lax.all_to_all(slots_x, "gx", 0, 0, tiled=True)
         slots_y, strip = call(
-            strip_kernel, "strip", [own, got_x, prepared[-1]], [(n_gy, *block), (3, ROWS, 128)]
+            strip_kernel, "strip", [own, got_x, *refill, prepared[-1]], [(n_gy, *block), (3, ROWS, 128)]
         )
         got_y = lax.all_to_all(slots_y, "gy", 0, 0, tiled=True)
         twin = lax.ppermute(strip, "gy", twins)
@@ -560,7 +659,7 @@
                 middle_kernel,
                 "middle",
                 operands,
-                [fields.shape, (n_gx, *block), (2, *block)],
+                [fields.shape, (n_gx, *row_block), (2, *block)],
                 scratch,
             )
         else:

time: 117 us -> 115 us (0.983)
  starting transfers between devices: 57.5 us -> 53 us
  blocking collectives: 21.5 us -> 23.7 us
    all_to_all x2, starting transfers between devices: 20.1 us -> 15.7 us  [shards(): got_y = lax.all_to_all(slots_y, 'gy', 0, 0, tiled=True)]
    all_to_all x1, blocking collectives: 21.5 us -> 23.7 us  [shards(): got_x = lax.all_to_all(slots_x, 'gx', 0, 0, tiled=True)]
    unnamed x43 -> x47, local copies, waits for them, and re-layouts: 10.6 us -> 10.6 us
  transfers between devices with their start and end apart: 7 -> 7, of which waited for: 5 -> 5; matrix products, arithmetic and copies ran while one was open for 0% -> 0% of each run, Pallas kernels for 2% -> 3%
where the time goes in v3:
time: 115 us; the launch traced here: 114 us
  starting transfers between devices  53 us (46%)
  blocking collectives  23.7 us (21%)
  Pallas kernels  14.7 us (13%)
  waiting for transfers between devices  11.9 us (10%)
  local copies, waits for them, and re-layouts  10.6 us (9%)
    all_to_all x1, blocking collectives, shards(): got_x = lax.all_to_all(slots_x, 'gx', 0, 0, tiled=True)  23.7 us
    all_to_all x1, starting transfers between devices, shards(): got_x = lax.all_to_all(slots_x, 'gx', 0, 0, tiled=True)  18.2 us
    all_to_all x2, starting transfers between devices, shards(): got_y = lax.all_to_all(slots_y, 'gy', 0, 0, tiled=True)  15.7 us
    pallas_call x6, Pallas kernels, call(): pl.pallas_call(body, name=name, out_shape=[pltpu.VMEM(*(r if isinstance(r...  14.7 us
    ppermute x2, starting transfers between devices, shards(): twin = lax.ppermute(strip, 'gy', twins)  12 us
    unnamed x47, local copies, waits for them, and re-layouts  10.6 us
    ppermute x2, starting transfers between devices, shards(): other = lax.ppermute(strip, 'gy', others)  7.08 us
    all_to_all x2, waiting for transfers between devices, shards(): got_y = lax.all_to_all(slots_y, 'gy', 0, 0, tiled=True)  6.65 us
  transfers between devices with their start and end apart: 7, of which 5 were waited for; matrix products, arithmetic and copies ran while one was open for 0% of the time, Pallas kernels for 3%

profile of v3, /device:TPU:1, one launch (start us, length us, event | category | flops | bytes accessed | tf_op | source)
XLA Modules:
  0.0 114.2 jit_solution(6721842801038347679)
XLA Ops:
  0.0 0.0 copy-start.8
  0.0 0.0 copy-start.1
  0.0 0.0 copy-start.9
  0.0 0.8 copy-done.9
  0.8 0.0 copy-start.14
  0.8 0.0 copy-start.15
  0.9 1.1 pool.1
  1.9 18.2 %all-to-all-start = ((f32[16,2,8,128]{3,2,1,0:T(8,128)}), f32[16,2,8,128]{3,2,1,0:T(8,128)S(1)}, u32[]{:S(2)}, u32[]{:S(2)}) async-start(f32[16,2,8,128]{3,2,1,0:T(8,128)} %get-tuple-element.21), calls=%async_computation | async-start | bytes 262144 | tf_op jit(solution)/shard_map/all_to_all | solution.py:640
  20.1 0.0 copy-start
  20.1 2.2 %copy-done = f32[2,8,8,64,64]{4,3,2,1,0:T(8,128)S(1)} copy-done((f32[2,8,8,64,64]{4,3,2,1,0:T(8,128)S(1)}, f32[2,8,8,64,64]{4,3,2,1,0:T(8,128)}, u32[]{:S(2)}) %copy-start) | copy-done | bytes 2097176
  22.3 0.0 copy-start.11
  22.3 0.8 copy-done.11
  23.1 0.0 copy-start.12
  23.1 0.8 copy-done.12
  23.8 0.0 copy-start.13
  23.8 0.8 copy-done.13
  24.6 0.0 copy-start.16
  24.6 0.7 copy-done.16
  25.3 0.0 copy-start.17
  25.3 0.7 copy-done.17
  26.0 0.0 copy-start.18
  26.0 0.7 copy-done.18
  26.6 0.0 copy-start.19
  26.6 0.7 copy-done.19
  27.3 0.0 copy-start.20
  27.3 0.7 copy-done.20
  27.9 0.0 copy-start.21
  27.9 0.7 copy-done.21
  28.6 0.0 copy-start.22
  28.6 0.7 copy-done.22
  29.2 0.0 copy-start.5
  29.3 0.0 copy-start.6
  29.3 0.0 copy-start.10
  29.3 2.9 %prepare.1 = (f32[1024,128]{1,0:T(8,128)S(1)}, bf16[64,48]{1,0:T(8,128)(2,1)S(1)}, bf16[136,192]{1,0:T(8,128)(2,1)S(1)}, f32[128,128]{1,0:T(8,128)S(1)}, f32[3,1...) custom-call(f32[12,64]{1,0:T(8,128)S(1)} %copy-done.16, f32[1,64]{1,0:T(1,128)S(1)} %bitcast.11, f32[2,64,64,64]{3,2,1,0:T(8,128)S(1)} %bitcast.8, ...), custom_call_target="tpu_custom_call" | custom-call | tf_op jit(solution)/shard_map/prepare/pallas_call | solution.py:569
  32.2 3.6 %all-to-all-done.got_ref = f32[16,2,8,128]{3,2,1,0:T(8,128)S(1)} async-done(((f32[16,2,8,128]{3,2,1,0:T(8,128)}), f32[16,2,8,128]{3,2,1,0:T(8,128)S(1)}, u32[]{:S(2)}, u32[]{:S(2)}) %all-to-all-start) | async-done | bytes 131104 | tf_op jit(solution)/shard_map/all_to_all | solution.py:640
  35.7 0.0 copy-done.8
  35.7 0.0 copy-done.7
  35.7 1.2 %strip.2 = (f32[32,3,8,128]{3,2,1,0:T(8,128)}, f32[3,32,128]{2,1,0:T(8,128)S(1)}) custom-call(f32[2,3,8,128]{3,2,1,0:T(8,128)S(1)} %get-tuple-element.20.own_ref, f32[16,2,8,128]{3,2,1,0:T(8,128)S(1)} %all-to-all-done.got_ref, bf16[256,256]{1,0:T(8,128)(2,1)S(1)} %copy-done.7, bf16[96,192]{1,0:T(8,128)(2,1)S(1)} %copy-done.8, ...), custom_call_target="tpu_custom_call" | custom-call | tf_op jit(solution)/shard_map/strip/pallas_call | solution.py:569
  37.0 9.1 %all-to-all-start.1 = ((f32[32,3,8,128]{3,2,1,0:T(8,128)}), f32[32,3,8,128]{3,2,1,0:T(8,128)S(1)}, u32[]{:S(2)}, u32[]{:S(2)}) async-start(f32[32,3,8,128]{3,2,1,0:T(8,128)} %get-tuple-element.24), calls=%async_computation.1 | async-start | bytes 786432 | tf_op jit(solution)/shard_map/all_to_all | solution.py:644
  46.1 3.5 %collective-permute-start.1 = (f32[3,32,128]{2,1,0:T(8,128)S(1)}, f32[3,32,128]{2,1,0:T(8,128)S(1)}, u32[]{:S(2)}, u32[]{:S(2)}) collective-permute-start(f32[3,32,128]{2,1,0:T(8,128)S(1)} %get-tuple-element.23.refs_1_), channel_id=1, source_target_pairs={{0,31},{1,2},{2,1},{3,4},{4,3},{5,6},{6,5},{7,8},{8,7},{9,10},{10,... | collective-permute-start | bytes 147464 | tf_op jit(solution)/shard_map/ppermute | solution.py:646
  49.6 6.0 %collective-permute-start = (f32[3,32,128]{2,1,0:T(8,128)S(1)}, f32[3,32,128]{2,1,0:T(8,128)S(1)}, u32[]{:S(2)}, u32[]{:S(2)}) collective-permute-start(f32[3,32,128]{2,1,0:T(8,128)S(1)} %get-tuple-element.23.refs_1_), channel_id=1, source_target_pairs={{0,1},{1,0},{2,3},{3,2},{4,5},{5,4},{6,7},{7,6},{8,9},{9,8},{10,11... | collective-permute-start | bytes 147464 | tf_op jit(solution)/shard_map/ppermute | solution.py:645
  55.7 0.0 collective-permute-done.1.refs_3_
  55.7 0.8 collective-permute-done.refs_2_
  56.5 3.3 %all-to-all-done.1.refs_4_ = f32[32,3,8,128]{3,2,1,0:T(8,128)S(1)} async-done(((f32[32,3,8,128]{3,2,1,0:T(8,128)}), f32[32,3,8,128]{3,2,1,0:T(8,128)S(1)}, u32[]{:S(2)}, u32[]{:S(2)}) %all-to-all-start.1) | async-done | bytes 393248 | tf_op jit(solution)/shard_map/all_to_all | solution.py:644
  59.9 0.0 copy-done.1
  59.9 0.0 copy-done.14
  59.9 0.0 copy-done.15
  59.9 0.0 copy-done.2
  59.9 0.0 copy-done.3
  59.9 0.0 copy-done.4
  59.9 0.0 copy-done.5
  59.9 0.0 copy-done.6
  59.9 0.0 copy-done.10
  59.9 4.4 %middle.1 = (f32[3,32,128]{2,1,0:T(8,128)S(1)}, f32[16,2,8,128]{3,2,1,0:T(8,128)S(1)}, f32[2,3,8,128]{3,2,1,0:T(8,128)S(1)}) custom-call(f32[3,32,128]{2,1,0:T(8,128)S(1)} %copy-done.10, f32[3,32,128]{2,1,0:T(8,128)S(1)} %get-tuple-element.23.refs_1_, f32[3,32,128]{2,1,0:T(8,128)S(1)} %collective-permute-done.refs_2_, ...), custom_call_target="tpu_custom_call" | custom-call | tf_op jit(solution)/shard_map/middle/pallas_call | solution.py:569
  64.3 23.7 %all_to_all.20.got_ref = f32[16,2,8,128]{3,2,1,0:T(8,128)S(1)} all-to-all(f32[16,2,8,128]{3,2,1,0:T(8,128)S(1)} %get-tuple-element.32), channel_id=1, replica_groups=mesh['gx'=16,'gy'=32] {'gx'}, dimensions={0} | all-to-all | bytes 262144 | tf_op jit(solution)/shard_map/all_to_all | solution.py:640
  88.0 1.2 %strip.3 = (f32[32,3,8,128]{3,2,1,0:T(8,128)}, f32[3,32,128]{2,1,0:T(8,128)S(1)}) custom-call(f32[2,3,8,128]{3,2,1,0:T(8,128)S(1)} %get-tuple-element.31.own_ref, f32[16,2,8,128]{3,2,1,0:T(8,128)S(1)} %all_to_all.20.got_ref, bf16[256,256]{1,0:T(8,128)(2,1)S(1)} %copy-done.7, bf16[96,192]{1,0:T(8,128)(2,1)S(1)} %copy-done.8, ...), custom_call_target="tpu_custom_call" | custom-call | tf_op jit(solution)/shard_map/strip/pallas_call | solution.py:569
  89.2 6.6 %all-to-all-start.3 = ((f32[32,3,8,128]{3,2,1,0:T(8,128)}), f32[32,3,8,128]{3,2,1,0:T(8,128)S(1)}, u32[]{:S(2)}, u32[]{:S(2)}) async-start(f32[32,3,8,128]{3,2,1,0:T(8,128)} %get-tuple-element.34), calls=%async_computation.3 | async-start | bytes 786432 | tf_op jit(solution)/shard_map/all_to_all | solution.py:644
  95.8 3.5 %collective-permute-start.3 = (f32[3,32,128]{2,1,0:T(8,128)S(1)}, f32[3,32,128]{2,1,0:T(8,128)S(1)}, u32[]{:S(2)}, u32[]{:S(2)}) collective-permute-start(f32[3,32,128]{2,1,0:T(8,128)S(1)} %get-tuple-element.33.refs_1_), channel_id=1, source_target_pairs={{0,31},{1,2},{2,1},{3,4},{4,3},{5,6},{6,5},{7,8},{8,7},{9,10},{10,... | collective-permute-start | bytes 147464 | tf_op jit(solution)/shard_map/ppermute | solution.py:646
  99.3 6.0 %collective-permute-start.2 = (f32[3,32,128]{2,1,0:T(8,128)S(1)}, f32[3,32,128]{2,1,0:T(8,128)S(1)}, u32[]{:S(2)}, u32[]{:S(2)}) collective-permute-start(f32[3,32,128]{2,1,0:T(8,128)S(1)} %get-tuple-element.33.refs_1_), channel_id=1, source_target_pairs={{0,1},{1,0},{2,3},{3,2},{4,5},{5,4},{6,7},{7,6},{8,9},{9,8},{10,11... | collective-permute-start | bytes 147464 | tf_op jit(solution)/shard_map/ppermute | solution.py:645
  105.4 0.0 collective-permute-done.3.refs_3_
  105.4 0.8 collective-permute-done.2.refs_2_
  106.2 3.3 %all-to-all-done.3.refs_4_ = f32[32,3,8,128]{3,2,1,0:T(8,128)S(1)} async-done(((f32[32,3,8,128]{3,2,1,0:T(8,128)}), f32[32,3,8,128]{3,2,1,0:T(8,128)S(1)}, u32[]{:S(2)}, u32[]{:S(2)}) %all-to-all-start.3) | async-done | bytes 393248 | tf_op jit(solution)/shard_map/all_to_all | solution.py:644
  109.5 4.0 %final.1 = f32[3,32,128]{2,1,0:T(8,128)S(1)} custom-call(f32[3,32,128]{2,1,0:T(8,128)S(1)} %get-tuple-element.30.refs_0_, f32[3,32,128]{2,1,0:T(8,128)S(1)} %get-tuple-element.33.refs_1_, f32[3,32,128]{2,1,0:T(8,128)S(1)} %collective-permute-done.2.refs_2_, f32[3,32,128]{2,1,0:T(8,128)S(1)} %collective-permute-done.3.refs_3_, ...), custom_call_target="tpu_custom_call" | custom-call | tf_op jit(solution)/shard_map/final/pallas_call | solution.py:569
  113.5 0.6 copy.19
  (4 shorter events, 0.0 us)
Async XLA Ops:
  0.0 35.7 %copy-start.8 = (bf16[96,192]{1,0:T(8,128)(2,1)S(1)}, bf16[96,192]{1,0:T(8,128)(2,1)}, u32[]{:S(2)}) copy-start(bf16[96,192]{1,0:T(8,128)(2,1)} %constant.19.rows_ref) | copy-start | bytes 110596
  0.0 59.9 %copy-start.1 = (bf16[512,256]{1,0:T(8,128)(2,1)S(1)}, bf16[512,256]{1,0:T(8,128)(2,1)}, u32[]{:S(2)}) copy-start(bf16[512,256]{1,0:T(8,128)(2,1)} %constant.35.refs_18_) | copy-start | bytes 786436
  0.0 0.8 copy-start.9
  0.8 59.0 %copy-start.14 = (bf16[16,128]{1,0:T(8,128)(2,1)S(1)}, bf16[16,128]{1,0:T(8,128)(2,1)}, u32[]{:S(2)}) copy-start(bf16[16,128]{1,0:T(8,128)(2,1)} %constant.27.refs_14_) | copy-start | bytes 12292
  0.8 59.0 %copy-start.15 = (bf16[16,128]{1,0:T(8,128)(2,1)S(1)}, bf16[16,128]{1,0:T(8,128)(2,1)}, u32[]{:S(2)}) copy-start(bf16[16,128]{1,0:T(8,128)(2,1)} %constant.24.refs_13_) | copy-start | bytes 12292
  1.9 33.8 %all-to-all-start = ((f32[16,2,8,128]{3,2,1,0:T(8,128)}), f32[16,2,8,128]{3,2,1,0:T(8,128)S(1)}, u32[]{:S(2)}, u32[]{:S(2)}) async-start(f32[16,2,8,128]{3,2,1,0:T(8,128)} %get-tuple-element.21), calls=%async_computation | async-start | bytes 262144 | tf_op jit(solution)/shard_map/all_to_all | solution.py:640
  20.1 2.2 %copy-start = (f32[2,8,8,64,64]{4,3,2,1,0:T(8,128)S(1)}, f32[2,8,8,64,64]{4,3,2,1,0:T(8,128)}, u32[]{:S(2)}) copy-start(f32[2,8,8,64,64]{4,3,2,1,0:T(8,128)} %param.21) | copy-start | bytes 6291460
  22.3 0.8 copy-start.11
  23.1 0.8 copy-start.12
  23.8 0.8 copy-start.13
  24.6 0.7 copy-start.16
  25.3 0.7 copy-start.17
  26.0 0.7 copy-start.18
  26.6 0.7 copy-start.19
  27.3 0.7 copy-start.20
  27.9 0.7 copy-start.21
  28.6 0.7 copy-start.22
  29.2 6.5 %copy-start.7 = (bf16[256,256]{1,0:T(8,128)(2,1)S(1)}, bf16[256,256]{1,0:T(8,128)(2,1)}, u32[]{:S(2)}) copy-start(bf16[256,256]{1,0:T(8,128)(2,1)} %constant.18.columns_ref) | copy-start | bytes 393220
  29.2 30.6 %copy-start.2 = (bf16[512,256]{1,0:T(8,128)(2,1)S(1)}, bf16[512,256]{1,0:T(8,128)(2,1)}, u32[]{:S(2)}) copy-start(bf16[512,256]{1,0:T(8,128)(2,1)} %constant.32.refs_17_) | copy-start | bytes 786436
  29.2 30.6 %copy-start.3 = (bf16[256,512]{1,0:T(8,128)(2,1)S(1)}, bf16[256,512]{1,0:T(8,128)(2,1)}, u32[]{:S(2)}) copy-start(bf16[256,512]{1,0:T(8,128)(2,1)} %constant.23.refs_12_) | copy-start | bytes 786436
  29.2 30.6 %copy-start.4 = (bf16[256,512]{1,0:T(8,128)(2,1)S(1)}, bf16[256,512]{1,0:T(8,128)(2,1)}, u32[]{:S(2)}) copy-start(bf16[256,512]{1,0:T(8,128)(2,1)} %constant.20.refs_11_) | copy-start | bytes 786436
  29.2 30.7 %copy-start.5 = (bf16[128,512]{1,0:T(8,128)(2,1)S(1)}, bf16[128,512]{1,0:T(8,128)(2,1)}, u32[]{:S(2)}) copy-start(bf16[128,512]{1,0:T(8,128)(2,1)} %constant.31.refs_16_) | copy-start | bytes 393220
  29.3 30.7 %copy-start.6 = (bf16[128,512]{1,0:T(8,128)(2,1)S(1)}, bf16[128,512]{1,0:T(8,128)(2,1)}, u32[]{:S(2)}) copy-start(bf16[128,512]{1,0:T(8,128)(2,1)} %constant.28.refs_15_) | copy-start | bytes 393220
  29.3 30.6 %copy-start.10 = (f32[3,32,128]{2,1,0:T(8,128)S(1)}, f32[3,32,128]{2,1,0:T(8,128)}, u32[]{:S(2)}) copy-start(f32[3,32,128]{2,1,0:T(8,128)} %refs_0_.1) | copy-start | bytes 147460
  37.0 22.9 %all-to-all-start.1 = ((f32[32,3,8,128]{3,2,1,0:T(8,128)}), f32[32,3,8,128]{3,2,1,0:T(8,128)S(1)}, u32[]{:S(2)}, u32[]{:S(2)}) async-start(f32[32,3,8,128]{3,2,1,0:T(8,128)} %get-tuple-element.24), calls=%async_computation.1 | async-start | bytes 786432 | tf_op jit(solution)/shard_map/all_to_all | solution.py:644
  46.1 9.6 %collective-permute-start.1 = (f32[3,32,128]{2,1,0:T(8,128)S(1)}, f32[3,32,128]{2,1,0:T(8,128)S(1)}, u32[]{:S(2)}, u32[]{:S(2)}) collective-permute-start(f32[3,32,128]{2,1,0:T(8,128)S(1)} %get-tuple-element.23.refs_1_), channel_id=1, source_target_pairs={{0,31},{1,2},{2,1},{3,4},{4,3},{5,6},{6,5},{7,8},{8,7},{9,10},{10,... | collective-permute-start | bytes 147464 | tf_op jit(solution)/shard_map/ppermute | solution.py:646
  49.6 6.9 %collective-permute-start = (f32[3,32,128]{2,1,0:T(8,128)S(1)}, f32[3,32,128]{2,1,0:T(8,128)S(1)}, u32[]{:S(2)}, u32[]{:S(2)}) collective-permute-start(f32[3,32,128]{2,1,0:T(8,128)S(1)} %get-tuple-element.23.refs_1_), channel_id=1, source_target_pairs={{0,1},{1,0},{2,3},{3,2},{4,5},{5,4},{6,7},{7,6},{8,9},{9,8},{10,11... | collective-permute-start | bytes 147464 | tf_op jit(solution)/shard_map/ppermute | solution.py:645
  89.2 20.4 %all-to-all-start.3 = ((f32[32,3,8,128]{3,2,1,0:T(8,128)}), f32[32,3,8,128]{3,2,1,0:T(8,128)S(1)}, u32[]{:S(2)}, u32[]{:S(2)}) async-start(f32[32,3,8,128]{3,2,1,0:T(8,128)} %get-tuple-element.34), calls=%async_computation.3 | async-start | bytes 786432 | tf_op jit(solution)/shard_map/all_to_all | solution.py:644
  95.8 9.6 %collective-permute-start.3 = (f32[3,32,128]{2,1,0:T(8,128)S(1)}, f32[3,32,128]{2,1,0:T(8,128)S(1)}, u32[]{:S(2)}, u32[]{:S(2)}) collective-permute-start(f32[3,32,128]{2,1,0:T(8,128)S(1)} %get-tuple-element.33.refs_1_), channel_id=1, source_target_pairs={{0,31},{1,2},{2,1},{3,4},{4,3},{5,6},{6,5},{7,8},{8,7},{9,10},{10,... | collective-permute-start | bytes 147464 | tf_op jit(solution)/shard_map/ppermute | solution.py:646
  99.3 6.9 %collective-permute-start.2 = (f32[3,32,128]{2,1,0:T(8,128)S(1)}, f32[3,32,128]{2,1,0:T(8,128)S(1)}, u32[]{:S(2)}, u32[]{:S(2)}) collective-permute-start(f32[3,32,128]{2,1,0:T(8,128)S(1)} %get-tuple-element.33.refs_1_), channel_id=1, source_target_pairs={{0,1},{1,0},{2,3},{3,2},{4,5},{5,4},{6,7},{7,6},{8,9},{9,8},{10,11... | collective-permute-start | bytes 147464 | tf_op jit(solution)/shard_map/ppermute | solution.py:645

commit v4 on v3

--- a/solution.py
+++ b/solution.py
@@ -565,10 +565,9 @@
     return pltpu.with_memory_space_constraint(operand, pltpu.VMEM)
 
 
-def call(body, name, operands, results, scratch=()):
+def call(body, operands, results, scratch=()):
     return pl.pallas_call(
         body,
-        name=name,
         out_shape=[pltpu.VMEM(*(r if isinstance(r[0], tuple) else (r, F32))) for r in results],
         in_specs=[VMEM] * len(operands),
         out_specs=[VMEM] * len(results),
@@ -604,12 +603,9 @@
 
     block = (3, 8, 128)
     row_block = (2, 8, 128)
-    slots_x, own = call(
-        pool_kernel, "pool", [fields], [(n_gx, *row_block), (2, *block)]
-    )
+    slots_x, own = call(pool_kernel, [fields], [(n_gx, *row_block), (2, *block)])
     prepared = call(
         prepare_kernel,
-        "prepare",
         [
             lift_weight,
             lift_bias[None],
@@ -639,11 +635,11 @@
     for step in range(STEPS):
         got_x = lax.all_to_all(slots_x, "gx", 0, 0, tiled=True)
         slots_y, strip = call(
-            strip_kernel, "strip", [own, got_x, *refill, prepared[-1]], [(n_gy, *block), (3, ROWS, 128)]
+            strip_kernel, [own, got_x, *refill, prepared[-1]], [(n_gy, *block), (3, ROWS, 128)]
         )
+        other = lax.ppermute(strip, "gy", others)
         got_y = lax.all_to_all(slots_y, "gy", 0, 0, tiled=True)
         twin = lax.ppermute(strip, "gy", twins)
-        other = lax.ppermute(strip, "gy", others)
         operands = [
             current,
             strip,
@@ -656,14 +652,10 @@
         scratch = [pltpu.VMEM((ROWS * PADDED, 128), F32), pltpu.VMEM((ROWS * 8, 128), F32), pltpu.VMEM((3, ROWS * 8, 128), F32)]
         if step + 1 < STEPS:
             current, slots_x, own = call(
-                middle_kernel,
-                "middle",
-                operands,
-                [fields.shape, (n_gx, *row_block), (2, *block)],
-                scratch,
+                middle_kernel, operands, [fields.shape, (n_gx, *row_block), (2, *block)], scratch
             )
         else:
-            (current,) = call(final_kernel, "final", operands, [fields.shape], scratch)
+            (current,) = call(final_kernel, operands, [fields.shape], scratch)
     return current
 
 

time: 115 us -> 115 us (level)
  no operation moved by 1% of the time
where the time goes in v4:
time: 115 us; the launch traced here: 114 us
  starting transfers between devices  53 us (46%)
  blocking collectives  23.7 us (21%)
  Pallas kernels  14.7 us (13%)
  waiting for transfers between devices  11.9 us (10%)
  local copies, waits for them, and re-layouts  10.6 us (9%)
    all_to_all x1, blocking collectives, shards(): got_x = lax.all_to_all(slots_x, 'gx', 0, 0, tiled=True)  23.7 us
    all_to_all x1, starting transfers between devices, shards(): got_x = lax.all_to_all(slots_x, 'gx', 0, 0, tiled=True)  18.2 us
    all_to_all x2, starting transfers between devices, shards(): got_y = lax.all_to_all(slots_y, 'gy', 0, 0, tiled=True)  15.7 us
    pallas_call x6, Pallas kernels, call(): pl.pallas_call(body, out_shape=[pltpu.VMEM(*(r if isinstance(r[0], tuple)...  14.7 us
    ppermute x2, starting transfers between devices, shards(): twin = lax.ppermute(strip, 'gy', twins)  12 us
    unnamed x47, local copies, waits for them, and re-layouts  10.6 us
    ppermute x2, starting transfers between devices, shards(): other = lax.ppermute(strip, 'gy', others)  7.08 us
    all_to_all x2, waiting for transfers between devices, shards(): got_y = lax.all_to_all(slots_y, 'gy', 0, 0, tiled=True)  6.65 us
  transfers between devices with their start and end apart: 7, of which 5 were waited for; matrix products, arithmetic and copies ran while one was open for 0% of the time, Pallas kernels for 3%

profile of v4, /device:TPU:1, one launch (start us, length us, event | category | flops | bytes accessed | tf_op | source)
XLA Modules:
  0.0 114.2 jit_solution(6721842801038347679)
XLA Ops:
  0.0 0.0 copy-start.8
  0.0 0.0 copy-start.1
  0.0 0.0 copy-start.9
  0.0 0.8 copy-done.9
  0.8 0.0 copy-start.14
  0.8 0.0 copy-start.15
  0.9 1.1 shard_map.172
  1.9 18.2 %all-to-all-start = ((f32[16,2,8,128]{3,2,1,0:T(8,128)}), f32[16,2,8,128]{3,2,1,0:T(8,128)S(1)}, u32[]{:S(2)}, u32[]{:S(2)}) async-start(f32[16,2,8,128]{3,2,1,0:T(8,128)} %get-tuple-element.21), calls=%async_computation | async-start | bytes 262144 | tf_op jit(solution)/shard_map/all_to_all | solution.py:636
  20.1 0.0 copy-start
  20.1 2.2 %copy-done = f32[2,8,8,64,64]{4,3,2,1,0:T(8,128)S(1)} copy-done((f32[2,8,8,64,64]{4,3,2,1,0:T(8,128)S(1)}, f32[2,8,8,64,64]{4,3,2,1,0:T(8,128)}, u32[]{:S(2)}) %copy-start) | copy-done | bytes 2097176
  22.3 0.0 copy-start.11
  22.3 0.8 copy-done.11
  23.1 0.0 copy-start.12
  23.1 0.8 copy-done.12
  23.8 0.8 copy-done.13
  24.6 0.0 copy-start.16
  24.6 0.7 copy-done.16
  25.3 0.0 copy-start.17
  25.3 0.7 copy-done.17
  26.0 0.0 copy-start.18
  26.0 0.7 copy-done.18
  26.6 0.0 copy-start.19
  26.6 0.7 copy-done.19
  27.3 0.0 copy-start.20
  27.3 0.7 copy-done.20
  27.9 0.0 copy-start.21
  27.9 0.7 copy-done.21
  28.6 0.0 copy-start.22
  28.6 0.7 copy-done.22
  29.2 0.0 copy-start.7
  29.2 0.0 copy-start.5
  29.3 0.0 copy-start.6
  29.3 0.0 copy-start.10
  29.3 2.9 %shard_map.173 = (f32[1024,128]{1,0:T(8,128)S(1)}, bf16[64,48]{1,0:T(8,128)(2,1)S(1)}, bf16[136,192]{1,0:T(8,128)(2,1)S(1)}, f32[128,128]{1,0:T(8,128)S(1)}, f32...) custom-call(f32[12,64]{1,0:T(8,128)S(1)} %copy-done.16, f32[1,64]{1,0:T(1,128)S(1)} %bitcast.11, ...), custom_call_target="tpu_custom_call" | custom-call | tf_op jit(solution)/shard_map/pallas_call | solution.py:569
  32.2 3.6 %all-to-all-done.got_ref = f32[16,2,8,128]{3,2,1,0:T(8,128)S(1)} async-done(((f32[16,2,8,128]{3,2,1,0:T(8,128)}), f32[16,2,8,128]{3,2,1,0:T(8,128)S(1)}, u32[]{:S(2)}, u32[]{:S(2)}) %all-to-all-start) | async-done | bytes 131104 | tf_op jit(solution)/shard_map/all_to_all | solution.py:636
  35.7 0.0 copy-done.8
  35.7 0.0 copy-done.7
  35.7 1.2 %shard_map.174 = (f32[32,3,8,128]{3,2,1,0:T(8,128)}, f32[3,32,128]{2,1,0:T(8,128)S(1)}) custom-call(f32[2,3,8,128]{3,2,1,0:T(8,128)S(1)} %get-tuple-element.20.own_ref, f32[16,2,8,128]{3,2,1,0:T(8,128)S(1)} %all-to-all-done.got_ref, bf16[256,256]{1,0:T(8,128)(2,1)S(1)} %copy-done.7, bf16[96,192]{1,0:T(8,128)(2,1)S(1)} %copy-done.8, ...), custom_call_target="tpu_custom_call" | custom-call | tf_op jit(solution)/shard_map/pallas_call | solution.py:569
  37.0 9.1 %all-to-all-start.1 = ((f32[32,3,8,128]{3,2,1,0:T(8,128)}), f32[32,3,8,128]{3,2,1,0:T(8,128)S(1)}, u32[]{:S(2)}, u32[]{:S(2)}) async-start(f32[32,3,8,128]{3,2,1,0:T(8,128)} %get-tuple-element.24), calls=%async_computation.1 | async-start | bytes 786432 | tf_op jit(solution)/shard_map/all_to_all | solution.py:641
  46.1 3.5 %collective-permute-start.1 = (f32[3,32,128]{2,1,0:T(8,128)S(1)}, f32[3,32,128]{2,1,0:T(8,128)S(1)}, u32[]{:S(2)}, u32[]{:S(2)}) collective-permute-start(f32[3,32,128]{2,1,0:T(8,128)S(1)} %get-tuple-element.23.refs_1_), channel_id=1, source_target_pairs={{0,31},{1,2},{2,1},{3,4},{4,3},{5,6},{6,5},{7,8},{8,7},{9,10},{10,... | collective-permute-start | bytes 147464 | tf_op jit(solution)/shard_map/ppermute | solution.py:640
  49.6 6.0 %collective-permute-start = (f32[3,32,128]{2,1,0:T(8,128)S(1)}, f32[3,32,128]{2,1,0:T(8,128)S(1)}, u32[]{:S(2)}, u32[]{:S(2)}) collective-permute-start(f32[3,32,128]{2,1,0:T(8,128)S(1)} %get-tuple-element.23.refs_1_), channel_id=1, source_target_pairs={{0,1},{1,0},{2,3},{3,2},{4,5},{5,4},{6,7},{7,6},{8,9},{9,8},{10,11... | collective-permute-start | bytes 147464 | tf_op jit(solution)/shard_map/ppermute | solution.py:642
  55.7 0.0 collective-permute-done.1.refs_3_
  55.7 0.8 collective-permute-done.refs_2_
  56.5 3.3 %all-to-all-done.1.refs_4_ = f32[32,3,8,128]{3,2,1,0:T(8,128)S(1)} async-done(((f32[32,3,8,128]{3,2,1,0:T(8,128)}), f32[32,3,8,128]{3,2,1,0:T(8,128)S(1)}, u32[]{:S(2)}, u32[]{:S(2)}) %all-to-all-start.1) | async-done | bytes 393248 | tf_op jit(solution)/shard_map/all_to_all | solution.py:641
  59.9 0.0 copy-done.1
  59.9 0.0 copy-done.14
  59.9 0.0 copy-done.15
  59.9 0.0 copy-done.2
  59.9 0.0 copy-done.3
  59.9 0.0 copy-done.4
  59.9 0.0 copy-done.5
  59.9 0.0 copy-done.6
  59.9 0.0 copy-done.10
  59.9 4.4 %shard_map.175 = (f32[3,32,128]{2,1,0:T(8,128)S(1)}, f32[16,2,8,128]{3,2,1,0:T(8,128)S(1)}, f32[2,3,8,128]{3,2,1,0:T(8,128)S(1)}) custom-call(f32[3,32,128]{2,1,0:T(8,128)S(1)} %copy-done.10, f32[3,32,128]{2,1,0:T(8,128)S(1)} %get-tuple-element.23.refs_1_, f32[3,32,128]{2,1,0:T(8,128)S(1)} %collective-permute-done.refs_2_, ...), custom_call_target="tpu_custom_call" | custom-call | tf_op jit(solution)/shard_map/pallas_call | solution.py:569
  64.3 23.7 %all_to_all.20.got_ref = f32[16,2,8,128]{3,2,1,0:T(8,128)S(1)} all-to-all(f32[16,2,8,128]{3,2,1,0:T(8,128)S(1)} %get-tuple-element.32), channel_id=1, replica_groups=mesh['gx'=16,'gy'=32] {'gx'}, dimensions={0} | all-to-all | bytes 262144 | tf_op jit(solution)/shard_map/all_to_all | solution.py:636
  88.0 1.2 %shard_map.176 = (f32[32,3,8,128]{3,2,1,0:T(8,128)}, f32[3,32,128]{2,1,0:T(8,128)S(1)}) custom-call(f32[2,3,8,128]{3,2,1,0:T(8,128)S(1)} %get-tuple-element.31.own_ref, f32[16,2,8,128]{3,2,1,0:T(8,128)S(1)} %all_to_all.20.got_ref, bf16[256,256]{1,0:T(8,128)(2,1)S(1)} %copy-done.7, bf16[96,192]{1,0:T(8,128)(2,1)S(1)} %copy-done.8, ...), custom_call_target="tpu_custom_call" | custom-call | tf_op jit(solution)/shard_map/pallas_call | solution.py:569
  89.2 6.6 %all-to-all-start.3 = ((f32[32,3,8,128]{3,2,1,0:T(8,128)}), f32[32,3,8,128]{3,2,1,0:T(8,128)S(1)}, u32[]{:S(2)}, u32[]{:S(2)}) async-start(f32[32,3,8,128]{3,2,1,0:T(8,128)} %get-tuple-element.34), calls=%async_computation.3 | async-start | bytes 786432 | tf_op jit(solution)/shard_map/all_to_all | solution.py:641
  95.8 3.5 %collective-permute-start.3 = (f32[3,32,128]{2,1,0:T(8,128)S(1)}, f32[3,32,128]{2,1,0:T(8,128)S(1)}, u32[]{:S(2)}, u32[]{:S(2)}) collective-permute-start(f32[3,32,128]{2,1,0:T(8,128)S(1)} %get-tuple-element.33.refs_1_), channel_id=1, source_target_pairs={{0,31},{1,2},{2,1},{3,4},{4,3},{5,6},{6,5},{7,8},{8,7},{9,10},{10,... | collective-permute-start | bytes 147464 | tf_op jit(solution)/shard_map/ppermute | solution.py:640
  99.3 6.0 %collective-permute-start.2 = (f32[3,32,128]{2,1,0:T(8,128)S(1)}, f32[3,32,128]{2,1,0:T(8,128)S(1)}, u32[]{:S(2)}, u32[]{:S(2)}) collective-permute-start(f32[3,32,128]{2,1,0:T(8,128)S(1)} %get-tuple-element.33.refs_1_), channel_id=1, source_target_pairs={{0,1},{1,0},{2,3},{3,2},{4,5},{5,4},{6,7},{7,6},{8,9},{9,8},{10,11... | collective-permute-start | bytes 147464 | tf_op jit(solution)/shard_map/ppermute | solution.py:642
  105.4 0.0 collective-permute-done.3.refs_3_
  105.4 0.8 collective-permute-done.2.refs_2_
  106.2 3.3 %all-to-all-done.3.refs_4_ = f32[32,3,8,128]{3,2,1,0:T(8,128)S(1)} async-done(((f32[32,3,8,128]{3,2,1,0:T(8,128)}), f32[32,3,8,128]{3,2,1,0:T(8,128)S(1)}, u32[]{:S(2)}, u32[]{:S(2)}) %all-to-all-start.3) | async-done | bytes 393248 | tf_op jit(solution)/shard_map/all_to_all | solution.py:641
  109.5 4.0 %shard_map.177 = f32[3,32,128]{2,1,0:T(8,128)S(1)} custom-call(f32[3,32,128]{2,1,0:T(8,128)S(1)} %get-tuple-element.30.refs_0_, f32[3,32,128]{2,1,0:T(8,128)S(1)} %get-tuple-element.33.refs_1_, f32[3,32,128]{2,1,0:T(8,128)S(1)} %collective-permute-done.2.refs_2_, f32[3,32,128]{2,1,0:T(8,128)S(1)} %collective-permute-done.3.refs_3_, ...), custom_call_target="tpu_custom_call" | custom-call | tf_op jit(solution)/shard_map/pallas_call | solution.py:569
  113.5 0.6 copy.19
  (4 shorter events, 0.0 us)
Async XLA Ops:
  0.0 35.7 %copy-start.8 = (bf16[96,192]{1,0:T(8,128)(2,1)S(1)}, bf16[96,192]{1,0:T(8,128)(2,1)}, u32[]{:S(2)}) copy-start(bf16[96,192]{1,0:T(8,128)(2,1)} %constant.19.rows_ref) | copy-start | bytes 110596
  0.0 59.9 %copy-start.1 = (bf16[512,256]{1,0:T(8,128)(2,1)S(1)}, bf16[512,256]{1,0:T(8,128)(2,1)}, u32[]{:S(2)}) copy-start(bf16[512,256]{1,0:T(8,128)(2,1)} %constant.35.refs_18_) | copy-start | bytes 786436
  0.0 0.8 copy-start.9
  0.8 59.0 %copy-start.14 = (bf16[16,128]{1,0:T(8,128)(2,1)S(1)}, bf16[16,128]{1,0:T(8,128)(2,1)}, u32[]{:S(2)}) copy-start(bf16[16,128]{1,0:T(8,128)(2,1)} %constant.27.refs_14_) | copy-start | bytes 12292
  0.8 59.0 %copy-start.15 = (bf16[16,128]{1,0:T(8,128)(2,1)S(1)}, bf16[16,128]{1,0:T(8,128)(2,1)}, u32[]{:S(2)}) copy-start(bf16[16,128]{1,0:T(8,128)(2,1)} %constant.24.refs_13_) | copy-start | bytes 12292
  1.9 33.8 %all-to-all-start = ((f32[16,2,8,128]{3,2,1,0:T(8,128)}), f32[16,2,8,128]{3,2,1,0:T(8,128)S(1)}, u32[]{:S(2)}, u32[]{:S(2)}) async-start(f32[16,2,8,128]{3,2,1,0:T(8,128)} %get-tuple-element.21), calls=%async_computation | async-start | bytes 262144 | tf_op jit(solution)/shard_map/all_to_all | solution.py:636
  20.1 2.2 %copy-start = (f32[2,8,8,64,64]{4,3,2,1,0:T(8,128)S(1)}, f32[2,8,8,64,64]{4,3,2,1,0:T(8,128)}, u32[]{:S(2)}) copy-start(f32[2,8,8,64,64]{4,3,2,1,0:T(8,128)} %param.21) | copy-start | bytes 6291460
  22.3 0.8 copy-start.11
  23.1 0.8 copy-start.12
  23.8 0.8 copy-start.13
  24.6 0.7 copy-start.16
  25.3 0.7 copy-start.17
  26.0 0.7 copy-start.18
  26.6 0.7 copy-start.19
  27.3 0.7 copy-start.20
  27.9 0.7 copy-start.21
  28.6 0.7 copy-start.22
  29.2 6.5 %copy-start.7 = (bf16[256,256]{1,0:T(8,128)(2,1)S(1)}, bf16[256,256]{1,0:T(8,128)(2,1)}, u32[]{:S(2)}) copy-start(bf16[256,256]{1,0:T(8,128)(2,1)} %constant.18.columns_ref) | copy-start | bytes 393220
  29.2 30.6 %copy-start.2 = (bf16[512,256]{1,0:T(8,128)(2,1)S(1)}, bf16[512,256]{1,0:T(8,128)(2,1)}, u32[]{:S(2)}) copy-start(bf16[512,256]{1,0:T(8,128)(2,1)} %constant.32.refs_17_) | copy-start | bytes 786436
  29.2 30.6 %copy-start.3 = (bf16[256,512]{1,0:T(8,128)(2,1)S(1)}, bf16[256,512]{1,0:T(8,128)(2,1)}, u32[]{:S(2)}) copy-start(bf16[256,512]{1,0:T(8,128)(2,1)} %constant.23.refs_12_) | copy-start | bytes 786436
  29.2 30.6 %copy-start.4 = (bf16[256,512]{1,0:T(8,128)(2,1)S(1)}, bf16[256,512]{1,0:T(8,128)(2,1)}, u32[]{:S(2)}) copy-start(bf16[256,512]{1,0:T(8,128)(2,1)} %constant.20.refs_11_) | copy-start | bytes 786436
  29.2 30.7 %copy-start.5 = (bf16[128,512]{1,0:T(8,128)(2,1)S(1)}, bf16[128,512]{1,0:T(8,128)(2,1)}, u32[]{:S(2)}) copy-start(bf16[128,512]{1,0:T(8,128)(2,1)} %constant.31.refs_16_) | copy-start | bytes 393220
  29.3 30.7 %copy-start.6 = (bf16[128,512]{1,0:T(8,128)(2,1)S(1)}, bf16[128,512]{1,0:T(8,128)(2,1)}, u32[]{:S(2)}) copy-start(bf16[128,512]{1,0:T(8,128)(2,1)} %constant.28.refs_15_) | copy-start | bytes 393220
  29.3 30.6 %copy-start.10 = (f32[3,32,128]{2,1,0:T(8,128)S(1)}, f32[3,32,128]{2,1,0:T(8,128)}, u32[]{:S(2)}) copy-start(f32[3,32,128]{2,1,0:T(8,128)} %refs_0_.1) | copy-start | bytes 147460
  37.0 22.9 %all-to-all-start.1 = ((f32[32,3,8,128]{3,2,1,0:T(8,128)}), f32[32,3,8,128]{3,2,1,0:T(8,128)S(1)}, u32[]{:S(2)}, u32[]{:S(2)}) async-start(f32[32,3,8,128]{3,2,1,0:T(8,128)} %get-tuple-element.24), calls=%async_computation.1 | async-start | bytes 786432 | tf_op jit(solution)/shard_map/all_to_all | solution.py:641
  46.1 9.6 %collective-permute-start.1 = (f32[3,32,128]{2,1,0:T(8,128)S(1)}, f32[3,32,128]{2,1,0:T(8,128)S(1)}, u32[]{:S(2)}, u32[]{:S(2)}) collective-permute-start(f32[3,32,128]{2,1,0:T(8,128)S(1)} %get-tuple-element.23.refs_1_), channel_id=1, source_target_pairs={{0,31},{1,2},{2,1},{3,4},{4,3},{5,6},{6,5},{7,8},{8,7},{9,10},{10,... | collective-permute-start | bytes 147464 | tf_op jit(solution)/shard_map/ppermute | solution.py:640
  49.6 6.9 %collective-permute-start = (f32[3,32,128]{2,1,0:T(8,128)S(1)}, f32[3,32,128]{2,1,0:T(8,128)S(1)}, u32[]{:S(2)}, u32[]{:S(2)}) collective-permute-start(f32[3,32,128]{2,1,0:T(8,128)S(1)} %get-tuple-element.23.refs_1_), channel_id=1, source_target_pairs={{0,1},{1,0},{2,3},{3,2},{4,5},{5,4},{6,7},{7,6},{8,9},{9,8},{10,11... | collective-permute-start | bytes 147464 | tf_op jit(solution)/shard_map/ppermute | solution.py:642
  89.2 20.4 %all-to-all-start.3 = ((f32[32,3,8,128]{3,2,1,0:T(8,128)}), f32[32,3,8,128]{3,2,1,0:T(8,128)S(1)}, u32[]{:S(2)}, u32[]{:S(2)}) async-start(f32[32,3,8,128]{3,2,1,0:T(8,128)} %get-tuple-element.34), calls=%async_computation.3 | async-start | bytes 786432 | tf_op jit(solution)/shard_map/all_to_all | solution.py:641
  95.8 9.6 %collective-permute-start.3 = (f32[3,32,128]{2,1,0:T(8,128)S(1)}, f32[3,32,128]{2,1,0:T(8,128)S(1)}, u32[]{:S(2)}, u32[]{:S(2)}) collective-permute-start(f32[3,32,128]{2,1,0:T(8,128)S(1)} %get-tuple-element.33.refs_1_), channel_id=1, source_target_pairs={{0,31},{1,2},{2,1},{3,4},{4,3},{5,6},{6,5},{7,8},{8,7},{9,10},{10,... | collective-permute-start | bytes 147464 | tf_op jit(solution)/shard_map/ppermute | solution.py:640
  99.3 6.9 %collective-permute-start.2 = (f32[3,32,128]{2,1,0:T(8,128)S(1)}, f32[3,32,128]{2,1,0:T(8,128)S(1)}, u32[]{:S(2)}, u32[]{:S(2)}) collective-permute-start(f32[3,32,128]{2,1,0:T(8,128)S(1)} %get-tuple-element.33.refs_1_), channel_id=1, source_target_pairs={{0,1},{1,0},{2,3},{3,2},{4,5},{5,4},{6,7},{7,6},{8,9},{9,8},{10,11... | collective-permute-start | bytes 147464 | tf_op jit(solution)/shard_map/ppermute | solution.py:642

commit v5 on v3

--- a/solution.py
+++ b/solution.py
@@ -497,38 +497,53 @@
     inner_left = inner_ref[...]
     inner_bias = jnp.concatenate([inner_bias_ref[...], inner_bias_ref[...]], axis=1)
     offset = jnp.concatenate([offset_ref[...], offset_ref[...]], axis=1)
+    pending = []
+
+    def finish(row, mixed):
+        wide = matmul(inner_left, stacked_right(mixed))
+        hidden = gelu_of_double(wide[:128] + inner_bias)
+        total = wide[128:136] + offset
+        for half in range(2):
+            lanes = slice(half * 128, half * 128 + 128)
+            results_ref[(row + half) * 8 : (row + half) * 8 + 8, :] = total[:, lanes]
+            for channel in range(3):
+                partial_ref[channel, (row + half) * 8 : (row + half) * 8 + 8] = jnp.sum(
+                    (hidden[:, lanes] * last_ref[channel]).reshape(16, 8, 128), axis=0
+                )
+
     for pair in range(4):
         table = (
             back_cols_high_ref[pair * 128 : pair * 128 + 128, :],
             back_cols_low_ref[pair * 128 : pair * 128 + 128, :],
         )
-        spectral = product(stacked, table)
+        spectral = matmul(
+            jnp.concatenate([stacked[0], stacked[0], stacked[1]], axis=1),
+            jnp.concatenate([table[0], table[1], table[0]], axis=0),
+        )
         for block in range(4):
             row = block * 8 + pair * 2
-            cells = jnp.concatenate(
-                [
-                    features_ref[row * PADDED : (row + 1) * PADDED, :],
-                    features_ref[(row + 1) * PADDED : (row + 2) * PADDED, :],
-                ],
-                axis=1,
-            )
-            mixed = gelu_of_double(
-                spectral[block * 64 : block * 64 + 64] + matmul(skip, stacked_right(cells))
-            )
-            wide = matmul(inner_left, stacked_right(mixed))
-            hidden = gelu_of_double(wide[:128] + inner_bias)
-            total = wide[128:136] + offset
-            for half in range(2):
-                lanes = slice(half * 128, half * 128 + 128)
-                results_ref[(row + half) * 8 : (row + half) * 8 + 8, :] = total[:, lanes]
-                for channel in range(3):
-                    partial = None
-                    for start in range(0, 128, 8):
-                        term = hidden[start : start + 8, lanes] * last_ref[
-                            channel, start : start + 8
-                        ]
-                        partial = term if partial is None else partial + term
-                    partial_ref[channel, (row + half) * 8 : (row + half) * 8 + 8] = partial
+            high, low = (
+                jnp.concatenate(
+                    [
+                        half[row * PADDED : (row + 1) * PADDED],
+                        half[(row + 1) * PADDED : (row + 2) * PADDED],
+                    ],
+                    axis=1,
+                )
+                for half in features
+            )
+            cells = jnp.concatenate([high, low, high], axis=0)
+            pending.append(
+                (
+                    row,
+                    gelu_of_double(
+                        spectral[block * 64 : block * 64 + 64] + matmul(skip, cells)
+                    ),
+                )
+            )
+            if len(pending) == 2:
+                finish(*pending.pop(0))
+    finish(*pending.pop(0))
 
     def sublane_sum(channel):
         total = results_ref[pl.ds(channel, ROWS, stride=8), :]

time: 115 us -> 114 us (level)
  no operation moved by 1% of the time
where the time goes in v5:
time: 114 us; the launch traced here: 113 us
  starting transfers between devices  53 us (46%)
  blocking collectives  23.7 us (21%)
  Pallas kernels  13.9 us (12%)
  waiting for transfers between devices  11.9 us (10%)
  local copies, waits for them, and re-layouts  10.6 us (9%)
    all_to_all x1, blocking collectives, shards(): got_x = lax.all_to_all(slots_x, 'gx', 0, 0, tiled=True)  23.7 us
    all_to_all x1, starting transfers between devices, shards(): got_x = lax.all_to_all(slots_x, 'gx', 0, 0, tiled=True)  18.2 us
    all_to_all x2, starting transfers between devices, shards(): got_y = lax.all_to_all(slots_y, 'gy', 0, 0, tiled=True)  15.7 us
    pallas_call x6, Pallas kernels, call(): pl.pallas_call(body, name=name, out_shape=[pltpu.VMEM(*(r if isinstance(r...  13.9 us
    ppermute x2, starting transfers between devices, shards(): twin = lax.ppermute(strip, 'gy', twins)  12 us
    unnamed x47, local copies, waits for them, and re-layouts  10.6 us
    ppermute x2, starting transfers between devices, shards(): other = lax.ppermute(strip, 'gy', others)  7.08 us
    all_to_all x2, waiting for transfers between devices, shards(): got_y = lax.all_to_all(slots_y, 'gy', 0, 0, tiled=True)  6.65 us
  transfers between devices with their start and end apart: 7, of which 5 were waited for; matrix products, arithmetic and copies ran while one was open for 0% of the time, Pallas kernels for 3%

profile of v5, /device:TPU:1, one launch (start us, length us, event | category | flops | bytes accessed | tf_op | source)
XLA Modules:
  0.0 113.3 jit_solution(4783059334646933649)
XLA Ops:
  0.0 0.0 copy-start.8
  0.0 0.0 copy-start.1
  0.0 0.0 copy-start.9
  0.0 0.8 copy-done.9
  0.8 0.0 copy-start.14
  0.8 0.0 copy-start.15
  0.9 1.1 pool.1
  1.9 18.2 %all-to-all-start = ((f32[16,2,8,128]{3,2,1,0:T(8,128)}), f32[16,2,8,128]{3,2,1,0:T(8,128)S(1)}, u32[]{:S(2)}, u32[]{:S(2)}) async-start(f32[16,2,8,128]{3,2,1,0:T(8,128)} %get-tuple-element.21), calls=%async_computation | async-start | bytes 262144 | tf_op jit(solution)/shard_map/all_to_all | solution.py:655
  20.1 0.0 copy-start
  20.1 2.2 %copy-done = f32[2,8,8,64,64]{4,3,2,1,0:T(8,128)S(1)} copy-done((f32[2,8,8,64,64]{4,3,2,1,0:T(8,128)S(1)}, f32[2,8,8,64,64]{4,3,2,1,0:T(8,128)}, u32[]{:S(2)}) %copy-start) | copy-done | bytes 2097176
  22.3 0.0 copy-start.11
  22.3 0.8 copy-done.11
  23.1 0.0 copy-start.12
  23.1 0.8 copy-done.12
  23.8 0.0 copy-start.13
  23.8 0.8 copy-done.13
  24.6 0.0 copy-start.16
  24.6 0.7 copy-done.16
  25.3 0.0 copy-start.17
  25.3 0.7 copy-done.17
  26.0 0.0 copy-start.18
  26.0 0.7 copy-done.18
  26.6 0.0 copy-start.19
  26.6 0.7 copy-done.19
  27.3 0.0 copy-start.20
  27.3 0.7 copy-done.20
  27.9 0.0 copy-start.21
  27.9 0.7 copy-done.21
  28.6 0.0 copy-start.22
  28.6 0.7 copy-done.22
  29.2 0.0 copy-start.5
  29.3 0.0 copy-start.6
  29.3 0.0 copy-start.10
  29.3 2.9 %prepare.1 = (f32[1024,128]{1,0:T(8,128)S(1)}, bf16[64,48]{1,0:T(8,128)(2,1)S(1)}, bf16[136,192]{1,0:T(8,128)(2,1)S(1)}, f32[128,128]{1,0:T(8,128)S(1)}, f32[3,1...) custom-call(f32[12,64]{1,0:T(8,128)S(1)} %copy-done.16, f32[1,64]{1,0:T(1,128)S(1)} %bitcast.11, f32[2,64,64,64]{3,2,1,0:T(8,128)S(1)} %bitcast.8, ...), custom_call_target="tpu_custom_call" | custom-call | tf_op jit(solution)/shard_map/prepare/pallas_call | solution.py:584
  32.2 3.6 %all-to-all-done.got_ref = f32[16,2,8,128]{3,2,1,0:T(8,128)S(1)} async-done(((f32[16,2,8,128]{3,2,1,0:T(8,128)}), f32[16,2,8,128]{3,2,1,0:T(8,128)S(1)}, u32[]{:S(2)}, u32[]{:S(2)}) %all-to-all-start) | async-done | bytes 131104 | tf_op jit(solution)/shard_map/all_to_all | solution.py:655
  35.7 0.0 copy-done.8
  35.7 0.0 copy-done.7
  35.7 1.2 %strip.2 = (f32[32,3,8,128]{3,2,1,0:T(8,128)}, f32[3,32,128]{2,1,0:T(8,128)S(1)}) custom-call(f32[2,3,8,128]{3,2,1,0:T(8,128)S(1)} %get-tuple-element.20.own_ref, f32[16,2,8,128]{3,2,1,0:T(8,128)S(1)} %all-to-all-done.got_ref, bf16[256,256]{1,0:T(8,128)(2,1)S(1)} %copy-done.7, bf16[96,192]{1,0:T(8,128)(2,1)S(1)} %copy-done.8, ...), custom_call_target="tpu_custom_call" | custom-call | tf_op jit(solution)/shard_map/strip/pallas_call | solution.py:584
  37.0 9.1 %all-to-all-start.1 = ((f32[32,3,8,128]{3,2,1,0:T(8,128)}), f32[32,3,8,128]{3,2,1,0:T(8,128)S(1)}, u32[]{:S(2)}, u32[]{:S(2)}) async-start(f32[32,3,8,128]{3,2,1,0:T(8,128)} %get-tuple-element.24), calls=%async_computation.1 | async-start | bytes 786432 | tf_op jit(solution)/shard_map/all_to_all | solution.py:659
  46.1 3.5 %collective-permute-start.1 = (f32[3,32,128]{2,1,0:T(8,128)S(1)}, f32[3,32,128]{2,1,0:T(8,128)S(1)}, u32[]{:S(2)}, u32[]{:S(2)}) collective-permute-start(f32[3,32,128]{2,1,0:T(8,128)S(1)} %get-tuple-element.23.refs_1_), channel_id=1, source_target_pairs={{0,31},{1,2},{2,1},{3,4},{4,3},{5,6},{6,5},{7,8},{8,7},{9,10},{10,... | collective-permute-start | bytes 147464 | tf_op jit(solution)/shard_map/ppermute | solution.py:661
  49.6 6.0 %collective-permute-start = (f32[3,32,128]{2,1,0:T(8,128)S(1)}, f32[3,32,128]{2,1,0:T(8,128)S(1)}, u32[]{:S(2)}, u32[]{:S(2)}) collective-permute-start(f32[3,32,128]{2,1,0:T(8,128)S(1)} %get-tuple-element.23.refs_1_), channel_id=1, source_target_pairs={{0,1},{1,0},{2,3},{3,2},{4,5},{5,4},{6,7},{7,6},{8,9},{9,8},{10,11... | collective-permute-start | bytes 147464 | tf_op jit(solution)/shard_map/ppermute | solution.py:660
  55.7 0.0 collective-permute-done.1.refs_3_
  55.7 0.8 collective-permute-done.refs_2_
  56.5 3.3 %all-to-all-done.1.refs_4_ = f32[32,3,8,128]{3,2,1,0:T(8,128)S(1)} async-done(((f32[32,3,8,128]{3,2,1,0:T(8,128)}), f32[32,3,8,128]{3,2,1,0:T(8,128)S(1)}, u32[]{:S(2)}, u32[]{:S(2)}) %all-to-all-start.1) | async-done | bytes 393248 | tf_op jit(solution)/shard_map/all_to_all | solution.py:659
  59.9 0.0 copy-done.1
  59.9 0.0 copy-done.14
  59.9 0.0 copy-done.15
  59.9 0.0 copy-done.2
  59.9 0.0 copy-done.3
  59.9 0.0 copy-done.4
  59.9 0.0 copy-done.5
  59.9 0.0 copy-done.6
  59.9 0.0 copy-done.10
  59.9 4.0 %middle.1 = (f32[3,32,128]{2,1,0:T(8,128)S(1)}, f32[16,2,8,128]{3,2,1,0:T(8,128)S(1)}, f32[2,3,8,128]{3,2,1,0:T(8,128)S(1)}) custom-call(f32[3,32,128]{2,1,0:T(8,128)S(1)} %copy-done.10, f32[3,32,128]{2,1,0:T(8,128)S(1)} %get-tuple-element.23.refs_1_, f32[3,32,128]{2,1,0:T(8,128)S(1)} %collective-permute-done.refs_2_, ...), custom_call_target="tpu_custom_call" | custom-call | tf_op jit(solution)/shard_map/middle/pallas_call | solution.py:584
  63.9 23.7 %all_to_all.20.got_ref = f32[16,2,8,128]{3,2,1,0:T(8,128)S(1)} all-to-all(f32[16,2,8,128]{3,2,1,0:T(8,128)S(1)} %get-tuple-element.32), channel_id=1, replica_groups=mesh['gx'=16,'gy'=32] {'gx'}, dimensions={0} | all-to-all | bytes 262144 | tf_op jit(solution)/shard_map/all_to_all | solution.py:655
  87.6 1.2 %strip.3 = (f32[32,3,8,128]{3,2,1,0:T(8,128)}, f32[3,32,128]{2,1,0:T(8,128)S(1)}) custom-call(f32[2,3,8,128]{3,2,1,0:T(8,128)S(1)} %get-tuple-element.31.own_ref, f32[16,2,8,128]{3,2,1,0:T(8,128)S(1)} %all_to_all.20.got_ref, bf16[256,256]{1,0:T(8,128)(2,1)S(1)} %copy-done.7, bf16[96,192]{1,0:T(8,128)(2,1)S(1)} %copy-done.8, ...), custom_call_target="tpu_custom_call" | custom-call | tf_op jit(solution)/shard_map/strip/pallas_call | solution.py:584
  88.8 6.6 %all-to-all-start.3 = ((f32[32,3,8,128]{3,2,1,0:T(8,128)}), f32[32,3,8,128]{3,2,1,0:T(8,128)S(1)}, u32[]{:S(2)}, u32[]{:S(2)}) async-start(f32[32,3,8,128]{3,2,1,0:T(8,128)} %get-tuple-element.34), calls=%async_computation.3 | async-start | bytes 786432 | tf_op jit(solution)/shard_map/all_to_all | solution.py:659
  95.4 3.5 %collective-permute-start.3 = (f32[3,32,128]{2,1,0:T(8,128)S(1)}, f32[3,32,128]{2,1,0:T(8,128)S(1)}, u32[]{:S(2)}, u32[]{:S(2)}) collective-permute-start(f32[3,32,128]{2,1,0:T(8,128)S(1)} %get-tuple-element.33.refs_1_), channel_id=1, source_target_pairs={{0,31},{1,2},{2,1},{3,4},{4,3},{5,6},{6,5},{7,8},{8,7},{9,10},{10,... | collective-permute-start | bytes 147464 | tf_op jit(solution)/shard_map/ppermute | solution.py:661
  98.9 6.0 %collective-permute-start.2 = (f32[3,32,128]{2,1,0:T(8,128)S(1)}, f32[3,32,128]{2,1,0:T(8,128)S(1)}, u32[]{:S(2)}, u32[]{:S(2)}) collective-permute-start(f32[3,32,128]{2,1,0:T(8,128)S(1)} %get-tuple-element.33.refs_1_), channel_id=1, source_target_pairs={{0,1},{1,0},{2,3},{3,2},{4,5},{5,4},{6,7},{7,6},{8,9},{9,8},{10,11... | collective-permute-start | bytes 147464 | tf_op jit(solution)/shard_map/ppermute | solution.py:660
  104.9 0.0 collective-permute-done.3.refs_3_
  104.9 0.8 collective-permute-done.2.refs_2_
  105.8 3.3 %all-to-all-done.3.refs_4_ = f32[32,3,8,128]{3,2,1,0:T(8,128)S(1)} async-done(((f32[32,3,8,128]{3,2,1,0:T(8,128)}), f32[32,3,8,128]{3,2,1,0:T(8,128)S(1)}, u32[]{:S(2)}, u32[]{:S(2)}) %all-to-all-start.3) | async-done | bytes 393248 | tf_op jit(solution)/shard_map/all_to_all | solution.py:659
  109.1 3.6 %final.1 = f32[3,32,128]{2,1,0:T(8,128)S(1)} custom-call(f32[3,32,128]{2,1,0:T(8,128)S(1)} %get-tuple-element.30.refs_0_, f32[3,32,128]{2,1,0:T(8,128)S(1)} %get-tuple-element.33.refs_1_, f32[3,32,128]{2,1,0:T(8,128)S(1)} %collective-permute-done.2.refs_2_, f32[3,32,128]{2,1,0:T(8,128)S(1)} %collective-permute-done.3.refs_3_, ...), custom_call_target="tpu_custom_call" | custom-call | tf_op jit(solution)/shard_map/final/pallas_call | solution.py:584
  112.7 0.6 copy.19
  (4 shorter events, 0.0 us)
Async XLA Ops:
  0.0 35.7 %copy-start.8 = (bf16[96,192]{1,0:T(8,128)(2,1)S(1)}, bf16[96,192]{1,0:T(8,128)(2,1)}, u32[]{:S(2)}) copy-start(bf16[96,192]{1,0:T(8,128)(2,1)} %constant.19.rows_ref) | copy-start | bytes 110596
  0.0 59.9 %copy-start.1 = (bf16[512,256]{1,0:T(8,128)(2,1)S(1)}, bf16[512,256]{1,0:T(8,128)(2,1)}, u32[]{:S(2)}) copy-start(bf16[512,256]{1,0:T(8,128)(2,1)} %constant.35.refs_18_) | copy-start | bytes 786436
  0.0 0.8 copy-start.9
  0.8 59.0 %copy-start.14 = (bf16[16,128]{1,0:T(8,128)(2,1)S(1)}, bf16[16,128]{1,0:T(8,128)(2,1)}, u32[]{:S(2)}) copy-start(bf16[16,128]{1,0:T(8,128)(2,1)} %constant.27.refs_14_) | copy-start | bytes 12292
  0.8 59.0 %copy-start.15 = (bf16[16,128]{1,0:T(8,128)(2,1)S(1)}, bf16[16,128]{1,0:T(8,128)(2,1)}, u32[]{:S(2)}) copy-start(bf16[16,128]{1,0:T(8,128)(2,1)} %constant.24.refs_13_) | copy-start | bytes 12292
  1.9 33.8 %all-to-all-start = ((f32[16,2,8,128]{3,2,1,0:T(8,128)}), f32[16,2,8,128]{3,2,1,0:T(8,128)S(1)}, u32[]{:S(2)}, u32[]{:S(2)}) async-start(f32[16,2,8,128]{3,2,1,0:T(8,128)} %get-tuple-element.21), calls=%async_computation | async-start | bytes 262144 | tf_op jit(solution)/shard_map/all_to_all | solution.py:655
  20.1 2.2 %copy-start = (f32[2,8,8,64,64]{4,3,2,1,0:T(8,128)S(1)}, f32[2,8,8,64,64]{4,3,2,1,0:T(8,128)}, u32[]{:S(2)}) copy-start(f32[2,8,8,64,64]{4,3,2,1,0:T(8,128)} %param.21) | copy-start | bytes 6291460
  22.3 0.8 copy-start.11
  23.1 0.8 copy-start.12
  23.8 0.8 copy-start.13
  24.6 0.7 copy-start.16
  25.3 0.7 copy-start.17
  26.0 0.7 copy-start.18
  26.6 0.7 copy-start.19
  27.3 0.7 copy-start.20
  27.9 0.7 copy-start.21
  28.6 0.7 copy-start.22
  29.2 6.5 %copy-start.7 = (bf16[256,256]{1,0:T(8,128)(2,1)S(1)}, bf16[256,256]{1,0:T(8,128)(2,1)}, u32[]{:S(2)}) copy-start(bf16[256,256]{1,0:T(8,128)(2,1)} %constant.18.columns_ref) | copy-start | bytes 393220
  29.2 30.6 %copy-start.2 = (bf16[512,256]{1,0:T(8,128)(2,1)S(1)}, bf16[512,256]{1,0:T(8,128)(2,1)}, u32[]{:S(2)}) copy-start(bf16[512,256]{1,0:T(8,128)(2,1)} %constant.32.refs_17_) | copy-start | bytes 786436
  29.2 30.6 %copy-start.3 = (bf16[256,512]{1,0:T(8,128)(2,1)S(1)}, bf16[256,512]{1,0:T(8,128)(2,1)}, u32[]{:S(2)}) copy-start(bf16[256,512]{1,0:T(8,128)(2,1)} %constant.23.refs_12_) | copy-start | bytes 786436
  29.2 30.6 %copy-start.4 = (bf16[256,512]{1,0:T(8,128)(2,1)S(1)}, bf16[256,512]{1,0:T(8,128)(2,1)}, u32[]{:S(2)}) copy-start(bf16[256,512]{1,0:T(8,128)(2,1)} %constant.20.refs_11_) | copy-start | bytes 786436
  29.2 30.7 %copy-start.5 = (bf16[128,512]{1,0:T(8,128)(2,1)S(1)}, bf16[128,512]{1,0:T(8,128)(2,1)}, u32[]{:S(2)}) copy-start(bf16[128,512]{1,0:T(8,128)(2,1)} %constant.31.refs_16_) | copy-start | bytes 393220
  29.3 30.7 %copy-start.6 = (bf16[128,512]{1,0:T(8,128)(2,1)S(1)}, bf16[128,512]{1,0:T(8,128)(2,1)}, u32[]{:S(2)}) copy-start(bf16[128,512]{1,0:T(8,128)(2,1)} %constant.28.refs_15_) | copy-start | bytes 393220
  29.3 30.6 %copy-start.10 = (f32[3,32,128]{2,1,0:T(8,128)S(1)}, f32[3,32,128]{2,1,0:T(8,128)}, u32[]{:S(2)}) copy-start(f32[3,32,128]{2,1,0:T(8,128)} %refs_0_.1) | copy-start | bytes 147460
  37.0 22.9 %all-to-all-start.1 = ((f32[32,3,8,128]{3,2,1,0:T(8,128)}), f32[32,3,8,128]{3,2,1,0:T(8,128)S(1)}, u32[]{:S(2)}, u32[]{:S(2)}) async-start(f32[32,3,8,128]{3,2,1,0:T(8,128)} %get-tuple-element.24), calls=%async_computation.1 | async-start | bytes 786432 | tf_op jit(solution)/shard_map/all_to_all | solution.py:659
  46.1 9.6 %collective-permute-start.1 = (f32[3,32,128]{2,1,0:T(8,128)S(1)}, f32[3,32,128]{2,1,0:T(8,128)S(1)}, u32[]{:S(2)}, u32[]{:S(2)}) collective-permute-start(f32[3,32,128]{2,1,0:T(8,128)S(1)} %get-tuple-element.23.refs_1_), channel_id=1, source_target_pairs={{0,31},{1,2},{2,1},{3,4},{4,3},{5,6},{6,5},{7,8},{8,7},{9,10},{10,... | collective-permute-start | bytes 147464 | tf_op jit(solution)/shard_map/ppermute | solution.py:661
  49.6 6.9 %collective-permute-start = (f32[3,32,128]{2,1,0:T(8,128)S(1)}, f32[3,32,128]{2,1,0:T(8,128)S(1)}, u32[]{:S(2)}, u32[]{:S(2)}) collective-permute-start(f32[3,32,128]{2,1,0:T(8,128)S(1)} %get-tuple-element.23.refs_1_), channel_id=1, source_target_pairs={{0,1},{1,0},{2,3},{3,2},{4,5},{5,4},{6,7},{7,6},{8,9},{9,8},{10,11... | collective-permute-start | bytes 147464 | tf_op jit(solution)/shard_map/ppermute | solution.py:660
  88.8 20.3 %all-to-all-start.3 = ((f32[32,3,8,128]{3,2,1,0:T(8,128)}), f32[32,3,8,128]{3,2,1,0:T(8,128)S(1)}, u32[]{:S(2)}, u32[]{:S(2)}) async-start(f32[32,3,8,128]{3,2,1,0:T(8,128)} %get-tuple-element.34), calls=%async_computation.3 | async-start | bytes 786432 | tf_op jit(solution)/shard_map/all_to_all | solution.py:659
  95.4 9.6 %collective-permute-start.3 = (f32[3,32,128]{2,1,0:T(8,128)S(1)}, f32[3,32,128]{2,1,0:T(8,128)S(1)}, u32[]{:S(2)}, u32[]{:S(2)}) collective-permute-start(f32[3,32,128]{2,1,0:T(8,128)S(1)} %get-tuple-element.33.refs_1_), channel_id=1, source_target_pairs={{0,31},{1,2},{2,1},{3,4},{4,3},{5,6},{6,5},{7,8},{8,7},{9,10},{10,... | collective-permute-start | bytes 147464 | tf_op jit(solution)/shard_map/ppermute | solution.py:661
  98.9 6.9 %collective-permute-start.2 = (f32[3,32,128]{2,1,0:T(8,128)S(1)}, f32[3,32,128]{2,1,0:T(8,128)S(1)}, u32[]{:S(2)}, u32[]{:S(2)}) collective-permute-start(f32[3,32,128]{2,1,0:T(8,128)S(1)} %get-tuple-element.33.refs_1_), channel_id=1, source_target_pairs={{0,1},{1,0},{2,3},{3,2},{4,5},{5,4},{6,7},{7,6},{8,9},{9,8},{10,11... | collective-permute-start | bytes 147464 | tf_op jit(solution)/shard_map/ppermute | solution.py:660

commit v6 on v5

--- a/solution.py
+++ b/solution.py
@@ -580,11 +580,16 @@
     return pltpu.with_memory_space_constraint(operand, pltpu.VMEM)
 
 
-def call(body, name, operands, results, scratch=()):
+def call(body, name, operands, results, scratch=(), resident_out=True):
     return pl.pallas_call(
         body,
         name=name,
-        out_shape=[pltpu.VMEM(*(r if isinstance(r[0], tuple) else (r, F32))) for r in results],
+        out_shape=[
+            (pltpu.VMEM if resident_out else jax.ShapeDtypeStruct)(
+                *(r if isinstance(r[0], tuple) else (r, F32))
+            )
+            for r in results
+        ],
         in_specs=[VMEM] * len(operands),
         out_specs=[VMEM] * len(results),
         scratch_shapes=list(scratch),
@@ -678,7 +683,9 @@
                 scratch,
             )
         else:
-            (current,) = call(final_kernel, "final", operands, [fields.shape], scratch)
+            (current,) = call(
+                final_kernel, "final", operands, [fields.shape], scratch, resident_out=False
+            )
     return current
 
 

time: 114 us -> 114 us (level)
    unnamed x47 -> x46, local copies, waits for them, and re-layouts: 10.6 us -> 9.99 us
where the time goes in v6:
time: 114 us; the launch traced here: 113 us
  starting transfers between devices  53 us (46%)
  blocking collectives  23.7 us (21%)
  Pallas kernels  14.5 us (13%)
  waiting for transfers between devices  11.9 us (10%)
  local copies, waits for them, and re-layouts  9.99 us (9%)
    all_to_all x1, blocking collectives, shards(): got_x = lax.all_to_all(slots_x, 'gx', 0, 0, tiled=True)  23.7 us
    all_to_all x1, starting transfers between devices, shards(): got_x = lax.all_to_all(slots_x, 'gx', 0, 0, tiled=True)  18.2 us
    all_to_all x2, starting transfers between devices, shards(): got_y = lax.all_to_all(slots_y, 'gy', 0, 0, tiled=True)  15.7 us
    pallas_call x6, Pallas kernels, call(): pl.pallas_call(body, name=name, out_shape=[(pltpu.VMEM if resident_out el...  14.5 us
    ppermute x2, starting transfers between devices, shards(): twin = lax.ppermute(strip, 'gy', twins)  12 us
    unnamed x46, local copies, waits for them, and re-layouts  9.99 us
    ppermute x2, starting transfers between devices, shards(): other = lax.ppermute(strip, 'gy', others)  7.08 us
    all_to_all x2, waiting for transfers between devices, shards(): got_y = lax.all_to_all(slots_y, 'gy', 0, 0, tiled=True)  6.65 us
  transfers between devices with their start and end apart: 7, of which 5 were waited for; matrix products, arithmetic and copies ran while one was open for 0% of the time, Pallas kernels for 3%

profile of v6, /device:TPU:1, one launch (start us, length us, event | category | flops | bytes accessed | tf_op | source)
XLA Modules:
  0.0 113.3 jit_solution(6642529090062822097)
XLA Ops:
  0.0 0.0 copy-start.8
  0.0 0.0 copy-start.1
  0.0 0.0 copy-start.9
  0.0 0.8 copy-done.9
  0.8 0.0 copy-start.14
  0.8 0.0 copy-start.15
  0.9 1.1 pool.1
  1.9 18.2 %all-to-all-start = ((f32[16,2,8,128]{3,2,1,0:T(8,128)}), f32[16,2,8,128]{3,2,1,0:T(8,128)S(1)}, u32[]{:S(2)}, u32[]{:S(2)}) async-start(f32[16,2,8,128]{3,2,1,0:T(8,128)} %get-tuple-element.21), calls=%async_computation | async-start | bytes 262144 | tf_op jit(solution)/shard_map/all_to_all | solution.py:660
  20.1 0.0 copy-start
  20.1 2.2 %copy-done = f32[2,8,8,64,64]{4,3,2,1,0:T(8,128)S(1)} copy-done((f32[2,8,8,64,64]{4,3,2,1,0:T(8,128)S(1)}, f32[2,8,8,64,64]{4,3,2,1,0:T(8,128)}, u32[]{:S(2)}) %copy-start) | copy-done | bytes 2097176
  22.3 0.0 copy-start.11
  22.3 0.8 copy-done.11
  23.1 0.0 copy-start.12
  23.1 0.8 copy-done.12
  23.8 0.0 copy-start.13
  23.8 0.8 copy-done.13
  24.6 0.0 copy-start.16
  24.6 0.7 copy-done.16
  25.3 0.0 copy-start.17
  25.3 0.7 copy-done.17
  26.0 0.0 copy-start.18
  26.0 0.7 copy-done.18
  26.6 0.0 copy-start.19
  26.6 0.7 copy-done.19
  27.3 0.0 copy-start.20
  27.3 0.7 copy-done.20
  27.9 0.0 copy-start.21
  27.9 0.7 copy-done.21
  28.6 0.0 copy-start.22
  28.6 0.7 copy-done.22
  29.2 0.0 copy-start.7
  29.2 0.0 copy-start.5
  29.3 0.0 copy-start.6
  29.3 0.0 copy-start.10
  29.3 2.9 %prepare.1 = (f32[1024,128]{1,0:T(8,128)S(1)}, bf16[64,48]{1,0:T(8,128)(2,1)S(1)}, bf16[136,192]{1,0:T(8,128)(2,1)S(1)}, f32[128,128]{1,0:T(8,128)S(1)}, f32[3,1...) custom-call(f32[12,64]{1,0:T(8,128)S(1)} %copy-done.16, f32[1,64]{1,0:T(1,128)S(1)} %bitcast.11, f32[2,64,64,64]{3,2,1,0:T(8,128)S(1)} %bitcast.8, ...), custom_call_target="tpu_custom_call" | custom-call | tf_op jit(solution)/shard_map/prepare/pallas_call | solution.py:584
  32.2 3.6 %all-to-all-done.got_ref = f32[16,2,8,128]{3,2,1,0:T(8,128)S(1)} async-done(((f32[16,2,8,128]{3,2,1,0:T(8,128)}), f32[16,2,8,128]{3,2,1,0:T(8,128)S(1)}, u32[]{:S(2)}, u32[]{:S(2)}) %all-to-all-start) | async-done | bytes 131104 | tf_op jit(solution)/shard_map/all_to_all | solution.py:660
  35.7 0.0 copy-done.8
  35.7 0.0 copy-done.7
  35.7 1.2 %strip.2 = (f32[32,3,8,128]{3,2,1,0:T(8,128)}, f32[3,32,128]{2,1,0:T(8,128)S(1)}) custom-call(f32[2,3,8,128]{3,2,1,0:T(8,128)S(1)} %get-tuple-element.20.own_ref, f32[16,2,8,128]{3,2,1,0:T(8,128)S(1)} %all-to-all-done.got_ref, bf16[256,256]{1,0:T(8,128)(2,1)S(1)} %copy-done.7, bf16[96,192]{1,0:T(8,128)(2,1)S(1)} %copy-done.8, ...), custom_call_target="tpu_custom_call" | custom-call | tf_op jit(solution)/shard_map/strip/pallas_call | solution.py:584
  37.0 9.1 %all-to-all-start.1 = ((f32[32,3,8,128]{3,2,1,0:T(8,128)}), f32[32,3,8,128]{3,2,1,0:T(8,128)S(1)}, u32[]{:S(2)}, u32[]{:S(2)}) async-start(f32[32,3,8,128]{3,2,1,0:T(8,128)} %get-tuple-element.24), calls=%async_computation.1 | async-start | bytes 786432 | tf_op jit(solution)/shard_map/all_to_all | solution.py:664
  46.1 3.5 %collective-permute-start.1 = (f32[3,32,128]{2,1,0:T(8,128)S(1)}, f32[3,32,128]{2,1,0:T(8,128)S(1)}, u32[]{:S(2)}, u32[]{:S(2)}) collective-permute-start(f32[3,32,128]{2,1,0:T(8,128)S(1)} %get-tuple-element.23.refs_1_), channel_id=1, source_target_pairs={{0,31},{1,2},{2,1},{3,4},{4,3},{5,6},{6,5},{7,8},{8,7},{9,10},{10,... | collective-permute-start | bytes 147464 | tf_op jit(solution)/shard_map/ppermute | solution.py:666
  49.6 6.0 %collective-permute-start = (f32[3,32,128]{2,1,0:T(8,128)S(1)}, f32[3,32,128]{2,1,0:T(8,128)S(1)}, u32[]{:S(2)}, u32[]{:S(2)}) collective-permute-start(f32[3,32,128]{2,1,0:T(8,128)S(1)} %get-tuple-element.23.refs_1_), channel_id=1, source_target_pairs={{0,1},{1,0},{2,3},{3,2},{4,5},{5,4},{6,7},{7,6},{8,9},{9,8},{10,11... | collective-permute-start | bytes 147464 | tf_op jit(solution)/shard_map/ppermute | solution.py:665
  55.7 0.0 collective-permute-done.1.refs_3_
  55.7 0.8 collective-permute-done.refs_2_
  56.5 3.3 %all-to-all-done.1.refs_4_ = f32[32,3,8,128]{3,2,1,0:T(8,128)S(1)} async-done(((f32[32,3,8,128]{3,2,1,0:T(8,128)}), f32[32,3,8,128]{3,2,1,0:T(8,128)S(1)}, u32[]{:S(2)}, u32[]{:S(2)}) %all-to-all-start.1) | async-done | bytes 393248 | tf_op jit(solution)/shard_map/all_to_all | solution.py:664
  59.9 0.0 copy-done.1
  59.9 0.0 copy-done.14
  59.9 0.0 copy-done.15
  59.9 0.0 copy-done.2
  59.9 0.0 copy-done.3
  59.9 0.0 copy-done.4
  59.9 0.0 copy-done.5
  59.9 0.0 copy-done.6
  59.9 0.0 copy-done.10
  59.9 4.0 %middle.1 = (f32[3,32,128]{2,1,0:T(8,128)S(1)}, f32[16,2,8,128]{3,2,1,0:T(8,128)S(1)}, f32[2,3,8,128]{3,2,1,0:T(8,128)S(1)}) custom-call(f32[3,32,128]{2,1,0:T(8,128)S(1)} %copy-done.10, f32[3,32,128]{2,1,0:T(8,128)S(1)} %get-tuple-element.23.refs_1_, f32[3,32,128]{2,1,0:T(8,128)S(1)} %collective-permute-done.refs_2_, ...), custom_call_target="tpu_custom_call" | custom-call | tf_op jit(solution)/shard_map/middle/pallas_call | solution.py:584
  63.9 23.7 %all_to_all.20.got_ref = f32[16,2,8,128]{3,2,1,0:T(8,128)S(1)} all-to-all(f32[16,2,8,128]{3,2,1,0:T(8,128)S(1)} %get-tuple-element.32), channel_id=1, replica_groups=mesh['gx'=16,'gy'=32] {'gx'}, dimensions={0} | all-to-all | bytes 262144 | tf_op jit(solution)/shard_map/all_to_all | solution.py:660
  87.6 1.2 %strip.3 = (f32[32,3,8,128]{3,2,1,0:T(8,128)}, f32[3,32,128]{2,1,0:T(8,128)S(1)}) custom-call(f32[2,3,8,128]{3,2,1,0:T(8,128)S(1)} %get-tuple-element.31.own_ref, f32[16,2,8,128]{3,2,1,0:T(8,128)S(1)} %all_to_all.20.got_ref, bf16[256,256]{1,0:T(8,128)(2,1)S(1)} %copy-done.7, bf16[96,192]{1,0:T(8,128)(2,1)S(1)} %copy-done.8, ...), custom_call_target="tpu_custom_call" | custom-call | tf_op jit(solution)/shard_map/strip/pallas_call | solution.py:584
  88.8 6.6 %all-to-all-start.3 = ((f32[32,3,8,128]{3,2,1,0:T(8,128)}), f32[32,3,8,128]{3,2,1,0:T(8,128)S(1)}, u32[]{:S(2)}, u32[]{:S(2)}) async-start(f32[32,3,8,128]{3,2,1,0:T(8,128)} %get-tuple-element.34), calls=%async_computation.3 | async-start | bytes 786432 | tf_op jit(solution)/shard_map/all_to_all | solution.py:664
  95.4 3.5 %collective-permute-start.3 = (f32[3,32,128]{2,1,0:T(8,128)S(1)}, f32[3,32,128]{2,1,0:T(8,128)S(1)}, u32[]{:S(2)}, u32[]{:S(2)}) collective-permute-start(f32[3,32,128]{2,1,0:T(8,128)S(1)} %get-tuple-element.33.refs_1_), channel_id=1, source_target_pairs={{0,31},{1,2},{2,1},{3,4},{4,3},{5,6},{6,5},{7,8},{8,7},{9,10},{10,... | collective-permute-start | bytes 147464 | tf_op jit(solution)/shard_map/ppermute | solution.py:666
  98.9 6.0 %collective-permute-start.2 = (f32[3,32,128]{2,1,0:T(8,128)S(1)}, f32[3,32,128]{2,1,0:T(8,128)S(1)}, u32[]{:S(2)}, u32[]{:S(2)}) collective-permute-start(f32[3,32,128]{2,1,0:T(8,128)S(1)} %get-tuple-element.33.refs_1_), channel_id=1, source_target_pairs={{0,1},{1,0},{2,3},{3,2},{4,5},{5,4},{6,7},{7,6},{8,9},{9,8},{10,11... | collective-permute-start | bytes 147464 | tf_op jit(solution)/shard_map/ppermute | solution.py:665
  104.9 0.0 collective-permute-done.3.refs_3_
  104.9 0.8 collective-permute-done.2.refs_2_
  105.8 3.3 %all-to-all-done.3.refs_4_ = f32[32,3,8,128]{3,2,1,0:T(8,128)S(1)} async-done(((f32[32,3,8,128]{3,2,1,0:T(8,128)}), f32[32,3,8,128]{3,2,1,0:T(8,128)S(1)}, u32[]{:S(2)}, u32[]{:S(2)}) %all-to-all-start.3) | async-done | bytes 393248 | tf_op jit(solution)/shard_map/all_to_all | solution.py:664
  109.1 4.2 %final.1 = f32[3,32,128]{2,1,0:T(8,128)} custom-call(f32[3,32,128]{2,1,0:T(8,128)S(1)} %get-tuple-element.30.refs_0_, f32[3,32,128]{2,1,0:T(8,128)S(1)} %get-tuple-element.33.refs_1_, f32[3,32,128]{2,1,0:T(8,128)S(1)} %collective-permute-done.2.refs_2_, f32[3,32,128]{2,1,0:T(8,128)S(1)} %collective-permute-done.3.refs_3_, ...), custom_call_target="tpu_custom_call" | custom-call | tf_op jit(solution)/shard_map/final/pallas_call | solution.py:584
  (3 shorter events, 0.0 us)
Async XLA Ops:
  0.0 35.7 %copy-start.8 = (bf16[96,192]{1,0:T(8,128)(2,1)S(1)}, bf16[96,192]{1,0:T(8,128)(2,1)}, u32[]{:S(2)}) copy-start(bf16[96,192]{1,0:T(8,128)(2,1)} %constant.19.rows_ref) | copy-start | bytes 110596
  0.0 59.9 %copy-start.1 = (bf16[512,256]{1,0:T(8,128)(2,1)S(1)}, bf16[512,256]{1,0:T(8,128)(2,1)}, u32[]{:S(2)}) copy-start(bf16[512,256]{1,0:T(8,128)(2,1)} %constant.35.refs_18_) | copy-start | bytes 786436
  0.0 0.8 copy-start.9
  0.8 59.0 %copy-start.14 = (bf16[16,128]{1,0:T(8,128)(2,1)S(1)}, bf16[16,128]{1,0:T(8,128)(2,1)}, u32[]{:S(2)}) copy-start(bf16[16,128]{1,0:T(8,128)(2,1)} %constant.27.refs_14_) | copy-start | bytes 12292
  0.8 59.0 %copy-start.15 = (bf16[16,128]{1,0:T(8,128)(2,1)S(1)}, bf16[16,128]{1,0:T(8,128)(2,1)}, u32[]{:S(2)}) copy-start(bf16[16,128]{1,0:T(8,128)(2,1)} %constant.24.refs_13_) | copy-start | bytes 12292
  1.9 33.8 %all-to-all-start = ((f32[16,2,8,128]{3,2,1,0:T(8,128)}), f32[16,2,8,128]{3,2,1,0:T(8,128)S(1)}, u32[]{:S(2)}, u32[]{:S(2)}) async-start(f32[16,2,8,128]{3,2,1,0:T(8,128)} %get-tuple-element.21), calls=%async_computation | async-start | bytes 262144 | tf_op jit(solution)/shard_map/all_to_all | solution.py:660
  20.1 2.2 %copy-start = (f32[2,8,8,64,64]{4,3,2,1,0:T(8,128)S(1)}, f32[2,8,8,64,64]{4,3,2,1,0:T(8,128)}, u32[]{:S(2)}) copy-start(f32[2,8,8,64,64]{4,3,2,1,0:T(8,128)} %param.21) | copy-start | bytes 6291460
  22.3 0.8 copy-start.11
  23.1 0.8 copy-start.12
  23.8 0.8 copy-start.13
  24.6 0.7 copy-start.16
  25.3 0.7 copy-start.17
  26.0 0.7 copy-start.18
  26.6 0.7 copy-start.19
  27.3 0.7 copy-start.20
  27.9 0.7 copy-start.21
  28.6 0.7 copy-start.22
  29.2 6.5 %copy-start.7 = (bf16[256,256]{1,0:T(8,128)(2,1)S(1)}, bf16[256,256]{1,0:T(8,128)(2,1)}, u32[]{:S(2)}) copy-start(bf16[256,256]{1,0:T(8,128)(2,1)} %constant.18.columns_ref) | copy-start | bytes 393220
  29.2 30.6 %copy-start.2 = (bf16[512,256]{1,0:T(8,128)(2,1)S(1)}, bf16[512,256]{1,0:T(8,128)(2,1)}, u32[]{:S(2)}) copy-start(bf16[512,256]{1,0:T(8,128)(2,1)} %constant.32.refs_17_) | copy-start | bytes 786436
  29.2 30.6 %copy-start.3 = (bf16[256,512]{1,0:T(8,128)(2,1)S(1)}, bf16[256,512]{1,0:T(8,128)(2,1)}, u32[]{:S(2)}) copy-start(bf16[256,512]{1,0:T(8,128)(2,1)} %constant.23.refs_12_) | copy-start | bytes 786436
  29.2 30.6 %copy-start.4 = (bf16[256,512]{1,0:T(8,128)(2,1)S(1)}, bf16[256,512]{1,0:T(8,128)(2,1)}, u32[]{:S(2)}) copy-start(bf16[256,512]{1,0:T(8,128)(2,1)} %constant.20.refs_11_) | copy-start | bytes 786436
  29.2 30.7 %copy-start.5 = (bf16[128,512]{1,0:T(8,128)(2,1)S(1)}, bf16[128,512]{1,0:T(8,128)(2,1)}, u32[]{:S(2)}) copy-start(bf16[128,512]{1,0:T(8,128)(2,1)} %constant.31.refs_16_) | copy-start | bytes 393220
  29.3 30.7 %copy-start.6 = (bf16[128,512]{1,0:T(8,128)(2,1)S(1)}, bf16[128,512]{1,0:T(8,128)(2,1)}, u32[]{:S(2)}) copy-start(bf16[128,512]{1,0:T(8,128)(2,1)} %constant.28.refs_15_) | copy-start | bytes 393220
  29.3 30.6 %copy-start.10 = (f32[3,32,128]{2,1,0:T(8,128)S(1)}, f32[3,32,128]{2,1,0:T(8,128)}, u32[]{:S(2)}) copy-start(f32[3,32,128]{2,1,0:T(8,128)} %refs_0_.1) | copy-start | bytes 147460
  37.0 22.9 %all-to-all-start.1 = ((f32[32,3,8,128]{3,2,1,0:T(8,128)}), f32[32,3,8,128]{3,2,1,0:T(8,128)S(1)}, u32[]{:S(2)}, u32[]{:S(2)}) async-start(f32[32,3,8,128]{3,2,1,0:T(8,128)} %get-tuple-element.24), calls=%async_computation.1 | async-start | bytes 786432 | tf_op jit(solution)/shard_map/all_to_all | solution.py:664
  46.1 9.6 %collective-permute-start.1 = (f32[3,32,128]{2,1,0:T(8,128)S(1)}, f32[3,32,128]{2,1,0:T(8,128)S(1)}, u32[]{:S(2)}, u32[]{:S(2)}) collective-permute-start(f32[3,32,128]{2,1,0:T(8,128)S(1)} %get-tuple-element.23.refs_1_), channel_id=1, source_target_pairs={{0,31},{1,2},{2,1},{3,4},{4,3},{5,6},{6,5},{7,8},{8,7},{9,10},{10,... | collective-permute-start | bytes 147464 | tf_op jit(solution)/shard_map/ppermute | solution.py:666
  49.6 6.9 %collective-permute-start = (f32[3,32,128]{2,1,0:T(8,128)S(1)}, f32[3,32,128]{2,1,0:T(8,128)S(1)}, u32[]{:S(2)}, u32[]{:S(2)}) collective-permute-start(f32[3,32,128]{2,1,0:T(8,128)S(1)} %get-tuple-element.23.refs_1_), channel_id=1, source_target_pairs={{0,1},{1,0},{2,3},{3,2},{4,5},{5,4},{6,7},{7,6},{8,9},{9,8},{10,11... | collective-permute-start | bytes 147464 | tf_op jit(solution)/shard_map/ppermute | solution.py:665
  88.8 20.3 %all-to-all-start.3 = ((f32[32,3,8,128]{3,2,1,0:T(8,128)}), f32[32,3,8,128]{3,2,1,0:T(8,128)S(1)}, u32[]{:S(2)}, u32[]{:S(2)}) async-start(f32[32,3,8,128]{3,2,1,0:T(8,128)} %get-tuple-element.34), calls=%async_computation.3 | async-start | bytes 786432 | tf_op jit(solution)/shard_map/all_to_all | solution.py:664
  95.4 9.6 %collective-permute-start.3 = (f32[3,32,128]{2,1,0:T(8,128)S(1)}, f32[3,32,128]{2,1,0:T(8,128)S(1)}, u32[]{:S(2)}, u32[]{:S(2)}) collective-permute-start(f32[3,32,128]{2,1,0:T(8,128)S(1)} %get-tuple-element.33.refs_1_), channel_id=1, source_target_pairs={{0,31},{1,2},{2,1},{3,4},{4,3},{5,6},{6,5},{7,8},{8,7},{9,10},{10,... | collective-permute-start | bytes 147464 | tf_op jit(solution)/shard_map/ppermute | solution.py:666
  98.9 6.9 %collective-permute-start.2 = (f32[3,32,128]{2,1,0:T(8,128)S(1)}, f32[3,32,128]{2,1,0:T(8,128)S(1)}, u32[]{:S(2)}, u32[]{:S(2)}) collective-permute-start(f32[3,32,128]{2,1,0:T(8,128)S(1)} %get-tuple-element.33.refs_1_), channel_id=1, source_target_pairs={{0,1},{1,0},{2,3},{3,2},{4,5},{5,4},{6,7},{7,6},{8,9},{9,8},{10,11... | collective-permute-start | bytes 147464 | tf_op jit(solution)/shard_map/ppermute | solution.py:665
